TPU v7x, 32 devices: a whole 2x2x4 slice. The times are simulated.
32 devices in a mesh: lon: 2 (over x), lat: 4 (over y, core), head: 4 (over z).
Axes of the slice: x: 2, y: 2, z: 4, core: 2. Of those that a mesh axis runs over, the one named last changes fastest.
Arguments:
- features: bfloat16 [8, 24, 24, 384], P(None, 'lat', 'lon'), may hold values from -6 to 6
- attend_weight: bfloat16 [3, 384, 384], P(None, None, 'head'), may hold values from -0.3125 to 0.3125
- output_weight: bfloat16 [384, 384], P('head'), may hold values from -0.3125 to 0.3125
- bias_table: float32 [64, 12, 3312], P(None, 'head'), may hold values from -3 to 304
- bias_type: int32 [4, 4], P(None, 'lat'), may hold values from 0 to 63
- window_shift: int32 [1], replicated, may hold values from 1 to 11
- grad_out: bfloat16 [8, 24, 24, 384], P(None, 'lat', 'lon'), may hold values from -6 to 6
Outputs:
- feature_grad: bfloat16 [8, 24, 24, 384], P(None, 'lat', 'lon', 'head')
- attend_grad: float32 [3, 384, 384], P(None, None, 'head')
- output_grad: float32 [384, 384], P('head')
- bias_grad: float32 [64, 12, 3312], P(None, 'head')
All inputs are finite; a program needn't handle non-finite values.
Results may differ from a plain program's by a relative error of at most 0.01.
Values may be sent and summed in bfloat16 or wider, within the bound.
No kernel may reach another device: no remote copies, remote signals or barrier semaphores. Data moves between devices by JAX's collectives and lax.ppermute only.
A program may use at most 128 MiB of HBM per device.

v0:
```python
import jax
import jax.numpy as jnp
from jax import lax
from jax.experimental import pallas as pl
from jax.experimental.pallas import tpu as pltpu
from jax.sharding import PartitionSpec as P

WIN_LEVEL = 2
WIN_LAT = 6
WIN_LON = 12
ROWS = WIN_LEVEL * WIN_LAT
PAD = 16
WIDE = WIN_LON * PAD
TOKENS = WIN_LON * ROWS
OFFSETS = 2 * WIN_LON - 1
LANES = 128
MASKED = -1e30
F32 = jnp.float32
BF16 = jnp.bfloat16


def dot_nn(a, b):
    return lax.dot_general(a, b, (((1,), (0,)), ((), ())), preferred_element_type=F32)


def dot_nt(a, b):
    return lax.dot_general(a, b, (((1,), (1,)), ((), ())), preferred_element_type=F32)


def dot_tn(a, b):
    return lax.dot_general(a, b, (((0,), (0,)), ((), ())), preferred_element_type=F32)


def grid_of(rows, cols):
    shape = (rows, cols)
    return lax.broadcasted_iota(jnp.int32, shape, 0), lax.broadcasted_iota(jnp.int32, shape, 1)


def one_hot(hit):
    return jnp.where(hit, 1.0, 0.0).astype(BF16)


def split16(index):
    return lax.shift_right_logical(index, 4), lax.bitwise_and(index, 15)


def copy_rows(source_ref, rows_ref, slot):
    for level in range(WIN_LEVEL):
        for lat in range(WIN_LAT):
            start = (level * WIN_LAT + lat) * PAD
            rows_ref[start : start + WIN_LON, :] = source_ref[slot * WIN_LEVEL + level, lat]


def pack_kernel(shift_ref, x_ref, g_ref, out_ref, rows_ref):
    half = WIN_LON // 2
    base = jnp.where(shift_ref[0] <= half, 0, WIN_LON - half)
    row, src = grid_of(half * ROWS, ROWS * PAD)
    place, col = split16(src)
    col = col - base
    sel = one_hot((col >= 0) & (col < half) & (row == col * ROWS + place))
    for slot in range(out_ref.shape[1]):
        for array, ref in enumerate((x_ref, g_ref)):
            rows = rows_ref.at[array, slot]
            rows[...] = jnp.zeros(rows.shape, BF16)
            copy_rows(ref, rows, slot)
            out_ref[array, slot] = dot_nn(sel, rows[...]).astype(BF16)


def window_selectors(shift):
    half = WIN_LON // 2
    low = shift <= half
    row, src = grid_of(WIDE, ROWS * PAD)
    lon, place = split16(row)
    src_place, col = split16(src)
    target = lon + shift - jnp.where(low, 0, WIN_LON)
    local = (place == src_place) & (col == target) & (col < WIN_LON) & (place < ROWS)
    row, src = grid_of(WIDE, half * ROWS)
    lon, place = split16(row)
    col = lon + shift - jnp.where(low, WIN_LON, WIN_LON - half)
    taken = (src == col * ROWS + place) & (place < ROWS)
    borrowed = taken & (col >= 0) & (low | (lon + shift < WIN_LON))
    return one_hot(local), one_hot(borrowed)


def main_kernel(
    shift_ref, x_ref, g_ref, far_ref, weight_ref, out_weight_ref, table_ref, *rest
):
    n_head = lax.axis_size("head")
    pieces = rest[:n_head]
    sums_ref, folded_ref, rows_ref, bias_ref = rest[n_head:]
    width = out_weight_ref.shape[0]
    heads = table_ref.shape[1] // PAD
    size = width // heads
    scaling = size ** (-0.5)
    mine = lax.axis_index("head")
    local, borrowed = window_selectors(shift_ref[0])
    row, src = grid_of(TOKENS, WIDE)
    lon, place = split16(src)
    compact = one_hot((row == lon * ROWS + place) & (place < ROWS))
    lane = lax.broadcasted_iota(jnp.int32, (WIDE, width), 1)
    masks = [(lane >= h * size) & (lane < (h + 1) * size) for h in range(heads)]
    span = table_ref.shape[2]
    sums = [jnp.zeros((width, x_ref.shape[3]), F32) for _ in range(4)]
    rows_ref[...] = jnp.zeros(rows_ref.shape, BF16)
    for slot in range(table_ref.shape[0]):
        copy_rows(x_ref, rows_ref.at[0], slot)
        copy_rows(g_ref, rows_ref.at[1], slot)
        tokens = (dot_nn(local, rows_ref[0]) + dot_nn(borrowed, far_ref[0, slot])).astype(BF16)
        grads = (dot_nn(local, rows_ref[1]) + dot_nn(borrowed, far_ref[1, slot])).astype(BF16)
        query = dot_nn(tokens, weight_ref[0]).astype(BF16)
        key = dot_nn(tokens, weight_ref[1]).astype(BF16)
        value = dot_nn(tokens, weight_ref[2]).astype(BF16)
        grad_attended = dot_nt(grads, out_weight_ref[...]).astype(BF16)
        table = table_ref[slot]
        for lon_i in range(WIN_LON):
            by = (WIN_LON - 1 - lon_i) * PAD
            turned = table if by == 0 else pltpu.roll(table, span - by, 1)
            for h in range(heads):
                bias_ref[h, lon_i * PAD : (lon_i + 1) * PAD, :] = turned[
                    h * PAD : (h + 1) * PAD, :WIDE
                ]
        attended = jnp.zeros((WIDE, width), F32)
        grad_query = jnp.zeros((WIDE, width), F32)
        grad_key = jnp.zeros((WIDE, width), F32)
        grad_value = jnp.zeros((WIDE, width), F32)
        for h in range(heads):
            query_h = jnp.where(masks[h], query, jnp.zeros_like(query))
            key_h = jnp.where(masks[h], key, jnp.zeros_like(key))
            value_h = jnp.where(masks[h], value, jnp.zeros_like(value))
            grad_h = jnp.where(masks[h], grad_attended, jnp.zeros_like(grad_attended))
            scores = dot_nt(query_h, key) * scaling + bias_ref[h]
            raised = jnp.exp(scores - jnp.max(scores, axis=1, keepdims=True))
            softened = raised * (1.0 / jnp.sum(raised, axis=1, keepdims=True))
            softened_half = softened.astype(BF16)
            attended = attended + dot_nn(softened_half, value_h)
            grad_value = grad_value + dot_tn(softened_half, grad_h)
            grad_softened = dot_nt(grad_h, value)
            inner = jnp.sum(softened * grad_softened, axis=1, keepdims=True)
            grad_scores = softened * (grad_softened - inner)
            grad_half = grad_scores.astype(BF16)
            grad_query = grad_query + dot_nn(grad_half, key_h)
            grad_key = grad_key + dot_tn(grad_half, query_h)
            padded = jnp.concatenate(
                [grad_scores, jnp.zeros((WIDE, span - WIDE), F32)], axis=1
            )
            total = jnp.zeros((PAD, span), F32)
            for lon_i in range(WIN_LON):
                by = (WIN_LON - 1 - lon_i) * PAD
                part = padded[lon_i * PAD : (lon_i + 1) * PAD, :]
                total = total + (part if by == 0 else pltpu.roll(part, by, 1))
            folded_ref[slot, h * PAD : (h + 1) * PAD, :] = total
        projected = [
            (grad_query * scaling).astype(BF16),
            (grad_key * scaling).astype(BF16),
            grad_value.astype(BF16),
        ]
        for c in range(3):
            sums[c] = sums[c] + dot_tn(projected[c], tokens)
        sums[3] = sums[3] + dot_tn(attended.astype(BF16), grads)
        packed = [dot_nn(compact, part).astype(BF16) for part in projected]
        for step in range(n_head):
            to = lax.rem(mine + step, n_head)
            start = pl.multiple_of(to * width, 16)
            piece = jnp.zeros((TOKENS, width), F32)
            for c in range(3):
                piece = piece + dot_nt(packed[c], weight_ref[c, pl.ds(start, width), :])
            pieces[step][slot * TOKENS : (slot + 1) * TOKENS, :] = piece.astype(BF16)
    for c in range(4):
        sums_ref[c] = sums[c].astype(BF16)


def sum_kernel(shift_ref, *refs):
    parts = refs[:-2]
    summed_ref, back_ref = refs[-2:]
    half = WIN_LON // 2
    shift = shift_ref[0]
    low = shift <= half
    row, src = grid_of(half * ROWS, TOKENS)
    by = (shift - jnp.where(low, WIN_LON, WIN_LON - half)) * ROWS
    back = one_hot((row == src + by) & (low | (src < (WIN_LON - shift) * ROWS)))
    for slot in range(summed_ref.shape[0] // TOKENS):
        at = slice(slot * TOKENS, (slot + 1) * TOKENS)
        total = parts[0][at, :].astype(F32)
        for part in parts[1:]:
            total = total + part[at, :].astype(F32)
        total = total.astype(BF16)
        summed_ref[at, :] = total
        count = half * ROWS
        back_ref[slot * count : (slot + 1) * count, :] = dot_nn(back, total).astype(BF16)


def place_kernel(shift_ref, summed_ref, back_ref, out_ref):
    half = WIN_LON // 2
    shift = shift_ref[0]
    low = shift <= half
    row, src = grid_of(ROWS * PAD, TOKENS)
    place, col = split16(row)
    lon = col - shift + jnp.where(low, 0, WIN_LON)
    own = one_hot(
        (src == lon * ROWS + place) & (lon >= 0) & (col < WIN_LON) & (low | (col < shift))
    )
    row, src = grid_of(ROWS * PAD, half * ROWS)
    place, col = split16(row)
    given = col - jnp.where(low, 0, WIN_LON - half)
    other = one_hot(
        (src == given * ROWS + place)
        & ((low & (col < shift)) | (~low & (col >= shift) & (col < WIN_LON)))
    )
    count = half * ROWS
    for slot in range(summed_ref.shape[0] // TOKENS):
        placed = dot_nn(own, summed_ref[slot * TOKENS : (slot + 1) * TOKENS, :]) + dot_nn(
            other, back_ref[slot * count : (slot + 1) * count, :]
        )
        placed = placed.astype(BF16)
        for level in range(WIN_LEVEL):
            for lat in range(WIN_LAT):
                start = (level * WIN_LAT + lat) * PAD
                out_ref[slot * WIN_LEVEL + level, lat] = placed[start : start + WIN_LON, :]


def finish_kernel(rows_ref, sums_ref, bias_ref, attend_ref, output_ref):
    types, heads, count = bias_ref.shape
    width = output_ref.shape[0]
    for c in range(3):
        attend_ref[c] = sums_ref[c * width : (c + 1) * width, :].astype(F32).T
    output_ref[...] = sums_ref[3 * width :, :].astype(F32)
    kind = rows_ref[:, count : count + 1].astype(F32)
    head = rows_ref[:, count + 1 : count + 2].astype(F32)
    lane = lax.broadcasted_iota(jnp.int32, (rows_ref.shape[0], types), 1).astype(F32)
    for h in range(heads):
        sel = one_hot((kind == lane) & (head == float(h)))
        bias_ref[:, h, :] = dot_tn(sel, rows_ref[:, :count])


SMEM = pl.BlockSpec(memory_space=pltpu.SMEM)
VMEM = pl.BlockSpec(memory_space=pltpu.VMEM)


def exchange(x, axis, shift, sign):
    count = lax.axis_size(axis)
    ahead = lax.ppermute(x, axis, [(i, (i - sign) % count) for i in range(count)])
    if count == 2:
        return ahead
    behind = lax.ppermute(x, axis, [(i, (i + sign) % count) for i in range(count)])
    return jnp.where(shift[0] <= WIN_LON // 2, ahead, behind)


def table_rows(bias_table, kinds):
    slots, heads = kinds.shape[0], bias_table.shape[1]
    chosen = jnp.take(bias_table, kinds, axis=0)
    shaped = chosen.reshape(slots, heads, WIN_LEVEL, WIN_LEVEL, WIN_LAT, WIN_LAT, OFFSETS)
    turned = shaped[..., ::-1].transpose(0, 1, 2, 4, 6, 3, 5)
    turned = turned.reshape(slots, heads, ROWS, OFFSETS, ROWS)
    turned = jnp.pad(turned, ((0, 0),) * 4 + ((0, PAD - ROWS),), constant_values=MASKED)
    turned = turned.reshape(slots, heads, ROWS, OFFSETS * PAD)
    span = -(-OFFSETS * PAD // LANES) * LANES
    edges = ((0, 0), (0, 0), (0, PAD - ROWS), (0, span - OFFSETS * PAD))
    return jnp.pad(turned, edges).reshape(slots, heads * PAD, span)


def natural_rows(folded, kinds, heads):
    slots = folded.shape[0]
    shaped = folded[:, :, : OFFSETS * PAD].reshape(slots, heads, PAD, OFFSETS, PAD)
    shaped = shaped[:, :, :ROWS, ::-1, :ROWS]
    shaped = shaped.reshape(slots, heads, WIN_LEVEL, WIN_LAT, OFFSETS, WIN_LEVEL, WIN_LAT)
    rows = shaped.transpose(0, 1, 2, 5, 3, 6, 4).reshape(slots * heads, -1).astype(BF16)
    kind = jnp.repeat(kinds, heads).astype(BF16)
    head = jnp.tile(jnp.arange(heads), slots).astype(BF16)
    extra = -rows.shape[1] % LANES
    tail = jnp.stack([kind, head] + [jnp.zeros_like(kind)] * (extra - 2), axis=1)
    return jnp.concatenate([rows, tail], axis=1)


def per_device(
    features, attend_weight, output_weight, bias_table, bias_type, window_shift, grad_out
):
    levels, lat_rows, lon_cols, model_width = features.shape
    assert lat_rows == WIN_LAT and lon_cols == WIN_LON and levels % WIN_LEVEL == 0
    slots = levels // WIN_LEVEL
    width, heads = output_weight.shape[0], bias_table.shape[1]
    half_rows = WIN_LON // 2 * ROWS
    n_head = lax.axis_size("head")
    kinds = bias_type[:, 0]
    shape = jax.ShapeDtypeStruct
    slab = pl.pallas_call(
        pack_kernel,
        name="pack",
        out_shape=shape((2, slots, half_rows, model_width), BF16),
        in_specs=[SMEM, VMEM, VMEM],
        out_specs=VMEM,
        scratch_shapes=[pltpu.VMEM((2, slots, ROWS * PAD, model_width), BF16)],
    )(window_shift, features, grad_out)
    far = exchange(slab, "lon", window_shift, 1)
    table = table_rows(bias_table, kinds)
    *pieces, sums, folded = pl.pallas_call(
        main_kernel,
        name="main",
        out_shape=[shape((slots * TOKENS, width), BF16)] * n_head
        + [
            shape((4, width, model_width), BF16),
            shape(table.shape, F32),
        ],
        in_specs=[SMEM] + [VMEM] * 6,
        out_specs=[VMEM] * (n_head + 2),
        scratch_shapes=[
            pltpu.VMEM((2, ROWS * PAD, model_width), BF16),
            pltpu.VMEM((heads, WIDE, WIDE), F32),
        ],
    )(window_shift, features, grad_out, far, attend_weight, output_weight, table)
    parts = [pieces[0]]
    for step in range(1, n_head):
        ring = [(i, (i + step) % n_head) for i in range(n_head)]
        parts.append(lax.ppermute(pieces[step], "head", ring))
    summed, back = pl.pallas_call(
        sum_kernel,
        name="sum_heads",
        out_shape=[
            shape((slots * TOKENS, width), BF16),
            shape((slots * half_rows, width), BF16),
        ],
        in_specs=[SMEM] + [VMEM] * n_head,
        out_specs=[VMEM] * 2,
    )(window_shift, *parts)
    returned = exchange(back, "lon", window_shift, -1)
    feature_grad = pl.pallas_call(
        place_kernel,
        name="place",
        out_shape=shape((levels, lat_rows, lon_cols, width), BF16),
        in_specs=[SMEM, VMEM, VMEM],
        out_specs=VMEM,
    )(window_shift, summed, returned)
    every = ("lon", "lat")
    n_every = lax.axis_size("lon") * lax.axis_size("lat")
    shares = sums.reshape(n_every, 4 * width // n_every, model_width)
    shares = lax.all_to_all(shares, every, 0, 0)
    share = jnp.sum(shares.astype(F32), axis=0).astype(BF16)
    sums = lax.all_gather(share, every, axis=0, tiled=True)
    rows = lax.all_gather(natural_rows(folded, kinds, heads), every, axis=0, tiled=True)
    bias_grad, attend_grad, output_grad = pl.pallas_call(
        finish_kernel,
        name="finish",
        out_shape=[
            shape(bias_table.shape, F32),
            shape(attend_weight.shape, F32),
            shape(output_weight.shape, F32),
        ],
        in_specs=[VMEM] * 2,
        out_specs=[VMEM] * 3,
    )(rows, sums)
    return (feature_grad, attend_grad, output_grad, bias_grad)


def solution(mesh):
    placed = (
        P(None, "lat", "lon", None),
        P(None, None, "head"),
        P("head", None),
        P(None, "head", None),
        P(None, "lat"),
        P(),
        P(None, "lat", "lon", None),
    )
    return jax.shard_map(
        per_device,
        mesh=mesh,
        in_specs=placed,
        out_specs=(
            P(None, "lat", "lon", "head"),
            P(None, None, "head"),
            P("head", None),
            P(None, "head", None),
        ),
        check_vma=False,
    )
```

profile of v0, /device:TPU:0, one launch (start us, length us, event | category | flops | bytes accessed | tf_op | source)
XLA Modules:
  0.0 103.4 jit_solution(5682640093825459214)
XLA Ops:
  1.5 2.0 %copy.57.x_ref = bf16[8,6,12,384]{3,2,1,0:T(8,128)(2,1)} copy(bf16[8,6,12,384]{3,0,2,1:T(8,128)(2,1)} %param.7) | data formatting | bytes 884736 | tf_op args[0]
  4.4 2.4 %pack.1 = bf16[2,4,72,384]{3,2,1,0:T(8,128)(2,1)} custom-call(s32[1]{0:T(128)S(6)} %copy.70.shift_ref, bf16[8,6,12,384]{3,2,1,0:T(8,128)(2,1)} %copy.57.x_ref, bf16[8,6,12,384]{3,2,1,0:T(8,128)(2,1)} %copy.58.g_ref), custom_call_target="tpu_custom_call" | custom-call | tf_op jit(solution)/shard_map/pack/pallas_call | solution.py:285
  6.8 3.0 %collective-permute-start = (bf16[2,4,72,384]{3,2,1,0:T(8,128)(2,1)}, bf16[2,4,72,384]{3,2,1,0:T(8,128)(2,1)}, u32[]{:S(2)}, u32[]{:S(2)}) collective-permute-start(bf16[2,4,72,384]{3,2,1,0:T(8,128)(2,1)} %pack.1), channel_id=1, source_target_pairs={{0,16},{16,0},{1,17},{17,1},{2,18},{18,2},{3,19},{19,3},{4,20},{20... | collective-permute-start | bytes 1327112 | tf_op jit(solution)/shard_map/ppermute | solution.py:241
  11.6 1.8 %gather.7 = f32[4,3,2,2,6,6,23]{6,5,4,3,2,0,1:T(8,128)} reshape(f32[4,3,3312]{2,0,1:T(4,128)S(1)} %gather_fusion) | data formatting | bytes 317952 | tf_op jit(solution)/shard_map/jit(_take)/gather | solution.py:250
  13.4 2.5 %broadcast_select_fusion = f32[4,3,2,2,6,6,23]{6,5,4,3,2,0,1:T(8,128)} fusion(f32[4,3,2,2,6,6,23]{6,5,4,3,2,0,1:T(8,128)} %gather.7, pred[4]{0:T(512)(128)(4,1)S(1)} %and_bitcast_fusion), kind=kLoop, calls=%fused_computation.1 | loop fusion | flops 39744 | bytes 317956 | tf_op jit(solution)/shard_map/jit(_take)/select_n | solution.py:250
  15.9 3.4 %rev.6 = f32[4,3,2,2,6,6,23]{6,5,4,3,2,0,1:T(8,128)} reverse(f32[4,3,2,2,6,6,23]{6,5,4,3,2,0,1:T(8,128)} %broadcast_select_fusion), dimensions={6} | reverse | bytes 317952 | tf_op jit(solution)/shard_map/rev | solution.py:252
  19.3 1.8 %copy.54 = f32[4,3,2,6,23,2,6]{4,0,6,5,3,2,1:T(4,128)S(1)} copy(f32[4,3,2,6,23,2,6]{4,6,3,5,2,0,1:T(8,128)} %bitcast.18) | data formatting | bytes 317952 | tf_op jit(solution)/shard_map/transpose | solution.py:252
  21.2 2.1 %copy.68 = f32[4,3,12,23,12]{4,3,0,2,1:T(8,128)} copy(f32[4,3,12,23,12]{3,0,4,2,1:T(4,128)S(1)} %bitcast.19) | data formatting | bytes 317952
  23.2 2.9 %pad.8.clone = f32[4,3,12,23,16]{4,3,0,2,1:T(8,128)} pad(f32[4,3,12,23,12]{4,3,0,2,1:T(8,128)} %copy.68, f32[]{:T(128)} %constant.24.clone.1), padding=0_0x0_0x0_0x0_0x0_4 | pad | bytes 370948 | tf_op jit(solution)/shard_map/jit(_pad)/pad | solution.py:254
  26.1 2.0 %reshape.58 = f32[4,3,12,368]{3,0,2,1:T(4,128)S(1)} reshape(f32[4,3,12,23,16]{4,3,0,2,1:T(8,128)} %pad.8.clone) | data formatting | bytes 423936 | tf_op jit(solution)/shard_map/reshape | solution.py:255
  28.9 13.5 %main.1 = (bf16[576,96]{1,0:T(8,128)(2,1)}, bf16[576,96]{1,0:T(8,128)(2,1)}, bf16[576,96]{1,0:T(8,128)(2,1)}, bf16[576,96]{1,0:T(8,128)(2,1)}, bf16[4,96,384]{2,1,0:T(8,128)(2,1)}, /*index=5*/f32[4,48,384]{2,1,0:T(8,128)}) custom-call(s32[1]{0:T(128)S(6)} %copy.70.shift_ref, bf16[8,6,12,384]{3,2,1,0:T(8,128)(2,1)} %copy.57.x_ref, ...), custom_call_target="tpu_custom_call" | custom-call | tf_op jit(solution)/shard_map/main/pallas_call | solution.py:295
  42.4 4.1 %all-to-all-start = ((bf16[8,48,384]{2,1,0:T(8,128)(2,1)}), bf16[8,48,384]{2,1,0:T(8,128)(2,1)}, u32[]{:S(2)}, u32[]{:S(2)}) async-start(bf16[8,48,384]{2,1,0:T(8,128)(2,1)} %bitcast.23), calls=%async_computation | async-start | bytes 589824 | tf_op jit(solution)/shard_map/all_to_all | solution.py:335
  46.6 1.6 %collective-permute-start.1 = (bf16[576,96]{1,0:T(8,128)(2,1)}, bf16[576,96]{1,0:T(8,128)(2,1)}, u32[]{:S(2)}, u32[]{:S(2)}) collective-permute-start(bf16[576,96]{1,0:T(8,128)(2,1)} %get-tuple-element.16), channel_id=1, source_target_pairs={{0,1},{1,2},{2,3},{3,0},{4,5},{5,6},{6,7},{7,4},{8,9},{9,10},{10,1... | collective-permute-start | bytes 331784 | tf_op jit(solution)/shard_map/ppermute | solution.py:313
  48.2 2.6 %collective-permute-start.2 = (bf16[576,96]{1,0:T(8,128)(2,1)}, bf16[576,96]{1,0:T(8,128)(2,1)}, u32[]{:S(2)}, u32[]{:S(2)}) collective-permute-start(bf16[576,96]{1,0:T(8,128)(2,1)} %get-tuple-element.17), channel_id=1, source_target_pairs={{0,2},{1,3},{2,0},{3,1},{4,6},{5,7},{6,4},{7,5},{8,10},{9,11},{10,... | collective-permute-start | bytes 331784 | tf_op jit(solution)/shard_map/ppermute | solution.py:313
  50.8 1.3 %collective-permute-start.3 = (bf16[576,96]{1,0:T(8,128)(2,1)}, bf16[576,96]{1,0:T(8,128)(2,1)}, u32[]{:S(2)}, u32[]{:S(2)}) collective-permute-start(bf16[576,96]{1,0:T(8,128)(2,1)} %get-tuple-element.18), channel_id=1, source_target_pairs={{0,3},{1,0},{2,1},{3,2},{4,7},{5,4},{6,5},{7,6},{8,11},{9,8},{10,9... | collective-permute-start | bytes 331784 | tf_op jit(solution)/shard_map/ppermute | solution.py:313
  52.2 1.0 slice.6
  53.2 1.8 %reshape.60 = bf16[4,3,16,23,16]{4,3,2,1,0:T(8,128)(2,1)} reshape(bf16[4,48,368]{2,1,0:T(8,128)(2,1)S(1)} %slice.6) | data formatting | bytes 282624 | tf_op jit(solution)/shard_map/reshape | solution.py:263
  55.0 1.3 %slice.10 = bf16[4,3,12,23,12]{4,3,2,1,0:T(8,128)(2,1)S(1)} slice(bf16[4,3,16,23,16]{4,3,2,1,0:T(8,128)(2,1)} %reshape.60), slice={[0:4], [0:3], [0:12], [0:23], [0:12]} | slice | bytes 158976 | tf_op jit(solution)/shard_map/slice | solution.py:264
  56.4 2.0 %copy.67 = bf16[4,3,12,23,12]{3,0,4,2,1:T(4,128)(2,1)} copy(bf16[4,3,12,23,12]{4,3,2,1,0:T(8,128)(2,1)S(1)} %slice.10) | data formatting | bytes 158976
  58.4 3.6 %rev.7 = bf16[4,3,12,23,12]{3,0,4,2,1:T(4,128)(2,1)} reverse(bf16[4,3,12,23,12]{3,0,4,2,1:T(4,128)(2,1)} %copy.67), dimensions={3} | reverse | bytes 158976 | tf_op jit(solution)/shard_map/rev | solution.py:264
  62.0 1.1 %copy.61 = bf16[4,3,2,2,6,6,23]{6,5,4,3,2,1,0:T(8,128)(2,1)S(1)} copy(bf16[4,3,2,2,6,6,23]{6,0,5,3,4,2,1:T(4,128)(2,1)} %bitcast.20) | data formatting | bytes 158976 | tf_op jit(solution)/shard_map/convert_element_type | solution.py:266
  63.9 2.0 %sum_heads.1 = (bf16[576,96]{1,0:T(8,128)(2,1)}, bf16[288,96]{1,0:T(8,128)(2,1)}) custom-call(s32[1]{0:T(128)S(6)} %copy.70.shift_ref, bf16[576,96]{1,0:T(8,128)(2,1)} %get-tuple-element.15.refs_0_, bf16[576,96]{1,0:T(8,128)(2,1)} %collective-permute-done.1.refs_1_, bf16[576,96]{1,0:T(8,128)(2,1)} %collective-permute-done.2.refs_2_, ...), custom_call_target="tpu_custom_call" | custom-call | tf_op jit(solution)/shard_map/sum_heads/pallas_call | solution.py:314
  65.9 1.9 %collective-permute-start.4 = (bf16[288,96]{1,0:T(8,128)(2,1)}, bf16[288,96]{1,0:T(8,128)(2,1)}, u32[]{:S(2)}, u32[]{:S(2)}) collective-permute-start(bf16[288,96]{1,0:T(8,128)(2,1)} %get-tuple-element.20), channel_id=1, source_target_pairs={{0,16},{16,0},{1,17},{17,1},{2,18},{18,2},{3,19},{19,3},{4,20},{20... | collective-permute-start | bytes 165896 | tf_op jit(solution)/shard_map/ppermute | solution.py:241
  67.8 10.5 %all-gather = bf16[8,12,3328]{2,1,0:T(8,128)(2,1)S(1)} all-gather(bf16[1,12,3328]{2,1,0:T(8,128)(2,1)S(1)} %bitcast.22), channel_id=1, replica_groups=mesh['lon'=2,'lat'=4,'head'=4] {'lon','lat'}, dimensions={0}, use_global_device_ids=true | all-gather | bytes 718848 | tf_op jit(solution)/shard_map/all_gather | solution.py:338
  78.3 1.0 reshape.71.rows_ref
  79.2 2.0 %place.1 = bf16[8,6,12,96]{3,2,1,0:T(8,128)(2,1)} custom-call(s32[1]{0:T(128)S(6)} %copy.70.shift_ref, bf16[576,96]{1,0:T(8,128)(2,1)} %get-tuple-element.19.summed_ref, bf16[288,96]{1,0:T(8,128)(2,1)} %collective-permute-done.4.back_ref), custom_call_target="tpu_custom_call" | custom-call | tf_op jit(solution)/shard_map/place/pallas_call | solution.py:325
  81.2 1.6 %copy.64 = bf16[8,6,12,96]{3,0,2,1:T(8,128)(2,1)} copy(bf16[8,6,12,96]{3,2,1,0:T(8,128)(2,1)} %place.1) | data formatting | bytes 221184
  82.8 1.0 reduce_sum.12
  83.9 9.5 %all_gather.7.sums_ref = bf16[384,384]{1,0:T(8,128)(2,1)} all-gather(bf16[48,384]{1,0:T(8,128)(2,1)S(1)} %reduce_sum.12), channel_id=1, replica_groups=mesh['lon'=2,'lat'=4,'head'=4] {'lon','lat'}, dimensions={0}, use_global_device_ids=true | all-gather | bytes 331776 | tf_op jit(solution)/shard_map/all_gather | solution.py:337
  93.4 4.1 %finish.1 = (f32[64,3,3312]{2,1,0:T(4,128)}, f32[3,384,96]{2,1,0:T(8,128)}, f32[96,384]{1,0:T(8,128)}) custom-call(bf16[96,3328]{1,0:T(8,128)(2,1)} %reshape.71.rows_ref, bf16[384,384]{1,0:T(8,128)(2,1)} %all_gather.7.sums_ref), custom_call_target="tpu_custom_call" | custom-call | tf_op jit(solution)/shard_map/finish/pallas_call | solution.py:339
  97.4 2.1 %copy.65 = f32[3,384,96]{1,2,0:T(8,128)} copy(f32[3,384,96]{2,1,0:T(8,128)} %get-tuple-element.39) | data formatting | bytes 884736
  99.5 3.9 %copy.66 = f32[64,3,3312]{2,0,1:T(8,128)} copy(f32[64,3,3312]{2,1,0:T(4,128)} %get-tuple-element.41) | data formatting | bytes 5087232
  (31 shorter events, 4.5 us)
Async XLA Ops:
  0.6 10.1 %copy-start = (f32[64,3,3312]{2,0,1:T(8,128)S(1)}, f32[64,3,3312]{2,0,1:T(8,128)}, u32[]{:S(2)}) copy-start(f32[64,3,3312]{2,0,1:T(8,128)} %param.10) | copy-start | bytes 7630852
  0.6 2.8 %copy-start.1 = (bf16[8,6,12,384]{3,0,2,1:T(8,128)(2,1)S(1)}, bf16[8,6,12,384]{3,0,2,1:T(8,128)(2,1)}, u32[]{:S(2)}) copy-start(bf16[8,6,12,384]{3,0,2,1:T(8,128)(2,1)} %param.13) | copy-start | bytes 1327108
  3.5 6.3 %copy-start.3 = (s32[4,1]{0,1:T(1,128)S(1)}, s32[4,1]{0,1:T(1,128)}, u32[]{:S(2)}) copy-start(s32[4,1]{0,1:T(1,128)} %param.11) | copy-start | bytes 52
  3.5 6.3 %copy-start.2 = (bf16[3,384,96]{1,2,0:T(8,128)(2,1)S(1)}, bf16[3,384,96]{1,2,0:T(8,128)(2,1)}, u32[]{:S(2)}) copy-start(bf16[3,384,96]{1,2,0:T(8,128)(2,1)} %param.8) | copy-start | bytes 663556
  6.8 22.1 %collective-permute-start = (bf16[2,4,72,384]{3,2,1,0:T(8,128)(2,1)}, bf16[2,4,72,384]{3,2,1,0:T(8,128)(2,1)}, u32[]{:S(2)}, u32[]{:S(2)}) collective-permute-start(bf16[2,4,72,384]{3,2,1,0:T(8,128)(2,1)} %pack.1), channel_id=1, source_target_pairs={{0,16},{16,0},{1,17},{17,1},{2,18},{18,2},{3,19},{19,3},{4,20},{20... | collective-permute-start | bytes 1327112 | tf_op jit(solution)/shard_map/ppermute | solution.py:241
  42.4 40.5 %all-to-all-start = ((bf16[8,48,384]{2,1,0:T(8,128)(2,1)}), bf16[8,48,384]{2,1,0:T(8,128)(2,1)}, u32[]{:S(2)}, u32[]{:S(2)}) async-start(bf16[8,48,384]{2,1,0:T(8,128)(2,1)} %bitcast.23), calls=%async_computation | async-start | bytes 589824 | tf_op jit(solution)/shard_map/all_to_all | solution.py:335
  46.6 17.2 %collective-permute-start.1 = (bf16[576,96]{1,0:T(8,128)(2,1)}, bf16[576,96]{1,0:T(8,128)(2,1)}, u32[]{:S(2)}, u32[]{:S(2)}) collective-permute-start(bf16[576,96]{1,0:T(8,128)(2,1)} %get-tuple-element.16), channel_id=1, source_target_pairs={{0,1},{1,2},{2,3},{3,0},{4,5},{5,6},{6,7},{7,4},{8,9},{9,10},{10,1... | collective-permute-start | bytes 331784 | tf_op jit(solution)/shard_map/ppermute | solution.py:313
  48.2 15.7 %collective-permute-start.2 = (bf16[576,96]{1,0:T(8,128)(2,1)}, bf16[576,96]{1,0:T(8,128)(2,1)}, u32[]{:S(2)}, u32[]{:S(2)}) collective-permute-start(bf16[576,96]{1,0:T(8,128)(2,1)} %get-tuple-element.17), channel_id=1, source_target_pairs={{0,2},{1,3},{2,0},{3,1},{4,6},{5,7},{6,4},{7,5},{8,10},{9,11},{10,... | collective-permute-start | bytes 331784 | tf_op jit(solution)/shard_map/ppermute | solution.py:313
  50.8 13.1 %collective-permute-start.3 = (bf16[576,96]{1,0:T(8,128)(2,1)}, bf16[576,96]{1,0:T(8,128)(2,1)}, u32[]{:S(2)}, u32[]{:S(2)}) collective-permute-start(bf16[576,96]{1,0:T(8,128)(2,1)} %get-tuple-element.18), channel_id=1, source_target_pairs={{0,3},{1,0},{2,1},{3,2},{4,7},{5,4},{6,5},{7,6},{8,11},{9,8},{10,9... | collective-permute-start | bytes 331784 | tf_op jit(solution)/shard_map/ppermute | solution.py:313
  65.9 13.4 %collective-permute-start.4 = (bf16[288,96]{1,0:T(8,128)(2,1)}, bf16[288,96]{1,0:T(8,128)(2,1)}, u32[]{:S(2)}, u32[]{:S(2)}) collective-permute-start(bf16[288,96]{1,0:T(8,128)(2,1)} %get-tuple-element.20), channel_id=1, source_target_pairs={{0,16},{16,0},{1,17},{17,1},{2,18},{18,2},{3,19},{19,3},{4,20},{20... | collective-permute-start | bytes 165896 | tf_op jit(solution)/shard_map/ppermute | solution.py:241
where the time goes:
time: 104 us; the launch traced here: 103 us
  local copies, waits for them, and re-layouts  39.9 us (38%)
  Pallas kernels  24 us (23%)
  blocking collectives  20 us (19%)
  starting transfers between devices  14.5 us (14%)
  other arithmetic  3.52 us (3%)
  between operations  1.57 us (2%)
    unnamed x18, local copies, waits for them, and re-layouts  16.6 us
    pallas_call x1, Pallas kernels, per_device(): pl.pallas_call(main_kernel, name='main', out_shape=[shape((slots * TOKENS...  13.5 us
    all_gather x1, blocking collectives, per_device(): lax.all_gather(natural_rows(folded, kinds, heads), every, axis=0, tiled=T...  10.5 us
    all_gather x1, blocking collectives, per_device(): sums = lax.all_gather(share, every, axis=0, tiled=True)  9.5 us
    ppermute x3, starting transfers between devices, per_device(): parts.append(lax.ppermute(pieces[step], 'head', ring))  5.52 us
    ppermute x2, starting transfers between devices, exchange(): lax.ppermute(x, axis, [(i, (i - sign) % count) for i in range(count)])  4.88 us
    pallas_call x1, Pallas kernels, per_device(): pl.pallas_call(finish_kernel, name='finish', out_shape=[shape(bias_table....  4.1 us
    all_to_all x1, starting transfers between devices, per_device(): shares = lax.all_to_all(shares, every, 0, 0)  4.06 us
  transfers between devices with their start and end apart: 6, of which 0 were waited for; matrix products, arithmetic and copies ran while one was open for 32% of the time, Pallas kernels for 4%

commit v1 on v0

v1 whole, which is shorter than its diff:
```python
import jax
import jax.numpy as jnp
from jax import lax
from jax.experimental import pallas as pl
from jax.experimental.pallas import tpu as pltpu
from jax.sharding import PartitionSpec as P

WIN_LEVEL = 2
WIN_LAT = 6
WIN_LON = 12
ROWS = WIN_LEVEL * WIN_LAT
PAD = 16
WIDE = WIN_LON * PAD
HALF = WIN_LON // 2
OFFSETS = 2 * WIN_LON - 1
PIECE = WIN_LAT * OFFSETS
LANES = 128
SPAN = -(-OFFSETS * PAD // LANES) * LANES
MASKED = -1e30
F32 = jnp.float32
BF16 = jnp.bfloat16
SMEM = pl.BlockSpec(memory_space=pltpu.SMEM)
VMEM = pl.BlockSpec(memory_space=pltpu.VMEM)
ANY = pl.BlockSpec(memory_space=pl.ANY)


def dot_nn(a, b):
    return lax.dot_general(a, b, (((1,), (0,)), ((), ())), preferred_element_type=F32)


def dot_nt(a, b):
    return lax.dot_general(a, b, (((1,), (1,)), ((), ())), preferred_element_type=F32)


def dot_tn(a, b):
    return lax.dot_general(a, b, (((0,), (0,)), ((), ())), preferred_element_type=F32)


def grid_of(rows, cols):
    shape = (rows, cols)
    return lax.broadcasted_iota(jnp.int32, shape, 0), lax.broadcasted_iota(jnp.int32, shape, 1)


def one_hot(hit):
    return jnp.where(hit, 1.0, 0.0).astype(BF16)


def window_order(levels):
    row, src = grid_of(levels // WIN_LEVEL * PAD, WIN_LAT * levels)
    bits = levels.bit_length() - 1
    lat = lax.shift_right_logical(src, bits)
    level = lax.bitwise_and(src, levels - 1)
    slot = lax.shift_right_logical(level, 1)
    return one_hot(row == slot * PAD + lax.bitwise_and(level, 1) * WIN_LAT + lat)


def offset_order(level_j):
    src, lane = grid_of(2 * LANES, SPAN)
    back = lax.shift_right_logical(lane, 4)
    lat = lax.bitwise_and(lane, PAD - 1) - level_j * WIN_LAT
    hit = (src == lat * OFFSETS + OFFSETS - 1 - back) & (lat >= 0) & (lat < WIN_LAT)
    return one_hot(hit & (back < OFFSETS))


def table_pieces():
    for level_i in range(WIN_LEVEL):
        for level_j in range(WIN_LEVEL):
            for lat_i in range(WIN_LAT):
                index = (level_i * WIN_LEVEL + level_j) * WIN_LAT + lat_i
                yield level_i * WIN_LAT + lat_i, level_j, index * PIECE


def pack_kernel(shift_ref, x_ref, g_ref, out_ref, sems):
    base = jnp.where(shift_ref[0] <= HALF, 0, WIN_LON - HALF)
    copies = [
        pltpu.make_async_copy(ref.at[:, pl.ds(base, HALF)], out_ref.at[i], sems.at[i])
        for i, ref in enumerate((x_ref, g_ref))
    ]
    for copy in copies:
        copy.start()
    for copy in copies:
        copy.wait()


def project(rows_x, rows_g, weights):
    width = 3 * LANES
    return jnp.concatenate(
        [dot_nt(rows_x, weights[:width]), dot_nt(rows_g, weights[width:])], axis=1
    )


def prepare_kernel(
    kind_ref, x_ref, g_ref, weight_ref, out_weight_ref, table_ref,
    turned_ref, projected_ref, weights_ref, natural_ref, pieces_ref,
):
    lats, cols, levels, depth = x_ref.shape
    heads = table_ref.shape[0]
    slots = kind_ref.shape[0]
    count = table_ref.shape[2]
    width = out_weight_ref.shape[0]
    weights_ref[...] = jnp.zeros(weights_ref.shape, BF16)
    for c in range(3):
        weights_ref[c * LANES : c * LANES + width, :] = weight_ref[c]
    weights_ref[3 * LANES : 3 * LANES + width, :] = out_weight_ref[...]
    flat = (lats * cols * levels, depth)
    projected = project(x_ref[...].reshape(flat), g_ref[...].reshape(flat), weights_ref[...])
    for lat in range(lats):
        for col in range(cols):
            start = (lat * cols + col) * levels
            projected_ref[col, lat * levels : (lat + 1) * levels, :] = projected[
                start : start + levels, :
            ].astype(BF16)
    natural_ref[...] = jnp.zeros(natural_ref.shape, F32)
    pieces_ref[...] = jnp.zeros(pieces_ref.shape, F32)
    for h in range(heads):
        for slot in range(slots):
            row = h * slots + slot
            natural_ref[row : row + 1, :count] = table_ref[h, pl.ds(kind_ref[slot, 0], 1), :]
    number = heads * slots
    for place, level_j, start in table_pieces():
        low = start // LANES * LANES
        block = natural_ref[:, low : low + 3 * LANES]
        if start > low:
            block = pltpu.roll(block, 3 * LANES - (start - low), 1)
        for t in range(2):
            pieces_ref[2 * level_j + t, pl.ds(place, number, stride=PAD), :] = block[
                :number, t * LANES : (t + 1) * LANES
            ]
    turned = jnp.zeros((number * PAD, SPAN), F32)
    for level_j in range(WIN_LEVEL):
        order = offset_order(level_j)
        rest = jnp.concatenate([pieces_ref[2 * level_j], pieces_ref[2 * level_j + 1]], axis=1)
        for _ in range(3):
            part = rest.astype(BF16)
            turned = turned + dot_nn(part, order)
            rest = rest - part.astype(F32)
    lane = lax.broadcasted_iota(jnp.int32, turned.shape, 1)
    turned = jnp.where(lax.bitwise_and(lane, PAD - 1) < ROWS, turned, MASKED)
    for h in range(heads):
        turned_ref[h] = turned[h * slots * PAD : (h + 1) * slots * PAD, :]


def main_kernel(
    shift_ref, x_ref, g_ref, far_ref, near_ref, weights_ref, turned_ref, *rest
):
    n_head = lax.axis_size("head")
    pieces = rest[:n_head]
    sums_ref, folded_ref = rest[n_head : n_head + 2]
    beyond_ref, own_ref, ordered_ref, bias_ref, given_ref, back_ref, chunk_ref = rest[n_head + 2 :]
    lats, cols, levels, depth = x_ref.shape
    width = sums_ref.shape[1]
    heads, slot_rows = turned_ref.shape[0], turned_ref.shape[1]
    slots = slot_rows // PAD
    size = width // heads
    scaling = size ** (-0.5)
    mine = lax.axis_index("head")
    shift = shift_ref[0]
    low = shift <= HALF
    tall = lats * levels
    flat = (lats * HALF * levels, depth)
    projected = project(far_ref[0].reshape(flat), far_ref[1].reshape(flat), weights_ref[...])
    for lat in range(lats):
        for col in range(HALF):
            start = (lat * HALF + col) * levels
            beyond_ref[col, lat * levels : (lat + 1) * levels, :] = projected[
                start : start + levels, :
            ].astype(BF16)
    order = window_order(levels)
    for col in range(cols):
        at = col + shift
        inside = jnp.logical_xor(low, at >= cols)
        local = jnp.where(at >= cols, at - cols, at)
        taken = jnp.where(low, at - cols, at - (cols - HALF))
        taken = jnp.clip(taken, 0, HALF - 1)
        rows = jnp.where(inside, near_ref[local], beyond_ref[taken])
        ordered = dot_nn(order, rows).astype(BF16)
        for slot in range(slots):
            ordered_ref[slot, col * PAD : (col + 1) * PAD, :] = ordered[
                slot * PAD : (slot + 1) * PAD, :
            ]
        for array, ref in enumerate((x_ref, g_ref)):
            for lat in range(lats):
                start = col * tall + lat * levels
                own_ref[array, start : start + levels, :] = jnp.where(
                    inside, ref[lat, local], far_ref[array, lat, taken]
                )
    lane = lax.broadcasted_iota(jnp.int32, (WIDE, LANES), 1)
    masks = [(lane >= h * size) & (lane < (h + 1) * size) for h in range(heads)]
    none = jnp.zeros((WIDE, LANES), BF16)
    for slot in range(slots):
        query = ordered_ref[slot, :, :LANES]
        key = ordered_ref[slot, :, LANES : 2 * LANES]
        value = ordered_ref[slot, :, 2 * LANES : 3 * LANES]
        grad_attended = ordered_ref[slot, :, 3 * LANES :]
        at = slice(slot * PAD, (slot + 1) * PAD)
        attended = jnp.zeros((WIDE, LANES), F32)
        grad_query = jnp.zeros((WIDE, LANES), F32)
        grad_key = jnp.zeros((WIDE, LANES), F32)
        grad_value = jnp.zeros((WIDE, LANES), F32)
        for h in range(heads):
            table = turned_ref[h, at, :]
            for col in range(WIN_LON):
                by = (WIN_LON - 1 - col) * PAD
                moved = table if by == 0 else pltpu.roll(table, SPAN - by, 1)
                bias_ref[h, col * PAD : (col + 1) * PAD, :] = moved[:, :WIDE]
            query_h = jnp.where(masks[h], query, none)
            key_h = jnp.where(masks[h], key, none)
            value_h = jnp.where(masks[h], value, none)
            grad_h = jnp.where(masks[h], grad_attended, none)
            scores = dot_nt(query_h, key) * scaling + bias_ref[h]
            raised = jnp.exp(scores - jnp.max(scores, axis=1, keepdims=True))
            softened = raised * (1.0 / jnp.sum(raised, axis=1, keepdims=True))
            softened_half = softened.astype(BF16)
            attended = attended + dot_nn(softened_half, value_h)
            grad_value = grad_value + dot_tn(softened_half, grad_h)
            grad_softened = dot_nt(grad_h, value)
            inner = jnp.sum(softened * grad_softened, axis=1, keepdims=True)
            grad_scores = softened * (grad_softened - inner)
            grad_half = grad_scores.astype(BF16)
            grad_query = grad_query + dot_nn(grad_half, key_h)
            grad_key = grad_key + dot_tn(grad_half, query_h)
            padded = jnp.concatenate([grad_scores, jnp.zeros((WIDE, SPAN - WIDE), F32)], axis=1)
            total = jnp.zeros((PAD, SPAN), F32)
            for col in range(WIN_LON):
                by = (WIN_LON - 1 - col) * PAD
                part = padded[col * PAD : (col + 1) * PAD, :]
                total = total + (part if by == 0 else pltpu.roll(part, by, 1))
            folded_ref[h, at, :] = total
        results = (grad_query * scaling, grad_key * scaling, grad_value, attended)
        for c, result in enumerate(results):
            rounded = result.astype(BF16)
            for col in range(WIN_LON):
                given_ref[col, at, c * LANES : (c + 1) * LANES] = rounded[
                    col * PAD : (col + 1) * PAD, :
                ]
    for col in range(WIN_LON):
        back_ref[col * tall : (col + 1) * tall, :] = dot_tn(order, given_ref[col]).astype(BF16)
    grads = 3 * LANES
    piece = dot_nn(back_ref[:, :grads], weights_ref[:grads, :])
    group = WIN_LON // 4 * tall
    third = width // 3
    for to in range(n_head):
        lanes = piece[:, to * width : (to + 1) * width]
        for g in range(3):
            tail = lanes[3 * group :, g * third : (g + 1) * third]
            chunk_ref[to, g * group : (g + 1) * group, :] = jnp.concatenate(
                [lanes[g * group : (g + 1) * group, :], tail], axis=1
            ).astype(BF16)
    for step in range(n_head):
        pieces[step][...] = chunk_ref[lax.rem(mine + step, n_head)]
    summed = dot_tn(back_ref[:, :grads], own_ref[0])
    for c in range(3):
        sums_ref[c] = summed[c * LANES : c * LANES + width, :].astype(BF16)
    sums_ref[3] = dot_tn(back_ref[:, grads:], own_ref[1])[:width, :].astype(BF16)


def bias_kernel(kind_ref, folded_ref, out_ref, pieces_ref, natural_ref, dense_ref):
    heads, slot_rows, span = folded_ref.shape
    slots = slot_rows // PAD
    number = heads * slots
    rows = folded_ref[...].reshape(heads * slot_rows, span).astype(BF16)
    for level_j in range(WIN_LEVEL):
        moved = dot_nt(rows, offset_order(level_j))
        for t in range(2):
            pieces_ref[2 * level_j + t] = moved[:, t * LANES : (t + 1) * LANES]
    natural_ref[...] = jnp.zeros(natural_ref.shape, F32)
    for place, level_j, start in table_pieces():
        low = start // LANES * LANES
        parts = [
            pieces_ref[2 * level_j + t, pl.ds(place, number, stride=PAD), :] for t in range(2)
        ]
        part = jnp.concatenate(parts + [jnp.zeros((number, LANES), F32)], axis=1)
        if start > low:
            part = pltpu.roll(part, start - low, 1)
        at = (slice(0, number), slice(low, low + 3 * LANES))
        natural_ref[at] = natural_ref[at] + part
    count = WIN_LEVEL * WIN_LEVEL * WIN_LAT * PIECE
    low = count // LANES * LANES
    row, lane = grid_of(number, LANES)
    kind = jnp.zeros((number, LANES), F32)
    for slot in range(slots):
        kind = jnp.where(lax.rem(row, slots) == slot, kind_ref[slot, 0].astype(F32), kind)
    at = (slice(0, number), slice(low, low + LANES))
    natural_ref[at] = natural_ref[at] + jnp.where(lane == count - low, kind, 0.0)
    full = low + LANES
    middle = full // 2
    dense_ref[:, :full] = natural_ref[0:8, :full]
    dense_ref[0:4, full:] = natural_ref[8:12, :middle]
    dense_ref[4:8, full:] = natural_ref[8:12, middle:full]
    wide = out_ref.shape[1]
    for j in range(out_ref.shape[0] // 8):
        out_ref[j * 8 : (j + 1) * 8, :] = dense_ref[:, j * wide : (j + 1) * wide].astype(BF16)


def sum_kernel(shift_ref, *refs):
    parts = refs[:-2]
    summed_ref, back_ref = refs[-2:]
    shift = shift_ref[0]
    total = parts[0][...].astype(F32)
    for part in parts[1:]:
        total = total + part[...].astype(F32)
    cols, tall, width = summed_ref.shape
    group = cols // 4
    for g in range(3):
        for i in range(group):
            start = (g * group + i) * tall
            summed_ref[g * group + i] = total[start : start + tall, :width].astype(BF16)
    for i in range(group):
        tails = [
            total[(g * group + i) * tall : (g * group + i + 1) * tall, width:] for g in range(3)
        ]
        summed_ref[3 * group + i] = jnp.concatenate(tails, axis=1).astype(BF16)
    for col in range(HALF):
        source = col - shift + jnp.where(shift <= HALF, WIN_LON, WIN_LON - HALF)
        back_ref[col] = summed_ref[jnp.clip(source, 0, WIN_LON - 1)]


def share_kernel(shares_ref, rows_ref, out_ref):
    total = shares_ref[0].astype(F32)
    for i in range(1, shares_ref.shape[0]):
        total = total + shares_ref[i].astype(F32)
    count = rows_ref.shape[0]
    out_ref[:count, :] = rows_ref[...]
    out_ref[count:, :] = total.astype(BF16)


def finish_kernel(
    shift_ref, gathered_ref, summed_ref, returned_ref,
    feature_ref, attend_ref, output_ref, bias_ref, dense_ref,
):
    shift = shift_ref[0]
    low = shift <= HALF
    lats, cols, levels, width = feature_ref.shape
    for col in range(cols):
        own = jnp.logical_xor(low, col < shift)
        source = jnp.where(low, col - shift, col + cols - shift)
        given = jnp.where(low, col, col - (cols - HALF))
        rows = jnp.where(
            own,
            summed_ref[jnp.clip(source, 0, cols - 1)],
            returned_ref[jnp.clip(given, 0, HALF - 1)],
        )
        for lat in range(lats):
            feature_ref[lat, col] = rows[lat * levels : (lat + 1) * levels, :]
    heads, types, count = bias_ref.shape
    devices, height, wide = gathered_ref.shape
    dense = dense_ref.shape[1] // wide
    share = height - 8 * dense
    for i in range(devices):
        start = i * share
        block = gathered_ref[i, 8 * dense :, :].astype(F32)
        if start < 3 * width:
            attend_ref[start // width, start % width : start % width + share, :] = block
        else:
            output_ref[start - 3 * width : start - 3 * width + share, :] = block
        for j in range(dense):
            dense_ref[i * 8 : (i + 1) * 8, j * wide : (j + 1) * wide] = gathered_ref[
                i, j * 8 : (j + 1) * 8, :
            ]
    full = -(-count // LANES) * LANES
    middle = full // 2
    row, lane = grid_of(devices * 8, types)
    row = lax.bitwise_and(row, 7)
    tag = count - (full - LANES)
    lane = lane.astype(F32)
    kind = dense_ref[:, full - LANES : full].astype(F32)[:, tag : tag + 1]
    for h in range(2):
        mine = (row >= 4 * h) & (row < 4 * h + 4)
        sel = one_hot((kind == lane) & mine)
        bias_ref[h] = dot_tn(sel, dense_ref[:, :full])[:, :count]
    block = dense_ref[:, full + middle - LANES : full + middle].astype(F32)
    below = block[:, tag : tag + 1]
    above = pltpu.roll(block, devices * 8 - 4, 0)[:, tag : tag + 1]
    tail = dense_ref[:, full:]
    bias_ref[2, :, :middle] = dot_tn(one_hot((above == lane) & (row < 4)), tail)
    bias_ref[2, :, middle:] = dot_tn(one_hot((below == lane) & (row >= 4)), tail)[
        :, : count - middle
    ]


def exchange(x, axis, shift, sign):
    count = lax.axis_size(axis)
    ahead = lax.ppermute(x, axis, [(i, (i - sign) % count) for i in range(count)])
    if count == 2:
        return ahead
    behind = lax.ppermute(x, axis, [(i, (i + sign) % count) for i in range(count)])
    return jnp.where(shift[0] <= HALF, ahead, behind)


def per_device(
    features, attend_weight, output_weight, bias_table, bias_type, window_shift, grad_out
):
    levels, lats, cols, depth = features.shape
    slots = levels // WIN_LEVEL
    width, heads = output_weight.shape[0], bias_table.shape[1]
    types, count = bias_table.shape[0], bias_table.shape[2]
    assert lats == WIN_LAT and cols == WIN_LON and levels == 8 and heads * slots == 12
    assert count == WIN_LEVEL * WIN_LEVEL * WIN_LAT * PIECE
    n_head = lax.axis_size("head")
    tall = lats * levels
    number = heads * slots
    shape = jax.ShapeDtypeStruct
    x = features.transpose(1, 2, 0, 3)
    g = grad_out.transpose(1, 2, 0, 3)
    weight = attend_weight.transpose(0, 2, 1)
    table = bias_table.transpose(1, 0, 2)
    slab = pl.pallas_call(
        pack_kernel,
        name="pack",
        out_shape=shape((2, lats, HALF, levels, depth), BF16),
        in_specs=[SMEM, ANY, ANY],
        out_specs=ANY,
        scratch_shapes=[pltpu.SemaphoreType.DMA((2,))],
    )(window_shift, x, g)
    far = exchange(slab, "lon", window_shift, 1)
    natural = -(-count // LANES) * LANES + LANES
    turned, near, weights = pl.pallas_call(
        prepare_kernel,
        name="prepare",
        out_shape=[
            shape((heads, slots * PAD, SPAN), F32),
            shape((cols, tall, 4 * LANES), BF16),
            shape((4 * LANES, depth), BF16),
        ],
        in_specs=[SMEM] + [VMEM] * 5,
        out_specs=[VMEM] * 3,
        scratch_shapes=[
            pltpu.VMEM((PAD, natural), F32),
            pltpu.VMEM((2 * WIN_LEVEL, number * PAD, LANES), F32),
        ],
    )(bias_type, x, g, weight, output_weight, table)
    packed = 3 * (cols // 4) * tall
    *pieces, sums, folded = pl.pallas_call(
        main_kernel,
        name="main",
        out_shape=[shape((packed, LANES), BF16)] * n_head
        + [
            shape((4, width, depth), BF16),
            shape((heads, slots * PAD, SPAN), F32),
        ],
        in_specs=[SMEM] + [VMEM] * 6,
        out_specs=[VMEM] * (n_head + 2),
        scratch_shapes=[
            pltpu.VMEM((HALF, tall, 4 * LANES), BF16),
            pltpu.VMEM((2, cols * tall, depth), BF16),
            pltpu.VMEM((slots, WIDE, 4 * LANES), BF16),
            pltpu.VMEM((heads, WIDE, WIDE), F32),
            pltpu.VMEM((cols, slots * PAD, 4 * LANES), BF16),
            pltpu.VMEM((cols * tall, 4 * LANES), BF16),
            pltpu.VMEM((n_head, packed, LANES), BF16),
        ],
    )(window_shift, x, g, far, near, weights, turned)
    parts = [pieces[0]]
    for step in range(1, n_head):
        ring = [(i, (i + step) % n_head) for i in range(n_head)]
        parts.append(lax.ppermute(pieces[step], "head", ring))
    every = ("lon", "lat")
    n_every = lax.axis_size("lon") * lax.axis_size("lat")
    shares = sums.reshape(n_every, 4 * width // n_every, depth)
    shares = lax.all_to_all(shares, every, 0, 0)
    full = natural - LANES
    dense = full + full // 2
    rows = pl.pallas_call(
        bias_kernel,
        name="bias_rows",
        out_shape=shape((8 * dense // depth, depth), BF16),
        in_specs=[SMEM, VMEM],
        out_specs=VMEM,
        scratch_shapes=[
            pltpu.VMEM((2 * WIN_LEVEL, number * PAD, LANES), F32),
            pltpu.VMEM((PAD, natural), F32),
            pltpu.VMEM((8, dense), F32),
        ],
    )(bias_type, folded)
    summed, back = pl.pallas_call(
        sum_kernel,
        name="sum_heads",
        out_shape=[shape((cols, tall, width), BF16), shape((HALF, tall, width), BF16)],
        in_specs=[SMEM] + [VMEM] * n_head,
        out_specs=[VMEM] * 2,
    )(window_shift, *parts)
    returned = exchange(back, "lon", window_shift, -1)
    share = pl.pallas_call(
        share_kernel,
        name="share",
        out_shape=shape((rows.shape[0] + shares.shape[1], depth), BF16),
        in_specs=[VMEM] * 2,
        out_specs=VMEM,
    )(shares, rows)
    gathered = lax.all_gather(share, every, axis=0)
    feature_grad, attend_grad, output_grad, bias_grad = pl.pallas_call(
        finish_kernel,
        name="finish",
        out_shape=[
            shape((lats, cols, levels, width), BF16),
            shape((3, width, depth), F32),
            shape((width, depth), F32),
            shape((heads, types, count), F32),
        ],
        in_specs=[SMEM] + [VMEM] * 3,
        out_specs=[VMEM] * 4,
        scratch_shapes=[pltpu.VMEM((8 * n_every, dense), BF16)],
    )(window_shift, gathered, summed, returned)
    return (
        feature_grad.transpose(2, 0, 1, 3),
        attend_grad.transpose(0, 2, 1),
        output_grad,
        bias_grad.transpose(1, 0, 2),
    )


def solution(mesh):
    placed = (
        P(None, "lat", "lon", None),
        P(None, None, "head"),
        P("head", None),
        P(None, "head", None),
        P(None, "lat"),
        P(),
        P(None, "lat", "lon", None),
    )
    return jax.shard_map(
        per_device,
        mesh=mesh,
        in_specs=placed,
        out_specs=(
            P(None, "lat", "lon", "head"),
            P(None, None, "head"),
            P("head", None),
            P(None, "head", None),
        ),
        check_vma=False,
    )
```

time: 104 us -> 80.5 us (0.77)
  local copies, waits for them, and re-layouts: 39.9 us -> 4.06 us
  Pallas kernels: 24 us -> 38.5 us
  waiting for transfers between devices: 0.02 us -> 9.96 us
  blocking collectives: 20 us -> 11.7 us
  other arithmetic: 3.52 us -> 0 us
    pallas_call x5 -> x7, Pallas kernels: 24 us -> 38.5 us  [the longest x1 14.5 us: per_device(): pl.pallas_call(pack_kernel, name='pack', out_shape=shape((2, lats, HALF,...]
    unnamed x18 -> x13, local copies, waits for them, and re-layouts: 16.6 us -> 4.06 us
    all_gather x2 -> x1, blocking collectives: 20 us -> 11.7 us  [per_device(): gathered = lax.all_gather(share, every, axis=0)]
    rev x2 -> x0, local copies, waits for them, and re-layouts: 7.02 us -> none  [the longest x1 3.58 us: natural_rows(): shaped = shaped[:, :, :ROWS, ::-1, :ROWS]]
    ppermute x2, waiting for transfers between devices: 0.01 us -> 5.26 us  [exchange(): lax.ppermute(x, axis, [(i, (i - sign) % count) for i in range(count)])]
    ppermute x3, waiting for transfers between devices: 0.01 us -> 4.7 us  [per_device(): parts.append(lax.ppermute(pieces[step], 'head', ring))]
    reshape x2 -> x0, local copies, waits for them, and re-layouts: 3.85 us -> none  [the longest x1 2.01 us: table_rows(): turned = turned.reshape(slots, heads, ROWS, OFFSETS * PAD)]
    pad x2 -> x0, local copies, waits for them, and re-layouts: 3.63 us -> none  [the longest x1 2.89 us: table_rows(): jnp.pad(turned, ((0, 0),) * 4 + ((0, PAD - ROWS),), constant_values=MASKED)]
  transfers between devices with their start and end apart: 6 -> 6, of which waited for: 0 -> 3; matrix products, arithmetic and copies ran while one was open for 32% -> 2% of each run, Pallas kernels for 4% -> 12%
where the time goes in v1:
time: 80.5 us; the launch traced here: 79.8 us
  Pallas kernels  38.5 us (48%)
  starting transfers between devices  14.2 us (18%)
  blocking collectives  11.7 us (15%)
  waiting for transfers between devices  9.96 us (12%)
  local copies, waits for them, and re-layouts  4.06 us (5%)
  between operations  1.3 us (2%)
    pallas_call x1, Pallas kernels, per_device(): pl.pallas_call(pack_kernel, name='pack', out_shape=shape((2, lats, HALF,...  14.5 us
    all_gather x1, blocking collectives, per_device(): gathered = lax.all_gather(share, every, axis=0)  11.7 us
    pallas_call x1, Pallas kernels, per_device(): pl.pallas_call(main_kernel, name='main', out_shape=[shape((packed, LANES)...  11 us
    ppermute x3, starting transfers between devices, per_device(): parts.append(lax.ppermute(pieces[step], 'head', ring))  5.52 us
    ppermute x2, waiting for transfers between devices, exchange(): lax.ppermute(x, axis, [(i, (i - sign) % count) for i in range(count)])  5.26 us
    ppermute x3, waiting for transfers between devices, per_device(): parts.append(lax.ppermute(pieces[step], 'head', ring))  4.7 us
    ppermute x2, starting transfers between devices, exchange(): lax.ppermute(x, axis, [(i, (i - sign) % count) for i in range(count)])  4.69 us
    unnamed x13, local copies, waits for them, and re-layouts  4.06 us
  transfers between devices with their start and end apart: 6, of which 3 were waited for; matrix products, arithmetic and copies ran while one was open for 2% of the time, Pallas kernels for 12%

profile of v1, /device:TPU:0, one launch (start us, length us, event | category | flops | bytes accessed | tf_op | source)
XLA Modules:
  0.0 79.8 jit_solution(4171156296602025597)
XLA Ops:
  1.3 14.5 %pack.1 = bf16[2,6,6,8,384]{4,3,2,1,0:T(8,128)(2,1)} custom-call(s32[1]{0:T(128)S(6)} %copy.13.shift_ref, bf16[6,12,8,384]{3,2,1,0:T(8,128)(2,1)} %bitcast.9, bf16[6,12,8,384]{3,2,1,0:T(8,128)(2,1)} %bitcast.12), custom_call_target="tpu_custom_call" | custom-call | tf_op jit(solution)/shard_map/pack/pallas_call | solution.py:407
  15.8 3.0 %collective-permute-start = (bf16[2,6,6,8,384]{4,3,2,1,0:T(8,128)(2,1)}, bf16[2,6,6,8,384]{4,3,2,1,0:T(8,128)(2,1)S(1)}, u32[]{:S(2)}, u32[]{:S(2)}) collective-permute-start(bf16[2,6,6,8,384]{4,3,2,1,0:T(8,128)(2,1)} %pack.1), channel_id=1, source_target_pairs={{0,16},{16,0},{1,17},{17,1},{2,18},{18,2},{3,19},{19,3},{4,20},{20... | collective-permute-start | bytes 1327112 | tf_op jit(solution)/shard_map/ppermute | solution.py:383
  18.8 1.3 %copy.11.kind_ref = s32[4,1]{1,0:T(4,128)} copy(s32[4,1]{0,1:T(1,128)} %param.11) | data formatting | bytes 32 | tf_op args[4]
  20.1 3.8 %prepare.1 = (f32[3,64,384]{2,1,0:T(8,128)}, bf16[12,48,512]{2,1,0:T(8,128)(2,1)}, bf16[512,384]{1,0:T(8,128)(2,1)}) custom-call(s32[4,1]{1,0:T(4,128)} %copy.11.kind_ref, bf16[6,12,8,384]{3,2,1,0:T(8,128)(2,1)} %bitcast.10, bf16[6,12,8,384]{3,2,1,0:T(8,128)(2,1)} %bitcast.13, bf16[3,96,384]{2,1,0:T(8,128)(2,1)} %bitcast.18, bf16[96,384]{1,0:T(8,128)(2,1)} %out_weight_ref.1, ...), custom_call_target="tpu_custom_call" | custom-call | tf_op jit(solution)/shard_map/prepare/pallas_call | solution.py:417
  24.0 5.3 %collective-permute-done.far_ref = bf16[2,6,6,8,384]{4,3,2,1,0:T(8,128)(2,1)S(1)} collective-permute-done((bf16[2,6,6,8,384]{4,3,2,1,0:T(8,128)(2,1)}, bf16[2,6,6,8,384]{4,3,2,1,0:T(8,128)(2,1)S(1)}, u32[]{:S(2)}, u32[]{:S(2)}) %collective-permute-start) | collective-permute-done | bytes 442400 | tf_op jit(solution)/shard_map/ppermute | solution.py:383
  29.2 0.0 copy-start.1
  29.2 0.8 copy-done.1
  30.0 11.0 %main.1 = (bf16[432,128]{1,0:T(8,128)(2,1)}, bf16[432,128]{1,0:T(8,128)(2,1)}, bf16[432,128]{1,0:T(8,128)(2,1)}, bf16[432,128]{1,0:T(8,128)(2,1)}, bf16[4,96,384]{2,1,0:T(8,128)(2,1)}, /*index=5*/f32[3,64,384]{2,1,0:T(8,128)}) custom-call(s32[1]{0:T(128)S(6)} %copy.13.shift_ref, bf16[6,12,8,384]{3,2,1,0:T(8,128)(2,1)} %bitcast.11, ...), custom_call_target="tpu_custom_call" | custom-call | tf_op jit(solution)/shard_map/main/pallas_call | solution.py:433
  41.0 4.0 %all-to-all-start = ((bf16[8,48,384]{2,1,0:T(8,128)(2,1)}), bf16[8,48,384]{2,1,0:T(8,128)(2,1)S(1)}, u32[]{:S(2)}, u32[]{:S(2)}) async-start(bf16[8,48,384]{2,1,0:T(8,128)(2,1)} %bitcast.17), calls=%async_computation | async-start | bytes 589824 | tf_op jit(solution)/shard_map/all_to_all | solution.py:460
  44.9 1.6 %collective-permute-start.1 = (bf16[432,128]{1,0:T(8,128)(2,1)}, bf16[432,128]{1,0:T(8,128)(2,1)S(1)}, u32[]{:S(2)}, u32[]{:S(2)}) collective-permute-start(bf16[432,128]{1,0:T(8,128)(2,1)} %get-tuple-element.25), channel_id=1, source_target_pairs={{0,1},{1,2},{2,3},{3,0},{4,5},{5,6},{6,7},{7,4},{8,9},{9,10},{10,1... | collective-permute-start | bytes 331784 | tf_op jit(solution)/shard_map/ppermute | solution.py:456
  46.5 2.6 %collective-permute-start.2 = (bf16[432,128]{1,0:T(8,128)(2,1)}, bf16[432,128]{1,0:T(8,128)(2,1)S(1)}, u32[]{:S(2)}, u32[]{:S(2)}) collective-permute-start(bf16[432,128]{1,0:T(8,128)(2,1)} %get-tuple-element.26), channel_id=1, source_target_pairs={{0,2},{1,3},{2,0},{3,1},{4,6},{5,7},{6,4},{7,5},{8,10},{9,11},{10,... | collective-permute-start | bytes 331784 | tf_op jit(solution)/shard_map/ppermute | solution.py:456
  49.1 1.3 %collective-permute-start.3 = (bf16[432,128]{1,0:T(8,128)(2,1)}, bf16[432,128]{1,0:T(8,128)(2,1)S(1)}, u32[]{:S(2)}, u32[]{:S(2)}) collective-permute-start(bf16[432,128]{1,0:T(8,128)(2,1)} %get-tuple-element.27), channel_id=1, source_target_pairs={{0,3},{1,0},{2,1},{3,2},{4,7},{5,4},{6,5},{7,6},{8,11},{9,8},{10,9... | collective-permute-start | bytes 331784 | tf_op jit(solution)/shard_map/ppermute | solution.py:456
  50.4 2.1 %bias_rows.1.rows_ref = bf16[104,384]{1,0:T(8,128)(2,1)} custom-call(s32[4,1]{1,0:T(4,128)} %copy.11.kind_ref, f32[3,64,384]{2,1,0:T(8,128)} %get-tuple-element.23.folded_ref), custom_call_target="tpu_custom_call" | custom-call | tf_op jit(solution)/shard_map/bias_rows/pallas_call | solution.py:463
  52.6 0.4 collective-permute-done.1.refs_1_
  53.0 0.0 copy-start.2
  53.0 4.3 %collective-permute-done.2.refs_2_ = bf16[432,128]{1,0:T(8,128)(2,1)S(1)} collective-permute-done((bf16[432,128]{1,0:T(8,128)(2,1)}, bf16[432,128]{1,0:T(8,128)(2,1)S(1)}, u32[]{:S(2)}, u32[]{:S(2)}) %collective-permute-start.2) | collective-permute-done | bytes 110624 | tf_op jit(solution)/shard_map/ppermute | solution.py:456
  57.3 0.0 copy-start.3
  57.3 0.0 collective-permute-done.3.refs_3_
  57.3 0.0 copy-start.4
  57.3 0.0 copy-done.2
  57.3 0.6 copy-done.3
  57.9 0.0 copy-done.4
  58.0 1.9 %sum_heads.1 = (bf16[12,48,96]{2,1,0:T(8,128)(2,1)}, bf16[6,48,96]{2,1,0:T(8,128)(2,1)}) custom-call(s32[1]{0:T(128)S(6)} %copy.13.shift_ref, bf16[432,128]{1,0:T(8,128)(2,1)} %get-tuple-element.24.refs_0_, bf16[432,128]{1,0:T(8,128)(2,1)} %copy-done.2, bf16[432,128]{1,0:T(8,128)(2,1)} %copy-done.3, bf16[432,128]{1,0:T(8,128)(2,1)} %copy-done.4), custom_call_target="tpu_custom_call" | custom-call | tf_op jit(solution)/shard_map/sum_heads/pallas_call | solution.py:475
  59.8 1.7 %collective-permute-start.4 = (bf16[6,48,96]{2,1,0:T(8,128)(2,1)}, bf16[6,48,96]{2,1,0:T(8,128)(2,1)S(1)}, u32[]{:S(2)}, u32[]{:S(2)}) collective-permute-start(bf16[6,48,96]{2,1,0:T(8,128)(2,1)} %get-tuple-element.29), channel_id=1, source_target_pairs={{0,16},{16,0},{1,17},{17,1},{2,18},{18,2},{3,19},{19,3},{4,20},{20... | collective-permute-start | bytes 165896 | tf_op jit(solution)/shard_map/ppermute | solution.py:383
  61.5 0.0 all-to-all-done.shares_ref
  61.5 0.0 copy-start
  61.5 0.7 copy-done
  62.2 1.7 %share.1 = bf16[152,384]{1,0:T(8,128)(2,1)} custom-call(bf16[8,48,384]{2,1,0:T(8,128)(2,1)} %copy-done, bf16[104,384]{1,0:T(8,128)(2,1)} %bias_rows.1.rows_ref), custom_call_target="tpu_custom_call" | custom-call | tf_op jit(solution)/shard_map/share/pallas_call | solution.py:483
  63.9 11.7 %all-gather = bf16[1216,384]{1,0:T(8,128)(2,1)} all-gather(bf16[152,384]{1,0:T(8,128)(2,1)} %share.1), channel_id=2, replica_groups=mesh['lon'=2,'lat'=4,'head'=4] {'lon','lat'}, dimensions={0}, use_global_device_ids=true | all-gather | bytes 1050624 | tf_op jit(solution)/shard_map/all_gather | solution.py:490
  75.6 0.0 collective-permute-done.4.returned_ref
  75.6 0.6 copy-done.5
  76.3 3.5 %finish.1 = (bf16[6,12,8,96]{3,2,1,0:T(8,128)(2,1)}, f32[3,96,384]{2,1,0:T(8,128)}, f32[96,384]{1,0:T(8,128)}, f32[3,64,3312]{2,1,0:T(8,128)}) custom-call(s32[1]{0:T(128)S(6)} %copy.13.shift_ref, bf16[8,152,384]{2,1,0:T(8,128)(2,1)} %bitcast.15, bf16[12,48,96]{2,1,0:T(8,128)(2,1)} %get-tuple-element.28.summed_ref, bf16[6,48,96]{2,1,0:T(8,128)(2,1)} %copy-done.5), custom_call_target="tpu_custom_call" | custom-call | tf_op jit(solution)/shard_map/finish/pallas_call | solution.py:491
  (1 shorter events, 0.0 us)
Async XLA Ops:
  15.8 13.4 %collective-permute-start = (bf16[2,6,6,8,384]{4,3,2,1,0:T(8,128)(2,1)}, bf16[2,6,6,8,384]{4,3,2,1,0:T(8,128)(2,1)S(1)}, u32[]{:S(2)}, u32[]{:S(2)}) collective-permute-start(bf16[2,6,6,8,384]{4,3,2,1,0:T(8,128)(2,1)} %pack.1), channel_id=1, source_target_pairs={{0,16},{16,0},{1,17},{17,1},{2,18},{18,2},{3,19},{19,3},{4,20},{20... | collective-permute-start | bytes 1327112 | tf_op jit(solution)/shard_map/ppermute | solution.py:383
  29.2 0.8 copy-start.1
  41.0 20.5 %all-to-all-start = ((bf16[8,48,384]{2,1,0:T(8,128)(2,1)}), bf16[8,48,384]{2,1,0:T(8,128)(2,1)S(1)}, u32[]{:S(2)}, u32[]{:S(2)}) async-start(bf16[8,48,384]{2,1,0:T(8,128)(2,1)} %bitcast.17), calls=%async_computation | async-start | bytes 589824 | tf_op jit(solution)/shard_map/all_to_all | solution.py:460
  44.9 8.0 %collective-permute-start.1 = (bf16[432,128]{1,0:T(8,128)(2,1)}, bf16[432,128]{1,0:T(8,128)(2,1)S(1)}, u32[]{:S(2)}, u32[]{:S(2)}) collective-permute-start(bf16[432,128]{1,0:T(8,128)(2,1)} %get-tuple-element.25), channel_id=1, source_target_pairs={{0,1},{1,2},{2,3},{3,0},{4,5},{5,6},{6,7},{7,4},{8,9},{9,10},{10,1... | collective-permute-start | bytes 331784 | tf_op jit(solution)/shard_map/ppermute | solution.py:456
  46.5 10.8 %collective-permute-start.2 = (bf16[432,128]{1,0:T(8,128)(2,1)}, bf16[432,128]{1,0:T(8,128)(2,1)S(1)}, u32[]{:S(2)}, u32[]{:S(2)}) collective-permute-start(bf16[432,128]{1,0:T(8,128)(2,1)} %get-tuple-element.26), channel_id=1, source_target_pairs={{0,2},{1,3},{2,0},{3,1},{4,6},{5,7},{6,4},{7,5},{8,10},{9,11},{10,... | collective-permute-start | bytes 331784 | tf_op jit(solution)/shard_map/ppermute | solution.py:456
  49.1 8.2 %collective-permute-start.3 = (bf16[432,128]{1,0:T(8,128)(2,1)}, bf16[432,128]{1,0:T(8,128)(2,1)S(1)}, u32[]{:S(2)}, u32[]{:S(2)}) collective-permute-start(bf16[432,128]{1,0:T(8,128)(2,1)} %get-tuple-element.27), channel_id=1, source_target_pairs={{0,3},{1,0},{2,1},{3,2},{4,7},{5,4},{6,5},{7,6},{8,11},{9,8},{10,9... | collective-permute-start | bytes 331784 | tf_op jit(solution)/shard_map/ppermute | solution.py:456
  53.0 4.3 %copy-start.2 = (bf16[432,128]{1,0:T(8,128)(2,1)}, bf16[432,128]{1,0:T(8,128)(2,1)S(1)}, u32[]{:S(2)}) copy-start(bf16[432,128]{1,0:T(8,128)(2,1)S(1)} %collective-permute-done.1.refs_1_) | copy-start | bytes 331780
  57.3 0.6 copy-start.3
  57.3 0.7 copy-start.4
  59.8 15.8 %collective-permute-start.4 = (bf16[6,48,96]{2,1,0:T(8,128)(2,1)}, bf16[6,48,96]{2,1,0:T(8,128)(2,1)S(1)}, u32[]{:S(2)}, u32[]{:S(2)}) collective-permute-start(bf16[6,48,96]{2,1,0:T(8,128)(2,1)} %get-tuple-element.29), channel_id=1, source_target_pairs={{0,16},{16,0},{1,17},{17,1},{2,18},{18,2},{3,19},{19,3},{4,20},{20... | collective-permute-start | bytes 165896 | tf_op jit(solution)/shard_map/ppermute | solution.py:383
  61.5 0.7 copy-start
  75.6 0.6 copy-start.5

commit v2 on v1

--- a/solution.py
+++ b/solution.py
@@ -21,7 +21,7 @@
 BF16 = jnp.bfloat16
 SMEM = pl.BlockSpec(memory_space=pltpu.SMEM)
 VMEM = pl.BlockSpec(memory_space=pltpu.VMEM)
-ANY = pl.BlockSpec(memory_space=pl.ANY)
+HBM = pl.BlockSpec(memory_space=pltpu.HBM)
 
 
 def dot_nn(a, b):
@@ -378,6 +378,10 @@
     ]
 
 
+def small(mebibytes):
+    return pltpu.CompilerParams(vmem_limit_bytes=mebibytes << 20)
+
+
 def exchange(x, axis, shift, sign):
     count = lax.axis_size(axis)
     ahead = lax.ppermute(x, axis, [(i, (i - sign) % count) for i in range(count)])
@@ -408,9 +412,10 @@
         pack_kernel,
         name="pack",
         out_shape=shape((2, lats, HALF, levels, depth), BF16),
-        in_specs=[SMEM, ANY, ANY],
-        out_specs=ANY,
+        in_specs=[SMEM, HBM, HBM],
+        out_specs=VMEM,
         scratch_shapes=[pltpu.SemaphoreType.DMA((2,))],
+        compiler_params=small(4),
     )(window_shift, x, g)
     far = exchange(slab, "lon", window_shift, 1)
     natural = -(-count // LANES) * LANES + LANES
@@ -428,6 +433,7 @@
             pltpu.VMEM((PAD, natural), F32),
             pltpu.VMEM((2 * WIN_LEVEL, number * PAD, LANES), F32),
         ],
+        compiler_params=small(16),
     )(bias_type, x, g, weight, output_weight, table)
     packed = 3 * (cols // 4) * tall
     *pieces, sums, folded = pl.pallas_call(
@@ -449,6 +455,7 @@
             pltpu.VMEM((cols * tall, 4 * LANES), BF16),
             pltpu.VMEM((n_head, packed, LANES), BF16),
         ],
+        compiler_params=small(24),
     )(window_shift, x, g, far, near, weights, turned)
     parts = [pieces[0]]
     for step in range(1, n_head):
@@ -471,6 +478,7 @@
             pltpu.VMEM((PAD, natural), F32),
             pltpu.VMEM((8, dense), F32),
         ],
+        compiler_params=small(8),
     )(bias_type, folded)
     summed, back = pl.pallas_call(
         sum_kernel,
@@ -478,6 +486,7 @@
         out_shape=[shape((cols, tall, width), BF16), shape((HALF, tall, width), BF16)],
         in_specs=[SMEM] + [VMEM] * n_head,
         out_specs=[VMEM] * 2,
+        compiler_params=small(6),
     )(window_shift, *parts)
     returned = exchange(back, "lon", window_shift, -1)
     share = pl.pallas_call(
@@ -486,6 +495,7 @@
         out_shape=shape((rows.shape[0] + shares.shape[1], depth), BF16),
         in_specs=[VMEM] * 2,
         out_specs=VMEM,
+        compiler_params=small(4),
     )(shares, rows)
     gathered = lax.all_gather(share, every, axis=0)
     feature_grad, attend_grad, output_grad, bias_grad = pl.pallas_call(
@@ -500,6 +510,7 @@
         in_specs=[SMEM] + [VMEM] * 3,
         out_specs=[VMEM] * 4,
         scratch_shapes=[pltpu.VMEM((8 * n_every, dense), BF16)],
+        compiler_params=small(16),
     )(window_shift, gathered, summed, returned)
     return (
         feature_grad.transpose(2, 0, 1, 3),

time: 80.5 us -> 57.5 us (0.71)
  Pallas kernels: 38.5 us -> 14.2 us
  local copies, waits for them, and re-layouts: 4.06 us -> 8.33 us
  waiting for transfers between devices: 9.96 us -> 7.84 us
  blocking collectives: 11.7 us -> 10.7 us
    pallas_call x1, Pallas kernels: 14.5 us -> 0.11 us  [per_device(): pl.pallas_call(pack_kernel, name='pack', out_shape=shape((2, lats, HALF,...]
    unnamed x13 -> x19, local copies, waits for them, and re-layouts: 4.06 us -> 8.33 us
    ppermute x2, waiting for transfers between devices: 5.26 us -> 2.31 us  [exchange(): lax.ppermute(x, axis, [(i, (i - sign) % count) for i in range(count)])]
    pallas_call x1, Pallas kernels: 3.84 us -> 1.54 us  [per_device(): pl.pallas_call(prepare_kernel, name='prepare', out_shape=[shape((heads, s...]
    pallas_call x1, Pallas kernels: 11 us -> 9.05 us  [per_device(): pl.pallas_call(main_kernel, name='main', out_shape=[shape((packed, LANES)...]
    pallas_call x1, Pallas kernels: 1.88 us -> 0.15 us  [per_device(): pl.pallas_call(sum_kernel, name='sum_heads', out_shape=[shape((cols, tall...]
    pallas_call x1, Pallas kernels: 1.67 us -> 0.05 us  [per_device(): pl.pallas_call(share_kernel, name='share', out_shape=shape((rows.shape[0]...]
    pallas_call x1, Pallas kernels: 3.53 us -> 2.26 us  [per_device(): pl.pallas_call(finish_kernel, name='finish', out_shape=[shape((lats, cols...]
  transfers between devices with their start and end apart: 6 -> 6, of which waited for: 3 -> 3; matrix products, arithmetic and copies ran while one was open for 2% -> 1% of each run, Pallas kernels for 12% -> 5%
where the time goes in v2:
time: 57.5 us; the launch traced here: 56.7 us
  starting transfers between devices  14.3 us (25%)
  Pallas kernels  14.2 us (25%)
  blocking collectives  10.7 us (19%)
  local copies, waits for them, and re-layouts  8.33 us (14%)
  waiting for transfers between devices  7.84 us (14%)
  between operations  1.33 us (2%)
    all_gather x1, blocking collectives, per_device(): gathered = lax.all_gather(share, every, axis=0)  10.7 us
    pallas_call x1, Pallas kernels, per_device(): pl.pallas_call(main_kernel, name='main', out_shape=[shape((packed, LANES)...  9.05 us
    unnamed x19, local copies, waits for them, and re-layouts  8.33 us
    ppermute x3, waiting for transfers between devices, per_device(): parts.append(lax.ppermute(pieces[step], 'head', ring))  5.53 us
    ppermute x3, starting transfers between devices, per_device(): parts.append(lax.ppermute(pieces[step], 'head', ring))  5.52 us
    ppermute x2, starting transfers between devices, exchange(): lax.ppermute(x, axis, [(i, (i - sign) % count) for i in range(count)])  4.76 us
    all_to_all x1, starting transfers between devices, per_device(): shares = lax.all_to_all(shares, every, 0, 0)  3.97 us
    ppermute x2, waiting for transfers between devices, exchange(): lax.ppermute(x, axis, [(i, (i - sign) % count) for i in range(count)])  2.31 us
  transfers between devices with their start and end apart: 6, of which 3 were waited for; matrix products, arithmetic and copies ran while one was open for 1% of the time, Pallas kernels for 5%

profile of v2, /device:TPU:0, one launch (start us, length us, event | category | flops | bytes accessed | tf_op | source)
XLA Modules:
  0.0 56.7 jit_solution(4808010342639480376)
XLA Ops:
  1.3 0.0 copy-start
  1.3 1.0 %copy-done = bf16[8,6,12,384]{3,0,2,1:T(8,128)(2,1)S(1)} copy-done((bf16[8,6,12,384]{3,0,2,1:T(8,128)(2,1)S(1)}, bf16[8,6,12,384]{3,0,2,1:T(8,128)(2,1)}, u32[]{:S(2)}) %copy-start) | copy-done | bytes 442392
  2.3 0.0 copy-start.3
  2.3 1.0 %copy-done.3 = bf16[8,6,12,384]{3,0,2,1:T(8,128)(2,1)S(1)} copy-done((bf16[8,6,12,384]{3,0,2,1:T(8,128)(2,1)S(1)}, bf16[8,6,12,384]{3,0,2,1:T(8,128)(2,1)}, u32[]{:S(2)}) %copy-start.3) | copy-done | bytes 442392
  3.3 0.1 pack.1
  3.4 3.0 %collective-permute-start = (bf16[2,6,6,8,384]{4,3,2,1,0:T(8,128)(2,1)S(1)}, bf16[2,6,6,8,384]{4,3,2,1,0:T(8,128)(2,1)S(1)}, u32[]{:S(2)}, u32[]{:S(2)}) collective-permute-start(bf16[2,6,6,8,384]{4,3,2,1,0:T(8,128)(2,1)S(1)} %pack.1), channel_id=1, source_target_pairs={{0,16},{16,0},{1,17},{17,1},{2,18},{18,2},{3,19},{19,3},{4,20},{20... | collective-permute-start | bytes 1327112 | tf_op jit(solution)/shard_map/ppermute | solution.py:387
  6.5 0.7 %copy.11.kind_ref = s32[4,1]{1,0:T(4,128)S(1)} copy(s32[4,1]{0,1:T(1,128)} %param.11) | data formatting | bytes 32 | tf_op args[4]
  7.2 1.0 %copy-done.1 = bf16[8,6,12,384]{3,0,2,1:T(8,128)(2,1)S(1)} copy-done((bf16[8,6,12,384]{3,0,2,1:T(8,128)(2,1)S(1)}, bf16[8,6,12,384]{3,0,2,1:T(8,128)(2,1)}, u32[]{:S(2)}) %copy-start.1) | copy-done | bytes 442392
  8.2 1.0 %copy-done.4 = bf16[8,6,12,384]{3,0,2,1:T(8,128)(2,1)S(1)} copy-done((bf16[8,6,12,384]{3,0,2,1:T(8,128)(2,1)S(1)}, bf16[8,6,12,384]{3,0,2,1:T(8,128)(2,1)}, u32[]{:S(2)}) %copy-start.4) | copy-done | bytes 442392
  9.2 1.7 %copy-done.6 = f32[64,3,3312]{2,0,1:T(8,128)S(1)} copy-done((f32[64,3,3312]{2,0,1:T(8,128)S(1)}, f32[64,3,3312]{2,0,1:T(8,128)}, u32[]{:S(2)}) %copy-start.6) | copy-done | bytes 2543640
  11.0 0.9 %copy-done.7 = bf16[3,384,96]{1,2,0:T(8,128)(2,1)S(1)} copy-done((bf16[3,384,96]{1,2,0:T(8,128)(2,1)S(1)}, bf16[3,384,96]{1,2,0:T(8,128)(2,1)}, u32[]{:S(2)}) %copy-start.7) | copy-done | bytes 221208
  11.9 0.9 %copy-done.8 = bf16[96,384]{1,0:T(8,128)(2,1)S(1)} copy-done((bf16[96,384]{1,0:T(8,128)(2,1)S(1)}, bf16[96,384]{1,0:T(8,128)(2,1)}, u32[]{:S(2)}) %copy-start.8) | copy-done | bytes 73752
  12.8 1.5 %prepare.1 = (f32[3,64,384]{2,1,0:T(8,128)S(1)}, bf16[12,48,512]{2,1,0:T(8,128)(2,1)S(1)}, bf16[512,384]{1,0:T(8,128)(2,1)S(1)}) custom-call(s32[4,1]{1,0:T(4,128)S(1)} %copy.11.kind_ref, bf16[6,12,8,384]{3,2,1,0:T(8,128)(2,1)S(1)} %bitcast.10, bf16[6,12,8,384]{3,2,1,0:T(8,128)(2,1)S(1)} %bitcast.13, bf16[3,96,384]{2,1,0:T(8,128)(2,1)S(1)} %bitcast.17, ...), custom_call_target="tpu_custom_call" | custom-call | tf_op jit(solution)/shard_map/prepare/pallas_call | solution.py:422
  14.3 2.3 %collective-permute-done.far_ref = bf16[2,6,6,8,384]{4,3,2,1,0:T(8,128)(2,1)S(1)} collective-permute-done((bf16[2,6,6,8,384]{4,3,2,1,0:T(8,128)(2,1)S(1)}, bf16[2,6,6,8,384]{4,3,2,1,0:T(8,128)(2,1)S(1)}, u32[]{:S(2)}, u32[]{:S(2)}) %collective-permute-start) | collective-permute-done | bytes 442400 | tf_op jit(solution)/shard_map/ppermute | solution.py:387
  16.6 0.0 copy-done.2
  16.6 0.0 copy-done.5
  16.6 9.0 %main.1 = (bf16[432,128]{1,0:T(8,128)(2,1)S(1)}, bf16[432,128]{1,0:T(8,128)(2,1)S(1)}, bf16[432,128]{1,0:T(8,128)(2,1)S(1)}, bf16[432,128]{1,0:T(8,128)(2,1)S(1)...) custom-call(s32[1]{0:T(128)S(6)} %copy.13.shift_ref, bf16[6,12,8,384]{3,2,1,0:T(8,128)(2,1)S(1)} %bitcast.11, ...), custom_call_target="tpu_custom_call" | custom-call | tf_op jit(solution)/shard_map/main/pallas_call | solution.py:439
  25.7 4.0 %all-to-all-start = ((bf16[8,48,384]{2,1,0:T(8,128)(2,1)}), bf16[8,48,384]{2,1,0:T(8,128)(2,1)S(1)}, u32[]{:S(2)}, u32[]{:S(2)}) async-start(bf16[8,48,384]{2,1,0:T(8,128)(2,1)} %bitcast.4), calls=%async_computation | async-start | bytes 589824 | tf_op jit(solution)/shard_map/all_to_all | solution.py:467
  29.7 1.6 %collective-permute-start.1 = (bf16[432,128]{1,0:T(8,128)(2,1)S(1)}, bf16[432,128]{1,0:T(8,128)(2,1)S(1)}, u32[]{:S(2)}, u32[]{:S(2)}) collective-permute-start(bf16[432,128]{1,0:T(8,128)(2,1)S(1)} %get-tuple-element.25), channel_id=1, source_target_pairs={{0,1},{1,2},{2,3},{3,0},{4,5},{5,6},{6,7},{7,4},{8,9},{9,10},{10,1... | collective-permute-start | bytes 331784 | tf_op jit(solution)/shard_map/ppermute | solution.py:463
  31.2 2.6 %collective-permute-start.2 = (bf16[432,128]{1,0:T(8,128)(2,1)S(1)}, bf16[432,128]{1,0:T(8,128)(2,1)S(1)}, u32[]{:S(2)}, u32[]{:S(2)}) collective-permute-start(bf16[432,128]{1,0:T(8,128)(2,1)S(1)} %get-tuple-element.26), channel_id=1, source_target_pairs={{0,2},{1,3},{2,0},{3,1},{4,6},{5,7},{6,4},{7,5},{8,10},{9,11},{10,... | collective-permute-start | bytes 331784 | tf_op jit(solution)/shard_map/ppermute | solution.py:463
  33.8 1.4 %collective-permute-start.3 = (bf16[432,128]{1,0:T(8,128)(2,1)S(1)}, bf16[432,128]{1,0:T(8,128)(2,1)S(1)}, u32[]{:S(2)}, u32[]{:S(2)}) collective-permute-start(bf16[432,128]{1,0:T(8,128)(2,1)S(1)} %get-tuple-element.27), channel_id=1, source_target_pairs={{0,3},{1,0},{2,1},{3,2},{4,7},{5,4},{6,5},{7,6},{8,11},{9,8},{10,9... | collective-permute-start | bytes 331784 | tf_op jit(solution)/shard_map/ppermute | solution.py:463
  35.2 1.1 %bias_rows.1.rows_ref = bf16[104,384]{1,0:T(8,128)(2,1)S(1)} custom-call(s32[4,1]{1,0:T(4,128)S(1)} %copy.11.kind_ref, f32[3,64,384]{2,1,0:T(8,128)S(1)} %get-tuple-element.23.folded_ref), custom_call_target="tpu_custom_call" | custom-call | tf_op jit(solution)/shard_map/bias_rows/pallas_call | solution.py:470
  36.3 1.2 %collective-permute-done.1.refs_1_ = bf16[432,128]{1,0:T(8,128)(2,1)S(1)} collective-permute-done((bf16[432,128]{1,0:T(8,128)(2,1)S(1)}, bf16[432,128]{1,0:T(8,128)(2,1)S(1)}, u32[]{:S(2)}, u32[]{:S(2)}) %collective-permute-start.1) | collective-permute-done | bytes 110624 | tf_op jit(solution)/shard_map/ppermute | solution.py:463
  37.5 4.3 %collective-permute-done.2.refs_2_ = bf16[432,128]{1,0:T(8,128)(2,1)S(1)} collective-permute-done((bf16[432,128]{1,0:T(8,128)(2,1)S(1)}, bf16[432,128]{1,0:T(8,128)(2,1)S(1)}, u32[]{:S(2)}, u32[]{:S(2)}) %collective-permute-start.2) | collective-permute-done | bytes 110624 | tf_op jit(solution)/shard_map/ppermute | solution.py:463
  41.8 0.0 collective-permute-done.3.refs_3_
  41.8 0.1 sum_heads.1
  41.9 1.7 %collective-permute-start.4 = (bf16[6,48,96]{2,1,0:T(8,128)(2,1)S(1)}, bf16[6,48,96]{2,1,0:T(8,128)(2,1)S(1)}, u32[]{:S(2)}, u32[]{:S(2)}) collective-permute-start(bf16[6,48,96]{2,1,0:T(8,128)(2,1)S(1)} %get-tuple-element.29), channel_id=1, source_target_pairs={{0,16},{16,0},{1,17},{17,1},{2,18},{18,2},{3,19},{19,3},{4,20},{20... | collective-permute-start | bytes 165896 | tf_op jit(solution)/shard_map/ppermute | solution.py:387
  43.7 0.0 all-to-all-done.shares_ref
  43.7 0.1 share.1
  43.7 10.7 %all-gather = bf16[1216,384]{1,0:T(8,128)(2,1)S(1)} all-gather(bf16[152,384]{1,0:T(8,128)(2,1)S(1)} %share.1), channel_id=2, replica_groups=mesh['lon'=2,'lat'=4,'head'=4] {'lon','lat'}, dimensions={0}, use_global_device_ids=true | all-gather | bytes 1050624 | tf_op jit(solution)/shard_map/all_gather | solution.py:500
  54.4 0.0 collective-permute-done.4.returned_ref
  54.4 2.3 %finish.1 = (bf16[6,12,8,96]{3,2,1,0:T(8,128)(2,1)}, f32[3,96,384]{2,1,0:T(8,128)}, f32[96,384]{1,0:T(8,128)}, f32[3,64,3312]{2,1,0:T(8,128)}) custom-call(s32[1]{0:T(128)S(6)} %copy.13.shift_ref, bf16[8,152,384]{2,1,0:T(8,128)(2,1)S(1)} %bitcast.15, bf16[12,48,96]{2,1,0:T(8,128)(2,1)S(1)} %get-tuple-element.28.summed_ref, ...), custom_call_target="tpu_custom_call" | custom-call | tf_op jit(solution)/shard_map/finish/pallas_call | solution.py:501
  (7 shorter events, 0.0 us)
Async XLA Ops:
  1.3 1.0 %copy-start = (bf16[8,6,12,384]{3,0,2,1:T(8,128)(2,1)S(1)}, bf16[8,6,12,384]{3,0,2,1:T(8,128)(2,1)}, u32[]{:S(2)}) copy-start(bf16[8,6,12,384]{3,0,2,1:T(8,128)(2,1)} %param.7) | copy-start | bytes 1327108
  2.3 1.0 %copy-start.3 = (bf16[8,6,12,384]{3,0,2,1:T(8,128)(2,1)S(1)}, bf16[8,6,12,384]{3,0,2,1:T(8,128)(2,1)}, u32[]{:S(2)}) copy-start(bf16[8,6,12,384]{3,0,2,1:T(8,128)(2,1)} %param.13) | copy-start | bytes 1327108
  3.3 13.3 %copy-start.2 = (bf16[8,6,12,384]{3,0,2,1:T(8,128)(2,1)S(1)}, bf16[8,6,12,384]{3,0,2,1:T(8,128)(2,1)}, u32[]{:S(2)}) copy-start(bf16[8,6,12,384]{3,0,2,1:T(8,128)(2,1)} %param.7) | copy-start | bytes 1327108
  3.3 13.3 %copy-start.5 = (bf16[8,6,12,384]{3,0,2,1:T(8,128)(2,1)S(1)}, bf16[8,6,12,384]{3,0,2,1:T(8,128)(2,1)}, u32[]{:S(2)}) copy-start(bf16[8,6,12,384]{3,0,2,1:T(8,128)(2,1)} %param.13) | copy-start | bytes 1327108
  3.4 13.2 %collective-permute-start = (bf16[2,6,6,8,384]{4,3,2,1,0:T(8,128)(2,1)S(1)}, bf16[2,6,6,8,384]{4,3,2,1,0:T(8,128)(2,1)S(1)}, u32[]{:S(2)}, u32[]{:S(2)}) collective-permute-start(bf16[2,6,6,8,384]{4,3,2,1,0:T(8,128)(2,1)S(1)} %pack.1), channel_id=1, source_target_pairs={{0,16},{16,0},{1,17},{17,1},{2,18},{18,2},{3,19},{19,3},{4,20},{20... | collective-permute-start | bytes 1327112 | tf_op jit(solution)/shard_map/ppermute | solution.py:387
  7.2 1.0 %copy-start.1 = (bf16[8,6,12,384]{3,0,2,1:T(8,128)(2,1)S(1)}, bf16[8,6,12,384]{3,0,2,1:T(8,128)(2,1)}, u32[]{:S(2)}) copy-start(bf16[8,6,12,384]{3,0,2,1:T(8,128)(2,1)} %param.7) | copy-start | bytes 1327108
  8.2 1.0 %copy-start.4 = (bf16[8,6,12,384]{3,0,2,1:T(8,128)(2,1)S(1)}, bf16[8,6,12,384]{3,0,2,1:T(8,128)(2,1)}, u32[]{:S(2)}) copy-start(bf16[8,6,12,384]{3,0,2,1:T(8,128)(2,1)} %param.13) | copy-start | bytes 1327108
  9.2 1.7 %copy-start.6 = (f32[64,3,3312]{2,0,1:T(8,128)S(1)}, f32[64,3,3312]{2,0,1:T(8,128)}, u32[]{:S(2)}) copy-start(f32[64,3,3312]{2,0,1:T(8,128)} %param.10) | copy-start | bytes 7630852
  11.0 0.9 %copy-start.7 = (bf16[3,384,96]{1,2,0:T(8,128)(2,1)S(1)}, bf16[3,384,96]{1,2,0:T(8,128)(2,1)}, u32[]{:S(2)}) copy-start(bf16[3,384,96]{1,2,0:T(8,128)(2,1)} %param.8) | copy-start | bytes 663556
  11.9 0.9 %copy-start.8 = (bf16[96,384]{1,0:T(8,128)(2,1)S(1)}, bf16[96,384]{1,0:T(8,128)(2,1)}, u32[]{:S(2)}) copy-start(bf16[96,384]{1,0:T(8,128)(2,1)} %out_weight_ref.1) | copy-start | bytes 221188
  25.7 18.0 %all-to-all-start = ((bf16[8,48,384]{2,1,0:T(8,128)(2,1)}), bf16[8,48,384]{2,1,0:T(8,128)(2,1)S(1)}, u32[]{:S(2)}, u32[]{:S(2)}) async-start(bf16[8,48,384]{2,1,0:T(8,128)(2,1)} %bitcast.4), calls=%async_computation | async-start | bytes 589824 | tf_op jit(solution)/shard_map/all_to_all | solution.py:467
  29.7 7.8 %collective-permute-start.1 = (bf16[432,128]{1,0:T(8,128)(2,1)S(1)}, bf16[432,128]{1,0:T(8,128)(2,1)S(1)}, u32[]{:S(2)}, u32[]{:S(2)}) collective-permute-start(bf16[432,128]{1,0:T(8,128)(2,1)S(1)} %get-tuple-element.25), channel_id=1, source_target_pairs={{0,1},{1,2},{2,3},{3,0},{4,5},{5,6},{6,7},{7,4},{8,9},{9,10},{10,1... | collective-permute-start | bytes 331784 | tf_op jit(solution)/shard_map/ppermute | solution.py:463
  31.2 10.6 %collective-permute-start.2 = (bf16[432,128]{1,0:T(8,128)(2,1)S(1)}, bf16[432,128]{1,0:T(8,128)(2,1)S(1)}, u32[]{:S(2)}, u32[]{:S(2)}) collective-permute-start(bf16[432,128]{1,0:T(8,128)(2,1)S(1)} %get-tuple-element.26), channel_id=1, source_target_pairs={{0,2},{1,3},{2,0},{3,1},{4,6},{5,7},{6,4},{7,5},{8,10},{9,11},{10,... | collective-permute-start | bytes 331784 | tf_op jit(solution)/shard_map/ppermute | solution.py:463
  33.8 8.0 %collective-permute-start.3 = (bf16[432,128]{1,0:T(8,128)(2,1)S(1)}, bf16[432,128]{1,0:T(8,128)(2,1)S(1)}, u32[]{:S(2)}, u32[]{:S(2)}) collective-permute-start(bf16[432,128]{1,0:T(8,128)(2,1)S(1)} %get-tuple-element.27), channel_id=1, source_target_pairs={{0,3},{1,0},{2,1},{3,2},{4,7},{5,4},{6,5},{7,6},{8,11},{9,8},{10,9... | collective-permute-start | bytes 331784 | tf_op jit(solution)/shard_map/ppermute | solution.py:463
  41.9 12.5 %collective-permute-start.4 = (bf16[6,48,96]{2,1,0:T(8,128)(2,1)S(1)}, bf16[6,48,96]{2,1,0:T(8,128)(2,1)S(1)}, u32[]{:S(2)}, u32[]{:S(2)}) collective-permute-start(bf16[6,48,96]{2,1,0:T(8,128)(2,1)S(1)} %get-tuple-element.29), channel_id=1, source_target_pairs={{0,16},{16,0},{1,17},{17,1},{2,18},{18,2},{3,19},{19,3},{4,20},{20... | collective-permute-start | bytes 165896 | tf_op jit(solution)/shard_map/ppermute | solution.py:387

commit v3 on v2

--- a/solution.py
+++ b/solution.py
@@ -70,53 +70,70 @@
                 yield level_i * WIN_LAT + lat_i, level_j, index * PIECE
 
 
-def pack_kernel(shift_ref, x_ref, g_ref, out_ref, sems):
-    base = jnp.where(shift_ref[0] <= HALF, 0, WIN_LON - HALF)
-    copies = [
-        pltpu.make_async_copy(ref.at[:, pl.ds(base, HALF)], out_ref.at[i], sems.at[i])
-        for i, ref in enumerate((x_ref, g_ref))
-    ]
+def run_all(copies):
     for copy in copies:
         copy.start()
     for copy in copies:
         copy.wait()
 
 
-def project(rows_x, rows_g, weights):
-    width = 3 * LANES
-    return jnp.concatenate(
-        [dot_nt(rows_x, weights[:width]), dot_nt(rows_g, weights[width:])], axis=1
-    )
+def start_kernel(
+    shift_ref, x_ref, g_ref, weight_ref, out_weight_ref, raw_ref, projected_ref, rows_ref, sems
+):
+    base = jnp.where(shift_ref[0] <= HALF, 0, WIN_LON - HALF)
+    lats, _, levels, depth = x_ref.shape
+    width = out_weight_ref.shape[0]
+    moves = [(ref.at[:, pl.ds(base, HALF)], raw_ref.at[i]) for i, ref in enumerate((x_ref, g_ref))]
+    moves += [(weight_ref.at[c], rows_ref.at[pl.ds(c * width, width)]) for c in range(3)]
+    moves.append((out_weight_ref, rows_ref.at[pl.ds(3 * width, width)]))
+    run_all([pltpu.make_async_copy(a, b, sems.at[i]) for i, (a, b) in enumerate(moves)])
+    flat = (lats * HALF * levels, depth)
+    projected = jnp.concatenate(
+        [
+            dot_nt(raw_ref[0].reshape(flat), rows_ref[: 3 * width, :]),
+            dot_nt(raw_ref[1].reshape(flat), rows_ref[3 * width :, :]),
+        ],
+        axis=1,
+    ).astype(BF16)
+    for lat in range(lats):
+        for col in range(HALF):
+            start = (lat * HALF + col) * levels
+            projected_ref[col, lat * levels : (lat + 1) * levels, :] = projected[
+                start : start + levels, :
+            ]
 
 
 def prepare_kernel(
     kind_ref, x_ref, g_ref, weight_ref, out_weight_ref, table_ref,
-    turned_ref, projected_ref, weights_ref, natural_ref, pieces_ref,
+    bias_ref, near_ref, weights_ref,
+    own_ref, given_ref, chosen_ref, natural_ref, pieces_ref, sems,
 ):
     lats, cols, levels, depth = x_ref.shape
     heads = table_ref.shape[0]
     slots = kind_ref.shape[0]
     count = table_ref.shape[2]
     width = out_weight_ref.shape[0]
-    weights_ref[...] = jnp.zeros(weights_ref.shape, BF16)
-    for c in range(3):
-        weights_ref[c * LANES : c * LANES + width, :] = weight_ref[c]
-    weights_ref[3 * LANES : 3 * LANES + width, :] = out_weight_ref[...]
-    flat = (lats * cols * levels, depth)
-    projected = project(x_ref[...].reshape(flat), g_ref[...].reshape(flat), weights_ref[...])
-    for lat in range(lats):
-        for col in range(cols):
-            start = (lat * cols + col) * levels
-            projected_ref[col, lat * levels : (lat + 1) * levels, :] = projected[
-                start : start + levels, :
-            ].astype(BF16)
+    number = heads * slots
+    moves = []
+    for slot in range(slots):
+        for h in range(heads):
+            source = table_ref.at[h, pl.ds(kind_ref[slot, 0], 1), :]
+            moves.append((source, chosen_ref.at[pl.ds(h * slots + slot, 1), :]))
+    moves += [(x_ref, own_ref), (g_ref, given_ref)]
+    moves += [(weight_ref.at[c], weights_ref.at[pl.ds(c * LANES, width)]) for c in range(3)]
+    moves.append((out_weight_ref, weights_ref.at[pl.ds(3 * LANES, width)]))
+    copies = [pltpu.make_async_copy(a, b, sems.at[i]) for i, (a, b) in enumerate(moves)]
+    for copy in copies:
+        copy.start()
+    for c in range(4):
+        weights_ref[c * LANES + width : (c + 1) * LANES, :] = jnp.zeros(
+            (LANES - width, depth), BF16
+        )
     natural_ref[...] = jnp.zeros(natural_ref.shape, F32)
     pieces_ref[...] = jnp.zeros(pieces_ref.shape, F32)
-    for h in range(heads):
-        for slot in range(slots):
-            row = h * slots + slot
-            natural_ref[row : row + 1, :count] = table_ref[h, pl.ds(kind_ref[slot, 0], 1), :]
-    number = heads * slots
+    for copy in copies[:number]:
+        copy.wait()
+    natural_ref[:number, :count] = chosen_ref[...]
     for place, level_j, start in table_pieces():
         low = start // LANES * LANES
         block = natural_ref[:, low : low + 3 * LANES]
@@ -137,106 +154,139 @@
     lane = lax.broadcasted_iota(jnp.int32, turned.shape, 1)
     turned = jnp.where(lax.bitwise_and(lane, PAD - 1) < ROWS, turned, MASKED)
     for h in range(heads):
-        turned_ref[h] = turned[h * slots * PAD : (h + 1) * slots * PAD, :]
-
-
-def main_kernel(
-    shift_ref, x_ref, g_ref, far_ref, near_ref, weights_ref, turned_ref, *rest
-):
+        for slot in range(slots):
+            row = (h * slots + slot) * PAD
+            table = turned[row : row + PAD, :]
+            for col in range(WIN_LON):
+                by = (WIN_LON - 1 - col) * PAD
+                moved = table if by == 0 else pltpu.roll(table, SPAN - by, 1)
+                start = h * WIDE + col * PAD
+                bias_ref[slot, start : start + PAD, :] = moved[:, :WIDE]
+    for copy in copies[number:]:
+        copy.wait()
+    flat = (lats * cols * levels, depth)
+    projected = project(own_ref[...].reshape(flat), given_ref[...].reshape(flat), weights_ref[...])
+    for lat in range(lats):
+        for col in range(cols):
+            start = (lat * cols + col) * levels
+            near_ref[col, lat * levels : (lat + 1) * levels, :] = projected[
+                start : start + levels, :
+            ].astype(BF16)
+
+
+def project(rows_x, rows_g, weights):
+    width = 3 * LANES
+    return jnp.concatenate(
+        [dot_nt(rows_x, weights[:width]), dot_nt(rows_g, weights[width:])], axis=1
+    )
+
+
+def column_source(shift, col, cols):
+    low = shift <= HALF
+    at = col + shift
+    inside = jnp.logical_xor(low, at >= cols)
+    local = jnp.where(at >= cols, at - cols, at)
+    taken = jnp.where(low, at - cols, at - (cols - HALF))
+    return inside, local, jnp.clip(taken, 0, HALF - 1)
+
+
+def main_kernel(shift_ref, far_ref, near_ref, weights_ref, bias_ref, *rest):
     n_head = lax.axis_size("head")
     pieces = rest[:n_head]
-    sums_ref, folded_ref = rest[n_head : n_head + 2]
-    beyond_ref, own_ref, ordered_ref, bias_ref, given_ref, back_ref, chunk_ref = rest[n_head + 2 :]
-    lats, cols, levels, depth = x_ref.shape
-    width = sums_ref.shape[1]
-    heads, slot_rows = turned_ref.shape[0], turned_ref.shape[1]
-    slots = slot_rows // PAD
+    back_ref, folded_ref = rest[n_head : n_head + 2]
+    (
+        beyond_ref, ordered_ref, score_ref, slope_ref, soft_ref, grad_ref, exact_ref, given_ref,
+        chunk_ref,
+    ) = rest[n_head + 2 :]
+    cols, tall, _ = near_ref.shape
+    levels = tall // WIN_LAT
+    slots = bias_ref.shape[0]
+    heads = bias_ref.shape[1] // WIDE
+    width = far_ref.shape[2] // 4
     size = width // heads
     scaling = size ** (-0.5)
     mine = lax.axis_index("head")
     shift = shift_ref[0]
-    low = shift <= HALF
-    tall = lats * levels
-    flat = (lats * HALF * levels, depth)
-    projected = project(far_ref[0].reshape(flat), far_ref[1].reshape(flat), weights_ref[...])
-    for lat in range(lats):
-        for col in range(HALF):
-            start = (lat * HALF + col) * levels
-            beyond_ref[col, lat * levels : (lat + 1) * levels, :] = projected[
-                start : start + levels, :
-            ].astype(BF16)
+    for c in range(4):
+        beyond_ref[:, :, c * LANES : c * LANES + width] = far_ref[
+            :, :, c * width : (c + 1) * width
+        ]
+        beyond_ref[:, :, c * LANES + width : (c + 1) * LANES] = jnp.zeros(
+            (HALF, tall, LANES - width), BF16
+        )
     order = window_order(levels)
     for col in range(cols):
-        at = col + shift
-        inside = jnp.logical_xor(low, at >= cols)
-        local = jnp.where(at >= cols, at - cols, at)
-        taken = jnp.where(low, at - cols, at - (cols - HALF))
-        taken = jnp.clip(taken, 0, HALF - 1)
+        inside, local, taken = column_source(shift, col, cols)
         rows = jnp.where(inside, near_ref[local], beyond_ref[taken])
         ordered = dot_nn(order, rows).astype(BF16)
         for slot in range(slots):
             ordered_ref[slot, col * PAD : (col + 1) * PAD, :] = ordered[
                 slot * PAD : (slot + 1) * PAD, :
             ]
-        for array, ref in enumerate((x_ref, g_ref)):
-            for lat in range(lats):
-                start = col * tall + lat * levels
-                own_ref[array, start : start + levels, :] = jnp.where(
-                    inside, ref[lat, local], far_ref[array, lat, taken]
-                )
     lane = lax.broadcasted_iota(jnp.int32, (WIDE, LANES), 1)
     masks = [(lane >= h * size) & (lane < (h + 1) * size) for h in range(heads)]
     none = jnp.zeros((WIDE, LANES), BF16)
+
+    def by_head(array):
+        return jnp.concatenate([jnp.where(mask, array, none) for mask in masks], axis=0)
+
+    def own_lanes(array):
+        total = jnp.where(masks[0], array[:WIDE, :], 0.0)
+        for h in range(1, heads):
+            total = jnp.where(masks[h], array[h * WIDE : (h + 1) * WIDE, :], total)
+        return total
+
+    block = 3 * PAD
     for slot in range(slots):
+        half = slot % 2
         query = ordered_ref[slot, :, :LANES]
         key = ordered_ref[slot, :, LANES : 2 * LANES]
         value = ordered_ref[slot, :, 2 * LANES : 3 * LANES]
-        grad_attended = ordered_ref[slot, :, 3 * LANES :]
-        at = slice(slot * PAD, (slot + 1) * PAD)
-        attended = jnp.zeros((WIDE, LANES), F32)
-        grad_query = jnp.zeros((WIDE, LANES), F32)
-        grad_key = jnp.zeros((WIDE, LANES), F32)
-        grad_value = jnp.zeros((WIDE, LANES), F32)
-        for h in range(heads):
-            table = turned_ref[h, at, :]
-            for col in range(WIN_LON):
-                by = (WIN_LON - 1 - col) * PAD
-                moved = table if by == 0 else pltpu.roll(table, SPAN - by, 1)
-                bias_ref[h, col * PAD : (col + 1) * PAD, :] = moved[:, :WIDE]
-            query_h = jnp.where(masks[h], query, none)
-            key_h = jnp.where(masks[h], key, none)
-            value_h = jnp.where(masks[h], value, none)
-            grad_h = jnp.where(masks[h], grad_attended, none)
-            scores = dot_nt(query_h, key) * scaling + bias_ref[h]
+        queries = by_head(query)
+        grads = by_head(ordered_ref[slot, :, 3 * LANES :])
+        score_ref[half] = dot_nt(queries, key)
+        slope_ref[half] = dot_nt(grads, value)
+        for start in range(0, heads * WIDE, block):
+            at = slice(start, start + block)
+            scores = score_ref[half, at, :] * scaling + bias_ref[slot, at, :]
             raised = jnp.exp(scores - jnp.max(scores, axis=1, keepdims=True))
             softened = raised * (1.0 / jnp.sum(raised, axis=1, keepdims=True))
-            softened_half = softened.astype(BF16)
-            attended = attended + dot_nn(softened_half, value_h)
-            grad_value = grad_value + dot_tn(softened_half, grad_h)
-            grad_softened = dot_nt(grad_h, value)
-            inner = jnp.sum(softened * grad_softened, axis=1, keepdims=True)
-            grad_scores = softened * (grad_softened - inner)
-            grad_half = grad_scores.astype(BF16)
-            grad_query = grad_query + dot_nn(grad_half, key_h)
-            grad_key = grad_key + dot_tn(grad_half, query_h)
-            padded = jnp.concatenate([grad_scores, jnp.zeros((WIDE, SPAN - WIDE), F32)], axis=1)
+            soft_ref[half, at, :] = softened.astype(BF16)
+            slope = slope_ref[half, at, :]
+            inner = jnp.sum(softened * slope, axis=1, keepdims=True)
+            grad_scores = softened * (slope - inner)
+            grad_ref[half, at, :] = grad_scores.astype(BF16)
+            exact_ref[half, at, :WIDE] = grad_scores
+        for h in range(heads):
             total = jnp.zeros((PAD, SPAN), F32)
             for col in range(WIN_LON):
                 by = (WIN_LON - 1 - col) * PAD
-                part = padded[col * PAD : (col + 1) * PAD, :]
+                start = h * WIDE + col * PAD
+                part = jnp.concatenate(
+                    [
+                        exact_ref[half, start : start + PAD, :WIDE],
+                        jnp.zeros((PAD, SPAN - WIDE), F32),
+                    ],
+                    axis=1,
+                )
                 total = total + (part if by == 0 else pltpu.roll(part, by, 1))
-            folded_ref[h, at, :] = total
-        results = (grad_query * scaling, grad_key * scaling, grad_value, attended)
+            folded_ref[h, slot * PAD : (slot + 1) * PAD, :] = total
+        results = (
+            own_lanes(dot_nn(grad_ref[half], key)) * scaling,
+            dot_tn(grad_ref[half], queries) * scaling,
+            dot_tn(soft_ref[half], grads),
+            own_lanes(dot_nn(soft_ref[half], value)),
+        )
+        rows = slice(slot * PAD, (slot + 1) * PAD)
         for c, result in enumerate(results):
             rounded = result.astype(BF16)
             for col in range(WIN_LON):
-                given_ref[col, at, c * LANES : (c + 1) * LANES] = rounded[
+                given_ref[col, rows, c * LANES : (c + 1) * LANES] = rounded[
                     col * PAD : (col + 1) * PAD, :
                 ]
     for col in range(WIN_LON):
         back_ref[col * tall : (col + 1) * tall, :] = dot_tn(order, given_ref[col]).astype(BF16)
-    grads = 3 * LANES
-    piece = dot_nn(back_ref[:, :grads], weights_ref[:grads, :])
+    piece = dot_nn(back_ref[:, : 3 * LANES], weights_ref[: 3 * LANES, :])
     group = WIN_LON // 4 * tall
     third = width // 3
     for to in range(n_head):
@@ -248,6 +298,20 @@
             ).astype(BF16)
     for step in range(n_head):
         pieces[step][...] = chunk_ref[lax.rem(mine + step, n_head)]
+
+
+def sums_kernel(shift_ref, x_ref, g_ref, far_ref, back_ref, sums_ref, own_ref):
+    lats, cols, levels, _ = x_ref.shape
+    width = sums_ref.shape[1]
+    for col in range(cols):
+        inside, local, taken = column_source(shift_ref[0], col, cols)
+        for array, ref in enumerate((x_ref, g_ref)):
+            for lat in range(lats):
+                start = (col * lats + lat) * levels
+                own_ref[array, start : start + levels, :] = jnp.where(
+                    inside, ref[lat, local], far_ref[array, lat, taken]
+                )
+    grads = 3 * LANES
     summed = dot_tn(back_ref[:, :grads], own_ref[0])
     for c in range(3):
         sums_ref[c] = summed[c * LANES : c * LANES + width, :].astype(BF16)
@@ -408,55 +472,78 @@
     g = grad_out.transpose(1, 2, 0, 3)
     weight = attend_weight.transpose(0, 2, 1)
     table = bias_table.transpose(1, 0, 2)
-    slab = pl.pallas_call(
-        pack_kernel,
-        name="pack",
-        out_shape=shape((2, lats, HALF, levels, depth), BF16),
-        in_specs=[SMEM, HBM, HBM],
-        out_specs=VMEM,
-        scratch_shapes=[pltpu.SemaphoreType.DMA((2,))],
-        compiler_params=small(4),
-    )(window_shift, x, g)
-    far = exchange(slab, "lon", window_shift, 1)
+    stored = [
+        pltpu.with_memory_space_constraint(array, pltpu.HBM)
+        for array in (x, g, weight, output_weight, table)
+    ]
+    raw, projected = pl.pallas_call(
+        start_kernel,
+        name="start",
+        out_shape=[
+            shape((2, lats, HALF, levels, depth), BF16),
+            shape((HALF, tall, 4 * width), BF16),
+        ],
+        in_specs=[SMEM] + [HBM] * 4,
+        out_specs=[VMEM] * 2,
+        scratch_shapes=[pltpu.VMEM((4 * width, depth), BF16), pltpu.SemaphoreType.DMA((6,))],
+        compiler_params=small(8),
+    )(window_shift, *stored[:4])
+    far = exchange(projected, "lon", window_shift, 1)
+    far_raw = exchange(raw, "lon", window_shift, 1)
     natural = -(-count // LANES) * LANES + LANES
-    turned, near, weights = pl.pallas_call(
+    bias, near, weights = pl.pallas_call(
         prepare_kernel,
         name="prepare",
         out_shape=[
-            shape((heads, slots * PAD, SPAN), F32),
+            shape((slots, heads * WIDE, WIDE), F32),
             shape((cols, tall, 4 * LANES), BF16),
             shape((4 * LANES, depth), BF16),
         ],
-        in_specs=[SMEM] + [VMEM] * 5,
+        in_specs=[SMEM] + [HBM] * 5,
         out_specs=[VMEM] * 3,
         scratch_shapes=[
+            pltpu.VMEM((lats, cols, levels, depth), BF16),
+            pltpu.VMEM((lats, cols, levels, depth), BF16),
+            pltpu.VMEM((number, count), F32),
             pltpu.VMEM((PAD, natural), F32),
             pltpu.VMEM((2 * WIN_LEVEL, number * PAD, LANES), F32),
+            pltpu.SemaphoreType.DMA((number + 6,)),
         ],
         compiler_params=small(16),
-    )(bias_type, x, g, weight, output_weight, table)
+    )(bias_type, *stored)
     packed = 3 * (cols // 4) * tall
-    *pieces, sums, folded = pl.pallas_call(
+    *pieces, own_back, folded = pl.pallas_call(
         main_kernel,
         name="main",
         out_shape=[shape((packed, LANES), BF16)] * n_head
         + [
-            shape((4, width, depth), BF16),
+            shape((cols * tall, 4 * LANES), BF16),
             shape((heads, slots * PAD, SPAN), F32),
         ],
-        in_specs=[SMEM] + [VMEM] * 6,
+        in_specs=[SMEM] + [VMEM] * 4,
         out_specs=[VMEM] * (n_head + 2),
         scratch_shapes=[
             pltpu.VMEM((HALF, tall, 4 * LANES), BF16),
-            pltpu.VMEM((2, cols * tall, depth), BF16),
             pltpu.VMEM((slots, WIDE, 4 * LANES), BF16),
-            pltpu.VMEM((heads, WIDE, WIDE), F32),
+            pltpu.VMEM((2, heads * WIDE, WIDE), F32),
+            pltpu.VMEM((2, heads * WIDE, WIDE), F32),
+            pltpu.VMEM((2, heads * WIDE, WIDE), BF16),
+            pltpu.VMEM((2, heads * WIDE, WIDE), BF16),
+            pltpu.VMEM((2, heads * WIDE, WIDE), F32),
             pltpu.VMEM((cols, slots * PAD, 4 * LANES), BF16),
-            pltpu.VMEM((cols * tall, 4 * LANES), BF16),
             pltpu.VMEM((n_head, packed, LANES), BF16),
         ],
         compiler_params=small(24),
-    )(window_shift, x, g, far, near, weights, turned)
+    )(window_shift, far, near, weights, bias)
+    sums = pl.pallas_call(
+        sums_kernel,
+        name="weight_sums",
+        out_shape=shape((4, width, depth), BF16),
+        in_specs=[SMEM] + [VMEM] * 4,
+        out_specs=VMEM,
+        scratch_shapes=[pltpu.VMEM((2, cols * tall, depth), BF16)],
+        compiler_params=small(8),
+    )(window_shift, x, g, far_raw, own_back)
     parts = [pieces[0]]
     for step in range(1, n_head):
         ring = [(i, (i + step) % n_head) for i in range(n_head)]

time: 57.5 us -> 59.2 us (1.030)
  waiting for transfers between devices: 7.84 us -> 16.2 us
  local copies, waits for them, and re-layouts: 8.33 us -> 0.75 us
  Pallas kernels: 14.2 us -> 15.3 us
    ppermute x2 -> x3, waiting for transfers between devices: 2.31 us -> 10.7 us  [exchange(): lax.ppermute(x, axis, [(i, (i - sign) % count) for i in range(count)])]
    unnamed x19 -> x5, local copies, waits for them, and re-layouts: 8.33 us -> 0.75 us
    pallas_call x2 -> x3, Pallas kernels: 1.65 us -> 6.39 us  [the longest x1 3.39 us: per_device(): pl.pallas_call(prepare_kernel, name='prepare', out_shape=[shape((slots, h...]
    pallas_call x1, Pallas kernels: 9.05 us -> 5.35 us  [per_device(): pl.pallas_call(main_kernel, name='main', out_shape=[shape((packed, LANES)...]
    ppermute x2 -> x3, starting transfers between devices: 4.76 us -> 4.84 us  [exchange(): lax.ppermute(x, axis, [(i, (i - sign) % count) for i in range(count)])]
  transfers between devices with their start and end apart: 6 -> 7, of which waited for: 3 -> 3; matrix products, arithmetic and copies ran while one was open for 1% -> 1% of each run, Pallas kernels for 5% -> 17%
where the time goes in v3:
time: 59.2 us; the launch traced here: 58.6 us
  waiting for transfers between devices  16.2 us (27%)
  Pallas kernels  15.3 us (26%)
  starting transfers between devices  14.3 us (24%)
  blocking collectives  10.7 us (18%)
  between operations  1.36 us (2%)
  local copies, waits for them, and re-layouts  0.75 us (1%)
    all_gather x1, blocking collectives, per_device(): gathered = lax.all_gather(share, every, axis=0)  10.7 us
    ppermute x3, waiting for transfers between devices, exchange(): lax.ppermute(x, axis, [(i, (i - sign) % count) for i in range(count)])  10.7 us
    ppermute x3, waiting for transfers between devices, per_device(): parts.append(lax.ppermute(pieces[step], 'head', ring))  5.54 us
    ppermute x3, starting transfers between devices, per_device(): parts.append(lax.ppermute(pieces[step], 'head', ring))  5.48 us
    pallas_call x1, Pallas kernels, per_device(): pl.pallas_call(main_kernel, name='main', out_shape=[shape((packed, LANES)...  5.35 us
    ppermute x3, starting transfers between devices, exchange(): lax.ppermute(x, axis, [(i, (i - sign) % count) for i in range(count)])  4.84 us
    all_to_all x1, starting transfers between devices, per_device(): shares = lax.all_to_all(shares, every, 0, 0)  3.99 us
    pallas_call x1, Pallas kernels, per_device(): pl.pallas_call(prepare_kernel, name='prepare', out_shape=[shape((slots, h...  3.39 us
  transfers between devices with their start and end apart: 7, of which 3 were waited for; matrix products, arithmetic and copies ran while one was open for 1% of the time, Pallas kernels for 17%

profile of v3, /device:TPU:0, one launch (start us, length us, event | category | flops | bytes accessed | tf_op | source)
XLA Modules:
  0.0 58.6 jit_solution(18016288275780332876)
XLA Ops:
  1.3 1.7 %start.1 = (bf16[2,6,6,8,384]{4,3,2,1,0:T(8,128)(2,1)S(1)}, bf16[6,48,384]{2,1,0:T(8,128)(2,1)S(1)}) custom-call(s32[1]{0:T(128)S(6)} %copy.13.shift_ref, bf16[6,12,8,384]{3,2,1,0:T(8,128)(2,1)} %bitcast.9, bf16[6,12,8,384]{3,2,1,0:T(8,128)(2,1)} %bitcast.12, bf16[3,96,384]{2,1,0:T(8,128)(2,1)} %bitcast.17, bf16[96,384]{1,0:T(8,128)(2,1)} %out_weight_ref.3), custom_call_target="tpu_custom_call" | custom-call | tf_op jit(solution)/shard_map/start/pallas_call | solution.py:479
  3.0 3.0 %collective-permute-start = (bf16[2,6,6,8,384]{4,3,2,1,0:T(8,128)(2,1)S(1)}, bf16[2,6,6,8,384]{4,3,2,1,0:T(8,128)(2,1)S(1)}, u32[]{:S(2)}, u32[]{:S(2)}) collective-permute-start(bf16[2,6,6,8,384]{4,3,2,1,0:T(8,128)(2,1)S(1)} %get-tuple-element.21), channel_id=1, source_target_pairs={{0,16},{16,0},{1,17},{17,1},{2,18},{18,2},{3,19},{19,3},{4,20},{20... | collective-permute-start | bytes 1327112 | tf_op jit(solution)/shard_map/ppermute | solution.py:451
  6.0 0.1 collective-permute-start.1
  6.1 0.7 %copy.11.kind_ref = s32[4,1]{1,0:T(4,128)S(1)} copy(s32[4,1]{0,1:T(1,128)} %param.11) | data formatting | bytes 32 | tf_op args[4]
  6.8 3.4 %prepare.1 = (f32[4,576,192]{2,1,0:T(8,128)S(1)}, bf16[12,48,512]{2,1,0:T(8,128)(2,1)S(1)}, bf16[512,384]{1,0:T(8,128)(2,1)S(1)}) custom-call(s32[4,1]{1,0:T(4,128)S(1)} %copy.11.kind_ref, bf16[6,12,8,384]{3,2,1,0:T(8,128)(2,1)} %bitcast.10, bf16[6,12,8,384]{3,2,1,0:T(8,128)(2,1)} %bitcast.13, bf16[3,96,384]{2,1,0:T(8,128)(2,1)} %bitcast.18, ...), custom_call_target="tpu_custom_call" | custom-call | tf_op jit(solution)/shard_map/prepare/pallas_call | solution.py:494
  10.2 0.0 copy-start
  10.2 0.0 copy-start.1
  10.2 10.7 %collective-permute-done.1.far_ref = bf16[6,48,384]{2,1,0:T(8,128)(2,1)S(1)} collective-permute-done((bf16[6,48,384]{2,1,0:T(8,128)(2,1)S(1)}, bf16[6,48,384]{2,1,0:T(8,128)(2,1)S(1)}, u32[]{:S(2)}, u32[]{:S(2)}) %collective-permute-start.1) | collective-permute-done | bytes 221216 | tf_op jit(solution)/shard_map/ppermute | solution.py:451
  20.9 5.4 %main.1 = (bf16[432,128]{1,0:T(8,128)(2,1)S(1)}, bf16[432,128]{1,0:T(8,128)(2,1)S(1)}, bf16[432,128]{1,0:T(8,128)(2,1)S(1)}, bf16[432,128]{1,0:T(8,128)(2,1)S(1)...) custom-call(s32[1]{0:T(128)S(6)} %copy.13.shift_ref, bf16[6,48,384]{2,1,0:T(8,128)(2,1)S(1)} %collective-permute-done.1.far_ref, ...), custom_call_target="tpu_custom_call" | custom-call | tf_op jit(solution)/shard_map/main/pallas_call | solution.py:515
  26.3 0.0 collective-permute-done.far_ref
  26.3 0.0 copy-done
  26.3 0.0 copy-done.1
  26.3 1.3 %weight_sums.1 = bf16[4,96,384]{2,1,0:T(8,128)(2,1)} custom-call(s32[1]{0:T(128)S(6)} %copy.13.shift_ref, bf16[6,12,8,384]{3,2,1,0:T(8,128)(2,1)S(1)} %bitcast.11, bf16[6,12,8,384]{3,2,1,0:T(8,128)(2,1)S(1)} %bitcast.14, bf16[2,6,6,8,384]{4,3,2,1,0:T(8,128)(2,1)S(1)} %collective-permute-done.far_ref, bf16[576,512]{1,0:T(8,128)(2,1)S(1)} %get-tuple-element.26.back_ref), custom_call_target="tpu_custom_call" | custom-call | tf_op jit(solution)/shard_map/weight_sums/pallas_call | solution.py:538
  27.6 4.0 %all-to-all-start = ((bf16[8,48,384]{2,1,0:T(8,128)(2,1)}), bf16[8,48,384]{2,1,0:T(8,128)(2,1)S(1)}, u32[]{:S(2)}, u32[]{:S(2)}) async-start(bf16[8,48,384]{2,1,0:T(8,128)(2,1)} %bitcast.4), calls=%async_computation | async-start | bytes 589824 | tf_op jit(solution)/shard_map/all_to_all | solution.py:554
  31.6 1.6 %collective-permute-start.2 = (bf16[432,128]{1,0:T(8,128)(2,1)S(1)}, bf16[432,128]{1,0:T(8,128)(2,1)S(1)}, u32[]{:S(2)}, u32[]{:S(2)}) collective-permute-start(bf16[432,128]{1,0:T(8,128)(2,1)S(1)} %get-tuple-element.29), channel_id=1, source_target_pairs={{0,1},{1,2},{2,3},{3,0},{4,5},{5,6},{6,7},{7,4},{8,9},{9,10},{10,1... | collective-permute-start | bytes 331784 | tf_op jit(solution)/shard_map/ppermute | solution.py:550
  33.2 2.6 %collective-permute-start.3 = (bf16[432,128]{1,0:T(8,128)(2,1)S(1)}, bf16[432,128]{1,0:T(8,128)(2,1)S(1)}, u32[]{:S(2)}, u32[]{:S(2)}) collective-permute-start(bf16[432,128]{1,0:T(8,128)(2,1)S(1)} %get-tuple-element.30), channel_id=1, source_target_pairs={{0,2},{1,3},{2,0},{3,1},{4,6},{5,7},{6,4},{7,5},{8,10},{9,11},{10,... | collective-permute-start | bytes 331784 | tf_op jit(solution)/shard_map/ppermute | solution.py:550
  35.7 1.3 %collective-permute-start.4 = (bf16[432,128]{1,0:T(8,128)(2,1)S(1)}, bf16[432,128]{1,0:T(8,128)(2,1)S(1)}, u32[]{:S(2)}, u32[]{:S(2)}) collective-permute-start(bf16[432,128]{1,0:T(8,128)(2,1)S(1)} %get-tuple-element.31), channel_id=1, source_target_pairs={{0,3},{1,0},{2,1},{3,2},{4,7},{5,4},{6,5},{7,6},{8,11},{9,8},{10,9... | collective-permute-start | bytes 331784 | tf_op jit(solution)/shard_map/ppermute | solution.py:550
  37.1 1.1 %bias_rows.1.rows_ref = bf16[104,384]{1,0:T(8,128)(2,1)S(1)} custom-call(s32[4,1]{1,0:T(4,128)S(1)} %copy.11.kind_ref, f32[3,64,384]{2,1,0:T(8,128)S(1)} %get-tuple-element.27.folded_ref), custom_call_target="tpu_custom_call" | custom-call | tf_op jit(solution)/shard_map/bias_rows/pallas_call | solution.py:557
  38.2 1.3 %collective-permute-done.2.refs_1_ = bf16[432,128]{1,0:T(8,128)(2,1)S(1)} collective-permute-done((bf16[432,128]{1,0:T(8,128)(2,1)S(1)}, bf16[432,128]{1,0:T(8,128)(2,1)S(1)}, u32[]{:S(2)}, u32[]{:S(2)}) %collective-permute-start.2) | collective-permute-done | bytes 110624 | tf_op jit(solution)/shard_map/ppermute | solution.py:550
  39.4 4.3 %collective-permute-done.3.refs_2_ = bf16[432,128]{1,0:T(8,128)(2,1)S(1)} collective-permute-done((bf16[432,128]{1,0:T(8,128)(2,1)S(1)}, bf16[432,128]{1,0:T(8,128)(2,1)S(1)}, u32[]{:S(2)}, u32[]{:S(2)}) %collective-permute-start.3) | collective-permute-done | bytes 110624 | tf_op jit(solution)/shard_map/ppermute | solution.py:550
  43.7 0.0 collective-permute-done.4.refs_3_
  43.7 0.1 sum_heads.1
  43.9 1.7 %collective-permute-start.5 = (bf16[6,48,96]{2,1,0:T(8,128)(2,1)S(1)}, bf16[6,48,96]{2,1,0:T(8,128)(2,1)S(1)}, u32[]{:S(2)}, u32[]{:S(2)}) collective-permute-start(bf16[6,48,96]{2,1,0:T(8,128)(2,1)S(1)} %get-tuple-element.33), channel_id=1, source_target_pairs={{0,16},{16,0},{1,17},{17,1},{2,18},{18,2},{3,19},{19,3},{4,20},{20... | collective-permute-start | bytes 165896 | tf_op jit(solution)/shard_map/ppermute | solution.py:451
  45.6 0.0 all-to-all-done.shares_ref
  45.6 0.1 share.1
  45.7 10.7 %all-gather = bf16[1216,384]{1,0:T(8,128)(2,1)S(1)} all-gather(bf16[152,384]{1,0:T(8,128)(2,1)S(1)} %share.1), channel_id=2, replica_groups=mesh['lon'=2,'lat'=4,'head'=4] {'lon','lat'}, dimensions={0}, use_global_device_ids=true | all-gather | bytes 1050624 | tf_op jit(solution)/shard_map/all_gather | solution.py:587
  56.3 0.0 collective-permute-done.5.returned_ref
  56.4 2.3 %finish.1 = (bf16[6,12,8,96]{3,2,1,0:T(8,128)(2,1)}, f32[3,96,384]{2,1,0:T(8,128)}, f32[96,384]{1,0:T(8,128)}, f32[3,64,3312]{2,1,0:T(8,128)}) custom-call(s32[1]{0:T(128)S(6)} %copy.13.shift_ref, bf16[8,152,384]{2,1,0:T(8,128)(2,1)S(1)} %bitcast.15, bf16[12,48,96]{2,1,0:T(8,128)(2,1)S(1)} %get-tuple-element.32.summed_ref, ...), custom_call_target="tpu_custom_call" | custom-call | tf_op jit(solution)/shard_map/finish/pallas_call | solution.py:588
Async XLA Ops:
  3.0 23.3 %collective-permute-start = (bf16[2,6,6,8,384]{4,3,2,1,0:T(8,128)(2,1)S(1)}, bf16[2,6,6,8,384]{4,3,2,1,0:T(8,128)(2,1)S(1)}, u32[]{:S(2)}, u32[]{:S(2)}) collective-permute-start(bf16[2,6,6,8,384]{4,3,2,1,0:T(8,128)(2,1)S(1)} %get-tuple-element.21), channel_id=1, source_target_pairs={{0,16},{16,0},{1,17},{17,1},{2,18},{18,2},{3,19},{19,3},{4,20},{20... | collective-permute-start | bytes 1327112 | tf_op jit(solution)/shard_map/ppermute | solution.py:451
  6.0 14.9 %collective-permute-start.1 = (bf16[6,48,384]{2,1,0:T(8,128)(2,1)S(1)}, bf16[6,48,384]{2,1,0:T(8,128)(2,1)S(1)}, u32[]{:S(2)}, u32[]{:S(2)}) collective-permute-start(bf16[6,48,384]{2,1,0:T(8,128)(2,1)S(1)} %get-tuple-element.22), channel_id=1, source_target_pairs={{0,16},{16,0},{1,17},{17,1},{2,18},{18,2},{3,19},{19,3},{4,20},{20... | collective-permute-start | bytes 663560 | tf_op jit(solution)/shard_map/ppermute | solution.py:451
  10.2 16.1 %copy-start = (bf16[8,6,12,384]{3,0,2,1:T(8,128)(2,1)S(1)}, bf16[8,6,12,384]{3,0,2,1:T(8,128)(2,1)}, u32[]{:S(2)}) copy-start(bf16[8,6,12,384]{3,0,2,1:T(8,128)(2,1)} %param.7) | copy-start | bytes 1327108
  10.2 16.1 %copy-start.1 = (bf16[8,6,12,384]{3,0,2,1:T(8,128)(2,1)S(1)}, bf16[8,6,12,384]{3,0,2,1:T(8,128)(2,1)}, u32[]{:S(2)}) copy-start(bf16[8,6,12,384]{3,0,2,1:T(8,128)(2,1)} %param.13) | copy-start | bytes 1327108
  27.6 18.0 %all-to-all-start = ((bf16[8,48,384]{2,1,0:T(8,128)(2,1)}), bf16[8,48,384]{2,1,0:T(8,128)(2,1)S(1)}, u32[]{:S(2)}, u32[]{:S(2)}) async-start(bf16[8,48,384]{2,1,0:T(8,128)(2,1)} %bitcast.4), calls=%async_computation | async-start | bytes 589824 | tf_op jit(solution)/shard_map/all_to_all | solution.py:554
  31.6 7.8 %collective-permute-start.2 = (bf16[432,128]{1,0:T(8,128)(2,1)S(1)}, bf16[432,128]{1,0:T(8,128)(2,1)S(1)}, u32[]{:S(2)}, u32[]{:S(2)}) collective-permute-start(bf16[432,128]{1,0:T(8,128)(2,1)S(1)} %get-tuple-element.29), channel_id=1, source_target_pairs={{0,1},{1,2},{2,3},{3,0},{4,5},{5,6},{6,7},{7,4},{8,9},{9,10},{10,1... | collective-permute-start | bytes 331784 | tf_op jit(solution)/shard_map/ppermute | solution.py:550
  33.2 10.5 %collective-permute-start.3 = (bf16[432,128]{1,0:T(8,128)(2,1)S(1)}, bf16[432,128]{1,0:T(8,128)(2,1)S(1)}, u32[]{:S(2)}, u32[]{:S(2)}) collective-permute-start(bf16[432,128]{1,0:T(8,128)(2,1)S(1)} %get-tuple-element.30), channel_id=1, source_target_pairs={{0,2},{1,3},{2,0},{3,1},{4,6},{5,7},{6,4},{7,5},{8,10},{9,11},{10,... | collective-permute-start | bytes 331784 | tf_op jit(solution)/shard_map/ppermute | solution.py:550
  35.7 8.0 %collective-permute-start.4 = (bf16[432,128]{1,0:T(8,128)(2,1)S(1)}, bf16[432,128]{1,0:T(8,128)(2,1)S(1)}, u32[]{:S(2)}, u32[]{:S(2)}) collective-permute-start(bf16[432,128]{1,0:T(8,128)(2,1)S(1)} %get-tuple-element.31), channel_id=1, source_target_pairs={{0,3},{1,0},{2,1},{3,2},{4,7},{5,4},{6,5},{7,6},{8,11},{9,8},{10,9... | collective-permute-start | bytes 331784 | tf_op jit(solution)/shard_map/ppermute | solution.py:550
  43.9 12.5 %collective-permute-start.5 = (bf16[6,48,96]{2,1,0:T(8,128)(2,1)S(1)}, bf16[6,48,96]{2,1,0:T(8,128)(2,1)S(1)}, u32[]{:S(2)}, u32[]{:S(2)}) collective-permute-start(bf16[6,48,96]{2,1,0:T(8,128)(2,1)S(1)} %get-tuple-element.33), channel_id=1, source_target_pairs={{0,16},{16,0},{1,17},{17,1},{2,18},{18,2},{3,19},{19,3},{4,20},{20... | collective-permute-start | bytes 165896 | tf_op jit(solution)/shard_map/ppermute | solution.py:451

commit v4 on v3

--- a/solution.py
+++ b/solution.py
@@ -4,6 +4,7 @@
 from jax.experimental import pallas as pl
 from jax.experimental.pallas import tpu as pltpu
 from jax.sharding import PartitionSpec as P
+
 
 WIN_LEVEL = 2
 WIN_LAT = 6
@@ -78,20 +79,21 @@
 
 
 def start_kernel(
-    shift_ref, x_ref, g_ref, weight_ref, out_weight_ref, raw_ref, projected_ref, rows_ref, sems
+    shift_ref, x_ref, g_ref, weight_ref, out_weight_ref,
+    moved_ref, own_x_ref, own_g_ref, projected_ref, rows_ref, sems,
 ):
-    base = jnp.where(shift_ref[0] <= HALF, 0, WIN_LON - HALF)
     lats, _, levels, depth = x_ref.shape
     width = out_weight_ref.shape[0]
-    moves = [(ref.at[:, pl.ds(base, HALF)], raw_ref.at[i]) for i, ref in enumerate((x_ref, g_ref))]
+    moves = [(shift_ref, moved_ref), (x_ref, own_x_ref), (g_ref, own_g_ref)]
     moves += [(weight_ref.at[c], rows_ref.at[pl.ds(c * width, width)]) for c in range(3)]
     moves.append((out_weight_ref, rows_ref.at[pl.ds(3 * width, width)]))
     run_all([pltpu.make_async_copy(a, b, sems.at[i]) for i, (a, b) in enumerate(moves)])
+    base = jnp.where(moved_ref[0] <= HALF, 0, WIN_LON - HALF)
     flat = (lats * HALF * levels, depth)
     projected = jnp.concatenate(
         [
-            dot_nt(raw_ref[0].reshape(flat), rows_ref[: 3 * width, :]),
-            dot_nt(raw_ref[1].reshape(flat), rows_ref[3 * width :, :]),
+            dot_nt(own_x_ref[:, pl.ds(base, HALF)].reshape(flat), rows_ref[: 3 * width, :]),
+            dot_nt(own_g_ref[:, pl.ds(base, HALF)].reshape(flat), rows_ref[3 * width :, :]),
         ],
         axis=1,
     ).astype(BF16)
@@ -104,34 +106,44 @@
 
 
 def prepare_kernel(
-    kind_ref, x_ref, g_ref, weight_ref, out_weight_ref, table_ref,
-    bias_ref, near_ref, weights_ref,
-    own_ref, given_ref, chosen_ref, natural_ref, pieces_ref, sems,
+    shift_ref, x_ref, g_ref, rows_ref, kind_ref, table_ref,
+    kinds_ref, raw_ref, bias_ref, near_ref, weights_ref,
+    chosen_ref, natural_ref, pieces_ref, sems,
 ):
     lats, cols, levels, depth = x_ref.shape
     heads = table_ref.shape[0]
-    slots = kind_ref.shape[0]
+    slots = kind_ref.shape[1]
     count = table_ref.shape[2]
-    width = out_weight_ref.shape[0]
+    width = rows_ref.shape[0] // 4
     number = heads * slots
-    moves = []
+    run_all([pltpu.make_async_copy(kind_ref, kinds_ref, sems.at[number])])
+    copies = []
     for slot in range(slots):
         for h in range(heads):
-            source = table_ref.at[h, pl.ds(kind_ref[slot, 0], 1), :]
-            moves.append((source, chosen_ref.at[pl.ds(h * slots + slot, 1), :]))
-    moves += [(x_ref, own_ref), (g_ref, given_ref)]
-    moves += [(weight_ref.at[c], weights_ref.at[pl.ds(c * LANES, width)]) for c in range(3)]
-    moves.append((out_weight_ref, weights_ref.at[pl.ds(3 * LANES, width)]))
-    copies = [pltpu.make_async_copy(a, b, sems.at[i]) for i, (a, b) in enumerate(moves)]
-    for copy in copies:
-        copy.start()
+            row = h * slots + slot
+            source = table_ref.at[h, pl.ds(kinds_ref[0, slot], 1), :]
+            target = chosen_ref.at[pl.ds(row, 1), :]
+            copies.append(pltpu.make_async_copy(source, target, sems.at[row]))
+            copies[-1].start()
+    base = jnp.where(shift_ref[0] <= HALF, 0, WIN_LON - HALF)
+    raw_ref[0] = x_ref[:, pl.ds(base, HALF)]
+    raw_ref[1] = g_ref[:, pl.ds(base, HALF)]
     for c in range(4):
+        weights_ref[c * LANES : c * LANES + width, :] = rows_ref[c * width : (c + 1) * width, :]
         weights_ref[c * LANES + width : (c + 1) * LANES, :] = jnp.zeros(
             (LANES - width, depth), BF16
         )
+    flat = (lats * cols * levels, depth)
+    projected = project(x_ref[...].reshape(flat), g_ref[...].reshape(flat), weights_ref[...])
+    for lat in range(lats):
+        for col in range(cols):
+            start = (lat * cols + col) * levels
+            near_ref[col, lat * levels : (lat + 1) * levels, :] = projected[
+                start : start + levels, :
+            ].astype(BF16)
     natural_ref[...] = jnp.zeros(natural_ref.shape, F32)
     pieces_ref[...] = jnp.zeros(pieces_ref.shape, F32)
-    for copy in copies[:number]:
+    for copy in copies:
         copy.wait()
     natural_ref[:number, :count] = chosen_ref[...]
     for place, level_j, start in table_pieces():
@@ -162,16 +174,6 @@
                 moved = table if by == 0 else pltpu.roll(table, SPAN - by, 1)
                 start = h * WIDE + col * PAD
                 bias_ref[slot, start : start + PAD, :] = moved[:, :WIDE]
-    for copy in copies[number:]:
-        copy.wait()
-    flat = (lats * cols * levels, depth)
-    projected = project(own_ref[...].reshape(flat), given_ref[...].reshape(flat), weights_ref[...])
-    for lat in range(lats):
-        for col in range(cols):
-            start = (lat * cols + col) * levels
-            near_ref[col, lat * levels : (lat + 1) * levels, :] = projected[
-                start : start + levels, :
-            ].astype(BF16)
 
 
 def project(rows_x, rows_g, weights):
@@ -343,7 +345,7 @@
     row, lane = grid_of(number, LANES)
     kind = jnp.zeros((number, LANES), F32)
     for slot in range(slots):
-        kind = jnp.where(lax.rem(row, slots) == slot, kind_ref[slot, 0].astype(F32), kind)
+        kind = jnp.where(lax.rem(row, slots) == slot, kind_ref[0, slot].astype(F32), kind)
     at = (slice(0, number), slice(low, low + LANES))
     natural_ref[at] = natural_ref[at] + jnp.where(lane == count - low, kind, 0.0)
     full = low + LANES
@@ -406,7 +408,7 @@
         )
         for lat in range(lats):
             feature_ref[lat, col] = rows[lat * levels : (lat + 1) * levels, :]
-    heads, types, count = bias_ref.shape
+    _, types, count = bias_ref.shape
     devices, height, wide = gathered_ref.shape
     dense = dense_ref.shape[1] // wide
     share = height - 8 * dense
@@ -472,45 +474,49 @@
     g = grad_out.transpose(1, 2, 0, 3)
     weight = attend_weight.transpose(0, 2, 1)
     table = bias_table.transpose(1, 0, 2)
-    stored = [
-        pltpu.with_memory_space_constraint(array, pltpu.HBM)
-        for array in (x, g, weight, output_weight, table)
-    ]
-    raw, projected = pl.pallas_call(
+
+    def stored(array):
+        return pltpu.with_memory_space_constraint(array, pltpu.HBM)
+
+    grid = shape(x.shape, BF16)
+    shift, own_x, own_g, projected, rows = pl.pallas_call(
         start_kernel,
         name="start",
         out_shape=[
-            shape((2, lats, HALF, levels, depth), BF16),
+            shape((1,), jnp.int32),
+            grid,
+            grid,
             shape((HALF, tall, 4 * width), BF16),
-        ],
-        in_specs=[SMEM] + [HBM] * 4,
-        out_specs=[VMEM] * 2,
-        scratch_shapes=[pltpu.VMEM((4 * width, depth), BF16), pltpu.SemaphoreType.DMA((6,))],
+            shape((4 * width, depth), BF16),
+        ],
+        in_specs=[HBM] * 5,
+        out_specs=[SMEM] + [VMEM] * 4,
+        scratch_shapes=[pltpu.SemaphoreType.DMA((7,))],
         compiler_params=small(8),
-    )(window_shift, *stored[:4])
-    far = exchange(projected, "lon", window_shift, 1)
-    far_raw = exchange(raw, "lon", window_shift, 1)
+    )(window_shift, stored(x), stored(g), stored(weight), stored(output_weight))
+    far = exchange(projected, "lon", shift, 1)
     natural = -(-count // LANES) * LANES + LANES
-    bias, near, weights = pl.pallas_call(
+    kinds, raw, bias, near, weights = pl.pallas_call(
         prepare_kernel,
         name="prepare",
         out_shape=[
+            shape((1, slots), jnp.int32),
+            shape((2, lats, HALF, levels, depth), BF16),
             shape((slots, heads * WIDE, WIDE), F32),
             shape((cols, tall, 4 * LANES), BF16),
             shape((4 * LANES, depth), BF16),
         ],
-        in_specs=[SMEM] + [HBM] * 5,
-        out_specs=[VMEM] * 3,
+        in_specs=[SMEM] + [VMEM] * 3 + [HBM] * 2,
+        out_specs=[SMEM] + [VMEM] * 4,
         scratch_shapes=[
-            pltpu.VMEM((lats, cols, levels, depth), BF16),
-            pltpu.VMEM((lats, cols, levels, depth), BF16),
             pltpu.VMEM((number, count), F32),
             pltpu.VMEM((PAD, natural), F32),
             pltpu.VMEM((2 * WIN_LEVEL, number * PAD, LANES), F32),
-            pltpu.SemaphoreType.DMA((number + 6,)),
+            pltpu.SemaphoreType.DMA((number + 1,)),
         ],
         compiler_params=small(16),
-    )(bias_type, *stored)
+    )(shift, own_x, own_g, rows, bias_type.reshape(1, slots), stored(table))
+    far_raw = exchange(raw, "lon", shift, 1)
     packed = 3 * (cols // 4) * tall
     *pieces, own_back, folded = pl.pallas_call(
         main_kernel,
@@ -534,7 +540,11 @@
             pltpu.VMEM((n_head, packed, LANES), BF16),
         ],
         compiler_params=small(24),
-    )(window_shift, far, near, weights, bias)
+    )(shift, far, near, weights, bias)
+    parts = [pieces[0]]
+    for step in range(1, n_head):
+        ring = [(i, (i + step) % n_head) for i in range(n_head)]
+        parts.append(lax.ppermute(pieces[step], "head", ring))
     sums = pl.pallas_call(
         sums_kernel,
         name="weight_sums",
@@ -543,11 +553,7 @@
         out_specs=VMEM,
         scratch_shapes=[pltpu.VMEM((2, cols * tall, depth), BF16)],
         compiler_params=small(8),
-    )(window_shift, x, g, far_raw, own_back)
-    parts = [pieces[0]]
-    for step in range(1, n_head):
-        ring = [(i, (i + step) % n_head) for i in range(n_head)]
-        parts.append(lax.ppermute(pieces[step], "head", ring))
+    )(shift, own_x, own_g, far_raw, own_back)
     every = ("lon", "lat")
     n_every = lax.axis_size("lon") * lax.axis_size("lat")
     shares = sums.reshape(n_every, 4 * width // n_every, depth)
@@ -566,7 +572,7 @@
             pltpu.VMEM((8, dense), F32),
         ],
         compiler_params=small(8),
-    )(bias_type, folded)
+    )(kinds, folded)
     summed, back = pl.pallas_call(
         sum_kernel,
         name="sum_heads",
@@ -574,8 +580,8 @@
         in_specs=[SMEM] + [VMEM] * n_head,
         out_specs=[VMEM] * 2,
         compiler_params=small(6),
-    )(window_shift, *parts)
-    returned = exchange(back, "lon", window_shift, -1)
+    )(shift, *parts)
+    returned = exchange(back, "lon", shift, -1)
     share = pl.pallas_call(
         share_kernel,
         name="share",
@@ -598,7 +604,7 @@
         out_specs=[VMEM] * 4,
         scratch_shapes=[pltpu.VMEM((8 * n_every, dense), BF16)],
         compiler_params=small(16),
-    )(window_shift, gathered, summed, returned)
+    )(shift, gathered, summed, returned)
     return (
         feature_grad.transpose(2, 0, 1, 3),
         attend_grad.transpose(0, 2, 1),

time: 59.2 us -> 66.1 us (1.12)
  waiting for transfers between devices: 16.2 us -> 20.4 us
  Pallas kernels: 15.3 us -> 18 us
    ppermute x3, waiting for transfers between devices: 10.7 us -> 14.8 us  [exchange(): lax.ppermute(x, axis, [(i, (i - sign) % count) for i in range(count)])]
  transfers between devices with their start and end apart: 7 -> 7, of which waited for: 3 -> 3; matrix products, arithmetic and copies ran while one was open for 1% -> 0% of each run, Pallas kernels for 17% -> 12%
where the time goes in v4:
time: 66.1 us; the launch traced here: 65.4 us
  waiting for transfers between devices  20.4 us (31%)
  Pallas kernels  18 us (27%)
  starting transfers between devices  14.3 us (22%)
  blocking collectives  10.7 us (16%)
  between operations  1.34 us (2%)
    ppermute x3, waiting for transfers between devices, exchange(): lax.ppermute(x, axis, [(i, (i - sign) % count) for i in range(count)])  14.8 us
    all_gather x1, blocking collectives, per_device(): gathered = lax.all_gather(share, every, axis=0)  10.7 us
    pallas_call x1, Pallas kernels, per_device(): pl.pallas_call(main_kernel, name='main', out_shape=[shape((packed, LANES)...  5.96 us
    ppermute x3, waiting for transfers between devices, per_device(): parts.append(lax.ppermute(pieces[step], 'head', ring))  5.57 us
    ppermute x3, starting transfers between devices, per_device(): parts.append(lax.ppermute(pieces[step], 'head', ring))  5.49 us
    ppermute x3, starting transfers between devices, exchange(): lax.ppermute(x, axis, [(i, (i - sign) % count) for i in range(count)])  4.83 us
    all_to_all x1, starting transfers between devices, per_device(): shares = lax.all_to_all(shares, every, 0, 0)  3.97 us
    pallas_call x1, Pallas kernels, per_device(): pl.pallas_call(prepare_kernel, name='prepare', out_shape=[shape((1, slots...  3.73 us
  transfers between devices with their start and end apart: 7, of which 3 were waited for; matrix products, arithmetic and copies ran while one was open for 0% of the time, Pallas kernels for 12%

profile of v4, /device:TPU:0, one launch (start us, length us, event | category | flops | bytes accessed | tf_op | source)
XLA Modules:
  0.0 65.4 jit_solution(14965336439382216733)
XLA Ops:
  1.3 1.8 %start.1 = (s32[1]{0:T(128)}, bf16[6,12,8,384]{3,2,1,0:T(8,128)(2,1)S(1)}, bf16[6,12,8,384]{3,2,1,0:T(8,128)(2,1)S(1)}, bf16[6,48,384]{2,1,0:T(8,128)(2,1)S(1)}, bf16[384,384]{1,0:T(8,128)(2,1)S(1)}) custom-call(s32[1]{0:T(128)S(6)} %copy.11.shift_ref, bf16[6,12,8,384]{3,2,1,0:T(8,128)(2,1)} %bitcast.13, bf16[6,12,8,384]{3,2,1,0:T(8,128)(2,1)} %bitcast.14, ...), custom_call_target="tpu_custom_call" | custom-call | tf_op jit(solution)/shard_map/start/pallas_call | solution.py:482
  3.1 0.0 copy-start
  3.1 0.6 copy-done
  3.7 3.7 %prepare.1 = (s32[1,4]{1,0:T(1,128)S(1)}, bf16[2,6,6,8,384]{4,3,2,1,0:T(8,128)(2,1)S(1)}, f32[4,576,192]{2,1,0:T(8,128)S(1)}, bf16[12,48,512]{2,1,0:T(8,128)(2,1)S(1)}, bf16[512,384]{1,0:T(8,128)(2,1)S(1)}) custom-call(s32[1]{0:T(128)} %get-tuple-element.26.shift_ref, bf16[6,12,8,384]{3,2,1,0:T(8,128)(2,1)S(1)} %get-tuple-element.27.x_ref, ...), custom_call_target="tpu_custom_call" | custom-call | tf_op jit(solution)/shard_map/prepare/pallas_call | solution.py:499
  7.5 3.0 %collective-permute-start = (bf16[2,6,6,8,384]{4,3,2,1,0:T(8,128)(2,1)S(1)}, bf16[2,6,6,8,384]{4,3,2,1,0:T(8,128)(2,1)S(1)}, u32[]{:S(2)}, u32[]{:S(2)}) collective-permute-start(bf16[2,6,6,8,384]{4,3,2,1,0:T(8,128)(2,1)S(1)} %get-tuple-element.30), channel_id=1, source_target_pairs={{0,16},{16,0},{1,17},{17,1},{2,18},{18,2},{3,19},{19,3},{4,20},{20... | collective-permute-start | bytes 1327112 | tf_op jit(solution)/shard_map/ppermute | solution.py:453
  10.5 0.1 collective-permute-start.1
  10.6 14.8 %collective-permute-done.1.far_ref = bf16[6,48,384]{2,1,0:T(8,128)(2,1)S(1)} collective-permute-done((bf16[6,48,384]{2,1,0:T(8,128)(2,1)S(1)}, bf16[6,48,384]{2,1,0:T(8,128)(2,1)S(1)}, u32[]{:S(2)}, u32[]{:S(2)}) %collective-permute-start.1) | collective-permute-done | bytes 221216 | tf_op jit(solution)/shard_map/ppermute | solution.py:453
  25.4 6.0 %main.1 = (bf16[432,128]{1,0:T(8,128)(2,1)S(1)}, bf16[432,128]{1,0:T(8,128)(2,1)S(1)}, bf16[432,128]{1,0:T(8,128)(2,1)S(1)}, bf16[432,128]{1,0:T(8,128)(2,1)S(1)...) custom-call(s32[1]{0:T(128)} %get-tuple-element.26.shift_ref, ...), custom_call_target="tpu_custom_call" | custom-call | tf_op jit(solution)/shard_map/main/pallas_call | solution.py:521
  31.4 0.0 collective-permute-done.far_ref
  31.4 1.9 %weight_sums.1 = bf16[4,96,384]{2,1,0:T(8,128)(2,1)} custom-call(s32[1]{0:T(128)} %get-tuple-element.26.shift_ref, bf16[6,12,8,384]{3,2,1,0:T(8,128)(2,1)S(1)} %get-tuple-element.27.x_ref, bf16[6,12,8,384]{3,2,1,0:T(8,128)(2,1)S(1)} %get-tuple-element.28.g_ref, bf16[2,6,6,8,384]{4,3,2,1,0:T(8,128)(2,1)S(1)} %collective-permute-done.far_ref, ...), custom_call_target="tpu_custom_call" | custom-call | tf_op jit(solution)/shard_map/weight_sums/pallas_call | solution.py:548
  33.3 4.0 %all-to-all-start = ((bf16[8,48,384]{2,1,0:T(8,128)(2,1)}), bf16[8,48,384]{2,1,0:T(8,128)(2,1)S(1)}, u32[]{:S(2)}, u32[]{:S(2)}) async-start(bf16[8,48,384]{2,1,0:T(8,128)(2,1)} %bitcast.5), calls=%async_computation | async-start | bytes 589824 | tf_op jit(solution)/shard_map/all_to_all | solution.py:560
  37.3 1.6 %collective-permute-start.2 = (bf16[432,128]{1,0:T(8,128)(2,1)S(1)}, bf16[432,128]{1,0:T(8,128)(2,1)S(1)}, u32[]{:S(2)}, u32[]{:S(2)}) collective-permute-start(bf16[432,128]{1,0:T(8,128)(2,1)S(1)} %get-tuple-element.39), channel_id=1, source_target_pairs={{0,1},{1,2},{2,3},{3,0},{4,5},{5,6},{6,7},{7,4},{8,9},{9,10},{10,1... | collective-permute-start | bytes 331784 | tf_op jit(solution)/shard_map/ppermute | solution.py:547
  38.8 2.6 %collective-permute-start.3 = (bf16[432,128]{1,0:T(8,128)(2,1)S(1)}, bf16[432,128]{1,0:T(8,128)(2,1)S(1)}, u32[]{:S(2)}, u32[]{:S(2)}) collective-permute-start(bf16[432,128]{1,0:T(8,128)(2,1)S(1)} %get-tuple-element.40), channel_id=1, source_target_pairs={{0,2},{1,3},{2,0},{3,1},{4,6},{5,7},{6,4},{7,5},{8,10},{9,11},{10,... | collective-permute-start | bytes 331784 | tf_op jit(solution)/shard_map/ppermute | solution.py:547
  41.4 1.3 %collective-permute-start.4 = (bf16[432,128]{1,0:T(8,128)(2,1)S(1)}, bf16[432,128]{1,0:T(8,128)(2,1)S(1)}, u32[]{:S(2)}, u32[]{:S(2)}) collective-permute-start(bf16[432,128]{1,0:T(8,128)(2,1)S(1)} %get-tuple-element.41), channel_id=1, source_target_pairs={{0,3},{1,0},{2,1},{3,2},{4,7},{5,4},{6,5},{7,6},{8,11},{9,8},{10,9... | collective-permute-start | bytes 331784 | tf_op jit(solution)/shard_map/ppermute | solution.py:547
  42.8 1.1 %bias_rows.1.rows_ref = bf16[104,384]{1,0:T(8,128)(2,1)S(1)} custom-call(s32[1,4]{1,0:T(1,128)S(1)} %get-tuple-element.36.kind_ref, f32[3,64,384]{2,1,0:T(8,128)S(1)} %get-tuple-element.37.folded_ref), custom_call_target="tpu_custom_call" | custom-call | tf_op jit(solution)/shard_map/bias_rows/pallas_call | solution.py:563
  43.8 1.3 %collective-permute-done.2.refs_1_ = bf16[432,128]{1,0:T(8,128)(2,1)S(1)} collective-permute-done((bf16[432,128]{1,0:T(8,128)(2,1)S(1)}, bf16[432,128]{1,0:T(8,128)(2,1)S(1)}, u32[]{:S(2)}, u32[]{:S(2)}) %collective-permute-start.2) | collective-permute-done | bytes 110624 | tf_op jit(solution)/shard_map/ppermute | solution.py:547
  45.1 4.3 %collective-permute-done.3.refs_2_ = bf16[432,128]{1,0:T(8,128)(2,1)S(1)} collective-permute-done((bf16[432,128]{1,0:T(8,128)(2,1)S(1)}, bf16[432,128]{1,0:T(8,128)(2,1)S(1)}, u32[]{:S(2)}, u32[]{:S(2)}) %collective-permute-start.3) | collective-permute-done | bytes 110624 | tf_op jit(solution)/shard_map/ppermute | solution.py:547
  49.4 0.0 collective-permute-done.4.refs_3_
  49.4 0.7 %sum_heads.1 = (bf16[12,48,96]{2,1,0:T(8,128)(2,1)S(1)}, bf16[6,48,96]{2,1,0:T(8,128)(2,1)S(1)}) custom-call(s32[1]{0:T(128)} %get-tuple-element.26.shift_ref, bf16[432,128]{1,0:T(8,128)(2,1)S(1)} %get-tuple-element.38.refs_0_, bf16[432,128]{1,0:T(8,128)(2,1)S(1)} %collective-permute-done.2.refs_1_, bf16[432,128]{1,0:T(8,128)(2,1)S(1)} %collective-permute-done.3.refs_2_, ...), custom_call_target="tpu_custom_call" | custom-call | tf_op jit(solution)/shard_map/sum_heads/pallas_call | solution.py:576
  50.1 1.7 %collective-permute-start.5 = (bf16[6,48,96]{2,1,0:T(8,128)(2,1)S(1)}, bf16[6,48,96]{2,1,0:T(8,128)(2,1)S(1)}, u32[]{:S(2)}, u32[]{:S(2)}) collective-permute-start(bf16[6,48,96]{2,1,0:T(8,128)(2,1)S(1)} %get-tuple-element.43), channel_id=1, source_target_pairs={{0,16},{16,0},{1,17},{17,1},{2,18},{18,2},{3,19},{19,3},{4,20},{20... | collective-permute-start | bytes 165896 | tf_op jit(solution)/shard_map/ppermute | solution.py:453
  51.8 0.0 all-to-all-done.shares_ref
  51.8 0.1 share.1
  51.9 10.7 %all-gather = bf16[1216,384]{1,0:T(8,128)(2,1)S(1)} all-gather(bf16[152,384]{1,0:T(8,128)(2,1)S(1)} %share.1), channel_id=2, replica_groups=mesh['lon'=2,'lat'=4,'head'=4] {'lon','lat'}, dimensions={0}, use_global_device_ids=true | all-gather | bytes 1050624 | tf_op jit(solution)/shard_map/all_gather | solution.py:593
  62.6 0.0 collective-permute-done.5.returned_ref
  62.6 2.8 %finish.1 = (bf16[6,12,8,96]{3,2,1,0:T(8,128)(2,1)}, f32[3,96,384]{2,1,0:T(8,128)}, f32[96,384]{1,0:T(8,128)}, f32[3,64,3312]{2,1,0:T(8,128)}) custom-call(s32[1]{0:T(128)} %get-tuple-element.26.shift_ref, bf16[8,152,384]{2,1,0:T(8,128)(2,1)S(1)} %bitcast.10, bf16[12,48,96]{2,1,0:T(8,128)(2,1)S(1)} %get-tuple-element.42.summed_ref, ...), custom_call_target="tpu_custom_call" | custom-call | tf_op jit(solution)/shard_map/finish/pallas_call | solution.py:594
Async XLA Ops:
  3.1 0.7 %copy-start = (s32[4,1]{0,1:T(1,128)S(1)}, s32[4,1]{0,1:T(1,128)}, u32[]{:S(2)}) copy-start(s32[4,1]{0,1:T(1,128)} %param.11) | copy-start | bytes 52
  7.5 23.9 %collective-permute-start = (bf16[2,6,6,8,384]{4,3,2,1,0:T(8,128)(2,1)S(1)}, bf16[2,6,6,8,384]{4,3,2,1,0:T(8,128)(2,1)S(1)}, u32[]{:S(2)}, u32[]{:S(2)}) collective-permute-start(bf16[2,6,6,8,384]{4,3,2,1,0:T(8,128)(2,1)S(1)} %get-tuple-element.30), channel_id=1, source_target_pairs={{0,16},{16,0},{1,17},{17,1},{2,18},{18,2},{3,19},{19,3},{4,20},{20... | collective-permute-start | bytes 1327112 | tf_op jit(solution)/shard_map/ppermute | solution.py:453
  10.5 14.9 %collective-permute-start.1 = (bf16[6,48,384]{2,1,0:T(8,128)(2,1)S(1)}, bf16[6,48,384]{2,1,0:T(8,128)(2,1)S(1)}, u32[]{:S(2)}, u32[]{:S(2)}) collective-permute-start(bf16[6,48,384]{2,1,0:T(8,128)(2,1)S(1)} %get-tuple-element.31), channel_id=1, source_target_pairs={{0,16},{16,0},{1,17},{17,1},{2,18},{18,2},{3,19},{19,3},{4,20},{20... | collective-permute-start | bytes 663560 | tf_op jit(solution)/shard_map/ppermute | solution.py:453
  33.3 18.5 %all-to-all-start = ((bf16[8,48,384]{2,1,0:T(8,128)(2,1)}), bf16[8,48,384]{2,1,0:T(8,128)(2,1)S(1)}, u32[]{:S(2)}, u32[]{:S(2)}) async-start(bf16[8,48,384]{2,1,0:T(8,128)(2,1)} %bitcast.5), calls=%async_computation | async-start | bytes 589824 | tf_op jit(solution)/shard_map/all_to_all | solution.py:560
  37.3 7.8 %collective-permute-start.2 = (bf16[432,128]{1,0:T(8,128)(2,1)S(1)}, bf16[432,128]{1,0:T(8,128)(2,1)S(1)}, u32[]{:S(2)}, u32[]{:S(2)}) collective-permute-start(bf16[432,128]{1,0:T(8,128)(2,1)S(1)} %get-tuple-element.39), channel_id=1, source_target_pairs={{0,1},{1,2},{2,3},{3,0},{4,5},{5,6},{6,7},{7,4},{8,9},{9,10},{10,1... | collective-permute-start | bytes 331784 | tf_op jit(solution)/shard_map/ppermute | solution.py:547
  38.8 10.5 %collective-permute-start.3 = (bf16[432,128]{1,0:T(8,128)(2,1)S(1)}, bf16[432,128]{1,0:T(8,128)(2,1)S(1)}, u32[]{:S(2)}, u32[]{:S(2)}) collective-permute-start(bf16[432,128]{1,0:T(8,128)(2,1)S(1)} %get-tuple-element.40), channel_id=1, source_target_pairs={{0,2},{1,3},{2,0},{3,1},{4,6},{5,7},{6,4},{7,5},{8,10},{9,11},{10,... | collective-permute-start | bytes 331784 | tf_op jit(solution)/shard_map/ppermute | solution.py:547
  41.4 8.0 %collective-permute-start.4 = (bf16[432,128]{1,0:T(8,128)(2,1)S(1)}, bf16[432,128]{1,0:T(8,128)(2,1)S(1)}, u32[]{:S(2)}, u32[]{:S(2)}) collective-permute-start(bf16[432,128]{1,0:T(8,128)(2,1)S(1)} %get-tuple-element.41), channel_id=1, source_target_pairs={{0,3},{1,0},{2,1},{3,2},{4,7},{5,4},{6,5},{7,6},{8,11},{9,8},{10,9... | collective-permute-start | bytes 331784 | tf_op jit(solution)/shard_map/ppermute | solution.py:547
  50.1 12.5 %collective-permute-start.5 = (bf16[6,48,96]{2,1,0:T(8,128)(2,1)S(1)}, bf16[6,48,96]{2,1,0:T(8,128)(2,1)S(1)}, u32[]{:S(2)}, u32[]{:S(2)}) collective-permute-start(bf16[6,48,96]{2,1,0:T(8,128)(2,1)S(1)} %get-tuple-element.43), channel_id=1, source_target_pairs={{0,16},{16,0},{1,17},{17,1},{2,18},{18,2},{3,19},{19,3},{4,20},{20... | collective-permute-start | bytes 165896 | tf_op jit(solution)/shard_map/ppermute | solution.py:453

commit v5 on v4

--- a/solution.py
+++ b/solution.py
@@ -496,7 +496,7 @@
     )(window_shift, stored(x), stored(g), stored(weight), stored(output_weight))
     far = exchange(projected, "lon", shift, 1)
     natural = -(-count // LANES) * LANES + LANES
-    kinds, raw, bias, near, weights = pl.pallas_call(
+    prepare = pl.pallas_call(
         prepare_kernel,
         name="prepare",
         out_shape=[
@@ -515,7 +515,10 @@
             pltpu.SemaphoreType.DMA((number + 1,)),
         ],
         compiler_params=small(16),
-    )(shift, own_x, own_g, rows, bias_type.reshape(1, slots), stored(table))
+    )
+    kinds, raw, bias, near, weights = prepare(
+        shift, own_x, own_g, rows, bias_type.reshape(1, slots), stored(table)
+    )
     far_raw = exchange(raw, "lon", shift, 1)
     packed = 3 * (cols // 4) * tall
     *pieces, own_back, folded = pl.pallas_call(

time: 66.1 us -> 66.1 us (level)
  no operation moved by 1% of the time
where the time goes in v5:
time: 66.1 us; the launch traced here: 65.4 us
  waiting for transfers between devices  20.4 us (31%)
  Pallas kernels  18 us (27%)
  starting transfers between devices  14.3 us (22%)
  blocking collectives  10.7 us (16%)
  between operations  1.34 us (2%)
    ppermute x3, waiting for transfers between devices, exchange(): lax.ppermute(x, axis, [(i, (i - sign) % count) for i in range(count)])  14.8 us
    all_gather x1, blocking collectives, per_device(): gathered = lax.all_gather(share, every, axis=0)  10.7 us
    pallas_call x1, Pallas kernels, per_device(): pl.pallas_call(main_kernel, name='main', out_shape=[shape((packed, LANES)...  5.96 us
    ppermute x3, waiting for transfers between devices, per_device(): parts.append(lax.ppermute(pieces[step], 'head', ring))  5.57 us
    ppermute x3, starting transfers between devices, per_device(): parts.append(lax.ppermute(pieces[step], 'head', ring))  5.49 us
    ppermute x3, starting transfers between devices, exchange(): lax.ppermute(x, axis, [(i, (i - sign) % count) for i in range(count)])  4.83 us
    all_to_all x1, starting transfers between devices, per_device(): shares = lax.all_to_all(shares, every, 0, 0)  3.97 us
    pallas_call x1, Pallas kernels, per_device(): prepare(shift, own_x, own_g, rows, bias_type.reshape(1, slots), stored(ta...  3.73 us
  transfers between devices with their start and end apart: 7, of which 3 were waited for; matrix products, arithmetic and copies ran while one was open for 0% of the time, Pallas kernels for 12%

profile of v5, /device:TPU:0, one launch (start us, length us, event | category | flops | bytes accessed | tf_op | source)
XLA Modules:
  0.0 65.4 jit_solution(14965336439382216733)
XLA Ops:
  1.3 1.8 %start.1 = (s32[1]{0:T(128)}, bf16[6,12,8,384]{3,2,1,0:T(8,128)(2,1)S(1)}, bf16[6,12,8,384]{3,2,1,0:T(8,128)(2,1)S(1)}, bf16[6,48,384]{2,1,0:T(8,128)(2,1)S(1)}, bf16[384,384]{1,0:T(8,128)(2,1)S(1)}) custom-call(s32[1]{0:T(128)S(6)} %copy.11.shift_ref, bf16[6,12,8,384]{3,2,1,0:T(8,128)(2,1)} %bitcast.13, bf16[6,12,8,384]{3,2,1,0:T(8,128)(2,1)} %bitcast.14, ...), custom_call_target="tpu_custom_call" | custom-call | tf_op jit(solution)/shard_map/start/pallas_call | solution.py:482
  3.1 0.0 copy-start
  3.1 0.6 copy-done
  3.7 3.7 %prepare.1 = (s32[1,4]{1,0:T(1,128)S(1)}, bf16[2,6,6,8,384]{4,3,2,1,0:T(8,128)(2,1)S(1)}, f32[4,576,192]{2,1,0:T(8,128)S(1)}, bf16[12,48,512]{2,1,0:T(8,128)(2,1)S(1)}, bf16[512,384]{1,0:T(8,128)(2,1)S(1)}) custom-call(s32[1]{0:T(128)} %get-tuple-element.26.shift_ref, bf16[6,12,8,384]{3,2,1,0:T(8,128)(2,1)S(1)} %get-tuple-element.27.x_ref, ...), custom_call_target="tpu_custom_call" | custom-call | tf_op jit(solution)/shard_map/prepare/pallas_call | solution.py:519
  7.5 3.0 %collective-permute-start = (bf16[2,6,6,8,384]{4,3,2,1,0:T(8,128)(2,1)S(1)}, bf16[2,6,6,8,384]{4,3,2,1,0:T(8,128)(2,1)S(1)}, u32[]{:S(2)}, u32[]{:S(2)}) collective-permute-start(bf16[2,6,6,8,384]{4,3,2,1,0:T(8,128)(2,1)S(1)} %get-tuple-element.30), channel_id=1, source_target_pairs={{0,16},{16,0},{1,17},{17,1},{2,18},{18,2},{3,19},{19,3},{4,20},{20... | collective-permute-start | bytes 1327112 | tf_op jit(solution)/shard_map/ppermute | solution.py:453
  10.5 0.1 collective-permute-start.1
  10.6 14.8 %collective-permute-done.1.far_ref = bf16[6,48,384]{2,1,0:T(8,128)(2,1)S(1)} collective-permute-done((bf16[6,48,384]{2,1,0:T(8,128)(2,1)S(1)}, bf16[6,48,384]{2,1,0:T(8,128)(2,1)S(1)}, u32[]{:S(2)}, u32[]{:S(2)}) %collective-permute-start.1) | collective-permute-done | bytes 221216 | tf_op jit(solution)/shard_map/ppermute | solution.py:453
  25.4 6.0 %main.1 = (bf16[432,128]{1,0:T(8,128)(2,1)S(1)}, bf16[432,128]{1,0:T(8,128)(2,1)S(1)}, bf16[432,128]{1,0:T(8,128)(2,1)S(1)}, bf16[432,128]{1,0:T(8,128)(2,1)S(1)...) custom-call(s32[1]{0:T(128)} %get-tuple-element.26.shift_ref, ...), custom_call_target="tpu_custom_call" | custom-call | tf_op jit(solution)/shard_map/main/pallas_call | solution.py:524
  31.4 0.0 collective-permute-done.far_ref
  31.4 1.9 %weight_sums.1 = bf16[4,96,384]{2,1,0:T(8,128)(2,1)} custom-call(s32[1]{0:T(128)} %get-tuple-element.26.shift_ref, bf16[6,12,8,384]{3,2,1,0:T(8,128)(2,1)S(1)} %get-tuple-element.27.x_ref, bf16[6,12,8,384]{3,2,1,0:T(8,128)(2,1)S(1)} %get-tuple-element.28.g_ref, bf16[2,6,6,8,384]{4,3,2,1,0:T(8,128)(2,1)S(1)} %collective-permute-done.far_ref, ...), custom_call_target="tpu_custom_call" | custom-call | tf_op jit(solution)/shard_map/weight_sums/pallas_call | solution.py:551
  33.3 4.0 %all-to-all-start = ((bf16[8,48,384]{2,1,0:T(8,128)(2,1)}), bf16[8,48,384]{2,1,0:T(8,128)(2,1)S(1)}, u32[]{:S(2)}, u32[]{:S(2)}) async-start(bf16[8,48,384]{2,1,0:T(8,128)(2,1)} %bitcast.5), calls=%async_computation | async-start | bytes 589824 | tf_op jit(solution)/shard_map/all_to_all | solution.py:563
  37.3 1.6 %collective-permute-start.2 = (bf16[432,128]{1,0:T(8,128)(2,1)S(1)}, bf16[432,128]{1,0:T(8,128)(2,1)S(1)}, u32[]{:S(2)}, u32[]{:S(2)}) collective-permute-start(bf16[432,128]{1,0:T(8,128)(2,1)S(1)} %get-tuple-element.39), channel_id=1, source_target_pairs={{0,1},{1,2},{2,3},{3,0},{4,5},{5,6},{6,7},{7,4},{8,9},{9,10},{10,1... | collective-permute-start | bytes 331784 | tf_op jit(solution)/shard_map/ppermute | solution.py:550
  38.8 2.6 %collective-permute-start.3 = (bf16[432,128]{1,0:T(8,128)(2,1)S(1)}, bf16[432,128]{1,0:T(8,128)(2,1)S(1)}, u32[]{:S(2)}, u32[]{:S(2)}) collective-permute-start(bf16[432,128]{1,0:T(8,128)(2,1)S(1)} %get-tuple-element.40), channel_id=1, source_target_pairs={{0,2},{1,3},{2,0},{3,1},{4,6},{5,7},{6,4},{7,5},{8,10},{9,11},{10,... | collective-permute-start | bytes 331784 | tf_op jit(solution)/shard_map/ppermute | solution.py:550
  41.4 1.3 %collective-permute-start.4 = (bf16[432,128]{1,0:T(8,128)(2,1)S(1)}, bf16[432,128]{1,0:T(8,128)(2,1)S(1)}, u32[]{:S(2)}, u32[]{:S(2)}) collective-permute-start(bf16[432,128]{1,0:T(8,128)(2,1)S(1)} %get-tuple-element.41), channel_id=1, source_target_pairs={{0,3},{1,0},{2,1},{3,2},{4,7},{5,4},{6,5},{7,6},{8,11},{9,8},{10,9... | collective-permute-start | bytes 331784 | tf_op jit(solution)/shard_map/ppermute | solution.py:550
  42.8 1.1 %bias_rows.1.rows_ref = bf16[104,384]{1,0:T(8,128)(2,1)S(1)} custom-call(s32[1,4]{1,0:T(1,128)S(1)} %get-tuple-element.36.kind_ref, f32[3,64,384]{2,1,0:T(8,128)S(1)} %get-tuple-element.37.folded_ref), custom_call_target="tpu_custom_call" | custom-call | tf_op jit(solution)/shard_map/bias_rows/pallas_call | solution.py:566
  43.8 1.3 %collective-permute-done.2.refs_1_ = bf16[432,128]{1,0:T(8,128)(2,1)S(1)} collective-permute-done((bf16[432,128]{1,0:T(8,128)(2,1)S(1)}, bf16[432,128]{1,0:T(8,128)(2,1)S(1)}, u32[]{:S(2)}, u32[]{:S(2)}) %collective-permute-start.2) | collective-permute-done | bytes 110624 | tf_op jit(solution)/shard_map/ppermute | solution.py:550
  45.1 4.3 %collective-permute-done.3.refs_2_ = bf16[432,128]{1,0:T(8,128)(2,1)S(1)} collective-permute-done((bf16[432,128]{1,0:T(8,128)(2,1)S(1)}, bf16[432,128]{1,0:T(8,128)(2,1)S(1)}, u32[]{:S(2)}, u32[]{:S(2)}) %collective-permute-start.3) | collective-permute-done | bytes 110624 | tf_op jit(solution)/shard_map/ppermute | solution.py:550
  49.4 0.0 collective-permute-done.4.refs_3_
  49.4 0.7 %sum_heads.1 = (bf16[12,48,96]{2,1,0:T(8,128)(2,1)S(1)}, bf16[6,48,96]{2,1,0:T(8,128)(2,1)S(1)}) custom-call(s32[1]{0:T(128)} %get-tuple-element.26.shift_ref, bf16[432,128]{1,0:T(8,128)(2,1)S(1)} %get-tuple-element.38.refs_0_, bf16[432,128]{1,0:T(8,128)(2,1)S(1)} %collective-permute-done.2.refs_1_, bf16[432,128]{1,0:T(8,128)(2,1)S(1)} %collective-permute-done.3.refs_2_, ...), custom_call_target="tpu_custom_call" | custom-call | tf_op jit(solution)/shard_map/sum_heads/pallas_call | solution.py:579
  50.1 1.7 %collective-permute-start.5 = (bf16[6,48,96]{2,1,0:T(8,128)(2,1)S(1)}, bf16[6,48,96]{2,1,0:T(8,128)(2,1)S(1)}, u32[]{:S(2)}, u32[]{:S(2)}) collective-permute-start(bf16[6,48,96]{2,1,0:T(8,128)(2,1)S(1)} %get-tuple-element.43), channel_id=1, source_target_pairs={{0,16},{16,0},{1,17},{17,1},{2,18},{18,2},{3,19},{19,3},{4,20},{20... | collective-permute-start | bytes 165896 | tf_op jit(solution)/shard_map/ppermute | solution.py:453
  51.8 0.0 all-to-all-done.shares_ref
  51.8 0.1 share.1
  51.9 10.7 %all-gather = bf16[1216,384]{1,0:T(8,128)(2,1)S(1)} all-gather(bf16[152,384]{1,0:T(8,128)(2,1)S(1)} %share.1), channel_id=2, replica_groups=mesh['lon'=2,'lat'=4,'head'=4] {'lon','lat'}, dimensions={0}, use_global_device_ids=true | all-gather | bytes 1050624 | tf_op jit(solution)/shard_map/all_gather | solution.py:596
  62.6 0.0 collective-permute-done.5.returned_ref
  62.6 2.8 %finish.1 = (bf16[6,12,8,96]{3,2,1,0:T(8,128)(2,1)}, f32[3,96,384]{2,1,0:T(8,128)}, f32[96,384]{1,0:T(8,128)}, f32[3,64,3312]{2,1,0:T(8,128)}) custom-call(s32[1]{0:T(128)} %get-tuple-element.26.shift_ref, bf16[8,152,384]{2,1,0:T(8,128)(2,1)S(1)} %bitcast.10, bf16[12,48,96]{2,1,0:T(8,128)(2,1)S(1)} %get-tuple-element.42.summed_ref, ...), custom_call_target="tpu_custom_call" | custom-call | tf_op jit(solution)/shard_map/finish/pallas_call | solution.py:597
Async XLA Ops:
  3.1 0.7 %copy-start = (s32[4,1]{0,1:T(1,128)S(1)}, s32[4,1]{0,1:T(1,128)}, u32[]{:S(2)}) copy-start(s32[4,1]{0,1:T(1,128)} %param.11) | copy-start | bytes 52
  7.5 23.9 %collective-permute-start = (bf16[2,6,6,8,384]{4,3,2,1,0:T(8,128)(2,1)S(1)}, bf16[2,6,6,8,384]{4,3,2,1,0:T(8,128)(2,1)S(1)}, u32[]{:S(2)}, u32[]{:S(2)}) collective-permute-start(bf16[2,6,6,8,384]{4,3,2,1,0:T(8,128)(2,1)S(1)} %get-tuple-element.30), channel_id=1, source_target_pairs={{0,16},{16,0},{1,17},{17,1},{2,18},{18,2},{3,19},{19,3},{4,20},{20... | collective-permute-start | bytes 1327112 | tf_op jit(solution)/shard_map/ppermute | solution.py:453
  10.5 14.9 %collective-permute-start.1 = (bf16[6,48,384]{2,1,0:T(8,128)(2,1)S(1)}, bf16[6,48,384]{2,1,0:T(8,128)(2,1)S(1)}, u32[]{:S(2)}, u32[]{:S(2)}) collective-permute-start(bf16[6,48,384]{2,1,0:T(8,128)(2,1)S(1)} %get-tuple-element.31), channel_id=1, source_target_pairs={{0,16},{16,0},{1,17},{17,1},{2,18},{18,2},{3,19},{19,3},{4,20},{20... | collective-permute-start | bytes 663560 | tf_op jit(solution)/shard_map/ppermute | solution.py:453
  33.3 18.5 %all-to-all-start = ((bf16[8,48,384]{2,1,0:T(8,128)(2,1)}), bf16[8,48,384]{2,1,0:T(8,128)(2,1)S(1)}, u32[]{:S(2)}, u32[]{:S(2)}) async-start(bf16[8,48,384]{2,1,0:T(8,128)(2,1)} %bitcast.5), calls=%async_computation | async-start | bytes 589824 | tf_op jit(solution)/shard_map/all_to_all | solution.py:563
  37.3 7.8 %collective-permute-start.2 = (bf16[432,128]{1,0:T(8,128)(2,1)S(1)}, bf16[432,128]{1,0:T(8,128)(2,1)S(1)}, u32[]{:S(2)}, u32[]{:S(2)}) collective-permute-start(bf16[432,128]{1,0:T(8,128)(2,1)S(1)} %get-tuple-element.39), channel_id=1, source_target_pairs={{0,1},{1,2},{2,3},{3,0},{4,5},{5,6},{6,7},{7,4},{8,9},{9,10},{10,1... | collective-permute-start | bytes 331784 | tf_op jit(solution)/shard_map/ppermute | solution.py:550
  38.8 10.5 %collective-permute-start.3 = (bf16[432,128]{1,0:T(8,128)(2,1)S(1)}, bf16[432,128]{1,0:T(8,128)(2,1)S(1)}, u32[]{:S(2)}, u32[]{:S(2)}) collective-permute-start(bf16[432,128]{1,0:T(8,128)(2,1)S(1)} %get-tuple-element.40), channel_id=1, source_target_pairs={{0,2},{1,3},{2,0},{3,1},{4,6},{5,7},{6,4},{7,5},{8,10},{9,11},{10,... | collective-permute-start | bytes 331784 | tf_op jit(solution)/shard_map/ppermute | solution.py:550
  41.4 8.0 %collective-permute-start.4 = (bf16[432,128]{1,0:T(8,128)(2,1)S(1)}, bf16[432,128]{1,0:T(8,128)(2,1)S(1)}, u32[]{:S(2)}, u32[]{:S(2)}) collective-permute-start(bf16[432,128]{1,0:T(8,128)(2,1)S(1)} %get-tuple-element.41), channel_id=1, source_target_pairs={{0,3},{1,0},{2,1},{3,2},{4,7},{5,4},{6,5},{7,6},{8,11},{9,8},{10,9... | collective-permute-start | bytes 331784 | tf_op jit(solution)/shard_map/ppermute | solution.py:550
  50.1 12.5 %collective-permute-start.5 = (bf16[6,48,96]{2,1,0:T(8,128)(2,1)S(1)}, bf16[6,48,96]{2,1,0:T(8,128)(2,1)S(1)}, u32[]{:S(2)}, u32[]{:S(2)}) collective-permute-start(bf16[6,48,96]{2,1,0:T(8,128)(2,1)S(1)} %get-tuple-element.43), channel_id=1, source_target_pairs={{0,16},{16,0},{1,17},{17,1},{2,18},{18,2},{3,19},{19,3},{4,20},{20... | collective-permute-start | bytes 165896 | tf_op jit(solution)/shard_map/ppermute | solution.py:453

commit v6 on v5

--- a/solution.py
+++ b/solution.py
@@ -17,6 +17,7 @@
 PIECE = WIN_LAT * OFFSETS
 LANES = 128
 SPAN = -(-OFFSETS * PAD // LANES) * LANES
+BIAS_ROWS = 104
 MASKED = -1e30
 F32 = jnp.float32
 BF16 = jnp.bfloat16
@@ -302,7 +303,8 @@
         pieces[step][...] = chunk_ref[lax.rem(mine + step, n_head)]
 
 
-def sums_kernel(shift_ref, x_ref, g_ref, far_ref, back_ref, sums_ref, own_ref):
+def sums_kernel(shift_ref, x_ref, g_ref, far_ref, back_ref, *refs):
+    *halves, sums_ref, own_ref = refs
     lats, cols, levels, _ = x_ref.shape
     width = sums_ref.shape[1]
     for col in range(cols):
@@ -318,6 +320,34 @@
     for c in range(3):
         sums_ref[c] = summed[c * LANES : c * LANES + width, :].astype(BF16)
     sums_ref[3] = dot_tn(back_ref[:, grads:], own_ref[1])[:width, :].astype(BF16)
+    if halves:
+        core = lax.rem(lax.axis_index("lat"), 2)
+        for ref, side in zip(halves, (core, 1 - core)):
+            for i in range(2):
+                ref[i * width : (i + 1) * width, :] = sums_ref[2 * side + i]
+
+
+def pair_kernel(kept_ref, got_ref, rows_ref, out_ref):
+    count = rows_ref.shape[0]
+    out_ref[:count, :] = rows_ref[...]
+    out_ref[count:, :] = (kept_ref[...].astype(F32) + got_ref[...].astype(F32)).astype(BF16)
+
+
+def merge_kernel(*refs):
+    *parts, out_ref, all_ref = refs
+    chip = lax.axis_index("lon") * 2 + lax.div(lax.axis_index("lat"), 2)
+    for i, part in enumerate(parts):
+        all_ref[lax.bitwise_xor(chip, i)] = part[...]
+    share = (parts[0].shape[0] - BIAS_ROWS) // 2
+    for j in range(2):
+        low = all_ref[j, :BIAS_ROWS, :].astype(F32)
+        high = all_ref[2 + j, :BIAS_ROWS, :].astype(F32)
+        out_ref[j, :BIAS_ROWS, :] = (low + high).astype(BF16)
+        start = BIAS_ROWS + j * share
+        total = all_ref[0, start : start + share, :].astype(F32)
+        for i in range(1, 4):
+            total = total + all_ref[i, start : start + share, :].astype(F32)
+        out_ref[j, BIAS_ROWS:, :] = total.astype(BF16)
 
 
 def bias_kernel(kind_ref, folded_ref, out_ref, pieces_ref, natural_ref, dense_ref):
@@ -390,10 +420,23 @@
     out_ref[count:, :] = total.astype(BF16)
 
 
-def finish_kernel(
-    shift_ref, gathered_ref, summed_ref, returned_ref,
-    feature_ref, attend_ref, output_ref, bias_ref, dense_ref,
-):
+def finish_kernel(shift_ref, *refs):
+    *gathered, summed_ref, returned_ref, feature_ref, attend_ref, output_ref, bias_ref, dense_ref = refs
+    if len(gathered) == 1:
+        devices, height, wide = gathered[0].shape
+        copies = 1
+
+        def entry(i, rows):
+            return gathered[0][i, rows, :]
+    else:
+        devices, height, wide = 4, *gathered[0].shape[1:]
+        copies = 2
+        core = lax.rem(lax.axis_index("lat"), 2)
+
+        def entry(i, rows):
+            mine, other = (ref[i % 2, rows, :] for ref in gathered)
+            return jnp.where(core == i // 2, mine, other)
+
     shift = shift_ref[0]
     low = shift <= HALF
     lats, cols, levels, width = feature_ref.shape
@@ -409,26 +452,25 @@
         for lat in range(lats):
             feature_ref[lat, col] = rows[lat * levels : (lat + 1) * levels, :]
     _, types, count = bias_ref.shape
-    devices, height, wide = gathered_ref.shape
     dense = dense_ref.shape[1] // wide
     share = height - 8 * dense
     for i in range(devices):
         start = i * share
-        block = gathered_ref[i, 8 * dense :, :].astype(F32)
+        block = entry(i, slice(8 * dense, height)).astype(F32)
         if start < 3 * width:
             attend_ref[start // width, start % width : start % width + share, :] = block
         else:
             output_ref[start - 3 * width : start - 3 * width + share, :] = block
         for j in range(dense):
-            dense_ref[i * 8 : (i + 1) * 8, j * wide : (j + 1) * wide] = gathered_ref[
-                i, j * 8 : (j + 1) * 8, :
-            ]
+            dense_ref[i * 8 : (i + 1) * 8, j * wide : (j + 1) * wide] = entry(
+                i, slice(j * 8, (j + 1) * 8)
+            )
     full = -(-count // LANES) * LANES
     middle = full // 2
     row, lane = grid_of(devices * 8, types)
     row = lax.bitwise_and(row, 7)
     tag = count - (full - LANES)
-    lane = lane.astype(F32)
+    lane = lane.astype(F32) * copies
     kind = dense_ref[:, full - LANES : full].astype(F32)[:, tag : tag + 1]
     for h in range(2):
         mine = (row >= 4 * h) & (row < 4 * h + 4)
@@ -548,21 +590,28 @@
     for step in range(1, n_head):
         ring = [(i, (i + step) % n_head) for i in range(n_head)]
         parts.append(lax.ppermute(pieces[step], "head", ring))
-    sums = pl.pallas_call(
+    every = ("lon", "lat")
+    n_lon, n_lat = lax.axis_size("lon"), lax.axis_size("lat")
+    n_every = n_lon * n_lat
+    paired = n_lon == 2 and n_lat == 4
+    halves = [shape((2 * width, depth), BF16)] * 2 if paired else []
+    *halves, sums = pl.pallas_call(
         sums_kernel,
         name="weight_sums",
-        out_shape=shape((4, width, depth), BF16),
+        out_shape=halves + [shape((4, width, depth), BF16)],
         in_specs=[SMEM] + [VMEM] * 4,
-        out_specs=VMEM,
+        out_specs=[VMEM] * (len(halves) + 1),
         scratch_shapes=[pltpu.VMEM((2, cols * tall, depth), BF16)],
         compiler_params=small(8),
     )(shift, own_x, own_g, far_raw, own_back)
-    every = ("lon", "lat")
-    n_every = lax.axis_size("lon") * lax.axis_size("lat")
-    shares = sums.reshape(n_every, 4 * width // n_every, depth)
-    shares = lax.all_to_all(shares, every, 0, 0)
+    if paired:
+        got = lax.ppermute(halves[1], "lat", [(i, i ^ 1) for i in range(n_lat)])
+    else:
+        shares = sums.reshape(n_every, 4 * width // n_every, depth)
+        shares = lax.all_to_all(shares, every, 0, 0)
     full = natural - LANES
     dense = full + full // 2
+    assert 8 * dense == BIAS_ROWS * depth
     rows = pl.pallas_call(
         bias_kernel,
         name="bias_rows",
@@ -585,15 +634,40 @@
         compiler_params=small(6),
     )(shift, *parts)
     returned = exchange(back, "lon", shift, -1)
-    share = pl.pallas_call(
-        share_kernel,
-        name="share",
-        out_shape=shape((rows.shape[0] + shares.shape[1], depth), BF16),
-        in_specs=[VMEM] * 2,
-        out_specs=VMEM,
-        compiler_params=small(4),
-    )(shares, rows)
-    gathered = lax.all_gather(share, every, axis=0)
+    if paired:
+        part = pl.pallas_call(
+            pair_kernel,
+            name="pair",
+            out_shape=shape((rows.shape[0] + 2 * width, depth), BF16),
+            in_specs=[VMEM] * 3,
+            out_specs=VMEM,
+            compiler_params=small(4),
+        )(halves[0], got, rows)
+        chips = [part]
+        for step in range(1, 4):
+            ring = [(i, i ^ (2 * step)) for i in range(n_every)]
+            chips.append(lax.ppermute(part, every, ring))
+        merged = pl.pallas_call(
+            merge_kernel,
+            name="merge",
+            out_shape=shape((2, rows.shape[0] + width, depth), BF16),
+            in_specs=[VMEM] * 4,
+            out_specs=VMEM,
+            scratch_shapes=[pltpu.VMEM((4, *part.shape), BF16)],
+            compiler_params=small(6),
+        )(*chips)
+        other = lax.ppermute(merged, "lat", [(i, i ^ 1) for i in range(n_lat)])
+        gathered = [merged, other]
+    else:
+        share = pl.pallas_call(
+            share_kernel,
+            name="share",
+            out_shape=shape((rows.shape[0] + shares.shape[1], depth), BF16),
+            in_specs=[VMEM] * 2,
+            out_specs=VMEM,
+            compiler_params=small(4),
+        )(shares, rows)
+        gathered = [lax.all_gather(share, every, axis=0)]
     feature_grad, attend_grad, output_grad, bias_grad = pl.pallas_call(
         finish_kernel,
         name="finish",
@@ -603,11 +677,11 @@
             shape((width, depth), F32),
             shape((heads, types, count), F32),
         ],
-        in_specs=[SMEM] + [VMEM] * 3,
+        in_specs=[SMEM] + [VMEM] * (len(gathered) + 2),
         out_specs=[VMEM] * 4,
-        scratch_shapes=[pltpu.VMEM((8 * n_every, dense), BF16)],
+        scratch_shapes=[pltpu.VMEM((8 * (4 if paired else n_every), dense), BF16)],
         compiler_params=small(16),
-    )(shift, gathered, summed, returned)
+    )(shift, *gathered, summed, returned)
     return (
         feature_grad.transpose(2, 0, 1, 3),
         attend_grad.transpose(0, 2, 1),

time: 66.1 us -> 69.2 us (1.047)
  waiting for transfers between devices: 20.4 us -> 34.9 us
  blocking collectives: 10.7 us -> 0 us
    all_gather x1 -> x0, blocking collectives: 10.7 us -> none  [per_device(): gathered = lax.all_gather(share, every, axis=0)]
    ppermute x0 -> x5, waiting for transfers between devices: none -> 10.6 us  [the longest x3 10.3 us: per_device(): chips.append(lax.ppermute(part, every, ring))]
    all_to_all x1 -> x0, starting transfers between devices: 3.97 us -> none  [per_device(): shares = lax.all_to_all(shares, every, 0, 0)]
    ppermute x0 -> x5, starting transfers between devices: none -> 3.63 us  [the longest x3 3.55 us: per_device(): chips.append(lax.ppermute(part, every, ring))]
    ppermute x3, waiting for transfers between devices: 14.8 us -> 17.7 us  [exchange(): lax.ppermute(x, axis, [(i, (i - sign) % count) for i in range(count)])]
    ppermute x3, waiting for transfers between devices: 5.57 us -> 6.58 us  [per_device(): parts.append(lax.ppermute(pieces[step], 'head', ring))]
    pallas_call x2 -> x3, Pallas kernels: 1.94 us -> 2.16 us  [the longest x1 1.89 us: per_device(): pl.pallas_call(sums_kernel, name='weight_sums', out_shape=halves + [shape...]
  transfers between devices with their start and end apart: 7 -> 11, of which waited for: 3 -> 7; matrix products, arithmetic and copies ran while one was open for 0% -> 0% of each run, Pallas kernels for 12% -> 11%
where the time goes in v6:
time: 69.2 us; the launch traced here: 68.9 us
  waiting for transfers between devices  34.9 us (50%)
  Pallas kernels  18.2 us (26%)
  starting transfers between devices  13.8 us (20%)
  between operations  1.35 us (2%)
    ppermute x3, waiting for transfers between devices, exchange(): lax.ppermute(x, axis, [(i, (i - sign) % count) for i in range(count)])  17.7 us
    ppermute x3, waiting for transfers between devices, per_device(): chips.append(lax.ppermute(part, every, ring))  10.3 us
    ppermute x3, waiting for transfers between devices, per_device(): parts.append(lax.ppermute(pieces[step], 'head', ring))  6.58 us
    pallas_call x1, Pallas kernels, per_device(): pl.pallas_call(main_kernel, name='main', out_shape=[shape((packed, LANES)...  5.96 us
    ppermute x3, starting transfers between devices, per_device(): parts.append(lax.ppermute(pieces[step], 'head', ring))  5.55 us
    ppermute x3, starting transfers between devices, exchange(): lax.ppermute(x, axis, [(i, (i - sign) % count) for i in range(count)])  4.65 us
    pallas_call x1, Pallas kernels, per_device(): prepare(shift, own_x, own_g, rows, bias_type.reshape(1, slots), stored(ta...  3.72 us
    ppermute x3, starting transfers between devices, per_device(): chips.append(lax.ppermute(part, every, ring))  3.55 us
  transfers between devices with their start and end apart: 11, of which 7 were waited for; matrix products, arithmetic and copies ran while one was open for 0% of the time, Pallas kernels for 11%

profile of v6, /device:TPU:0, one launch (start us, length us, event | category | flops | bytes accessed | tf_op | source)
XLA Modules:
  0.0 68.9 jit_solution(1314946520476135911)
XLA Ops:
  1.3 1.8 %start.1 = (s32[1]{0:T(128)}, bf16[6,12,8,384]{3,2,1,0:T(8,128)(2,1)S(1)}, bf16[6,12,8,384]{3,2,1,0:T(8,128)(2,1)S(1)}, bf16[6,48,384]{2,1,0:T(8,128)(2,1)S(1)}, bf16[384,384]{1,0:T(8,128)(2,1)S(1)}) custom-call(s32[1]{0:T(128)S(6)} %copy.11.shift_ref, bf16[6,12,8,384]{3,2,1,0:T(8,128)(2,1)} %bitcast.10, bf16[6,12,8,384]{3,2,1,0:T(8,128)(2,1)} %bitcast.11, ...), custom_call_target="tpu_custom_call" | custom-call | tf_op jit(solution)/shard_map/start/pallas_call | solution.py:524
  3.1 0.0 copy-start
  3.1 0.6 copy-done
  3.7 3.7 %prepare.1 = (s32[1,4]{1,0:T(1,128)S(1)}, bf16[2,6,6,8,384]{4,3,2,1,0:T(8,128)(2,1)S(1)}, f32[4,576,192]{2,1,0:T(8,128)S(1)}, bf16[12,48,512]{2,1,0:T(8,128)(2,1)S(1)}, bf16[512,384]{1,0:T(8,128)(2,1)S(1)}) custom-call(s32[1]{0:T(128)} %get-tuple-element.28.shift_ref, bf16[6,12,8,384]{3,2,1,0:T(8,128)(2,1)S(1)} %get-tuple-element.29.x_ref, ...), custom_call_target="tpu_custom_call" | custom-call | tf_op jit(solution)/shard_map/prepare/pallas_call | solution.py:561
  7.5 3.0 %collective-permute-start = (bf16[2,6,6,8,384]{4,3,2,1,0:T(8,128)(2,1)S(1)}, bf16[2,6,6,8,384]{4,3,2,1,0:T(8,128)(2,1)S(1)}, u32[]{:S(2)}, u32[]{:S(2)}) collective-permute-start(bf16[2,6,6,8,384]{4,3,2,1,0:T(8,128)(2,1)S(1)} %get-tuple-element.32), channel_id=1, source_target_pairs={{0,16},{16,0},{1,17},{17,1},{2,18},{18,2},{3,19},{19,3},{4,20},{20... | collective-permute-start | bytes 1327112 | tf_op jit(solution)/shard_map/ppermute | solution.py:495
  10.5 0.1 collective-permute-start.1
  10.6 14.8 %collective-permute-done.1.far_ref = bf16[6,48,384]{2,1,0:T(8,128)(2,1)S(1)} collective-permute-done((bf16[6,48,384]{2,1,0:T(8,128)(2,1)S(1)}, bf16[6,48,384]{2,1,0:T(8,128)(2,1)S(1)}, u32[]{:S(2)}, u32[]{:S(2)}) %collective-permute-start.1) | collective-permute-done | bytes 221216 | tf_op jit(solution)/shard_map/ppermute | solution.py:495
  25.4 6.0 %main.1 = (bf16[432,128]{1,0:T(8,128)(2,1)S(1)}, bf16[432,128]{1,0:T(8,128)(2,1)S(1)}, bf16[432,128]{1,0:T(8,128)(2,1)S(1)}, bf16[432,128]{1,0:T(8,128)(2,1)S(1)...) custom-call(s32[1]{0:T(128)} %get-tuple-element.28.shift_ref, ...), custom_call_target="tpu_custom_call" | custom-call | tf_op jit(solution)/shard_map/main/pallas_call | solution.py:566
  31.4 0.0 collective-permute-done.far_ref
  31.4 1.9 %weight_sums.1 = (bf16[192,384]{1,0:T(8,128)(2,1)S(1)}, bf16[192,384]{1,0:T(8,128)(2,1)S(1)}, bf16[4,96,384]{2,1,0:T(8,128)(2,1)}) custom-call(s32[1]{0:T(128)} %get-tuple-element.28.shift_ref, bf16[6,12,8,384]{3,2,1,0:T(8,128)(2,1)S(1)} %get-tuple-element.29.x_ref, bf16[6,12,8,384]{3,2,1,0:T(8,128)(2,1)S(1)} %get-tuple-element.30.g_ref, ...), custom_call_target="tpu_custom_call" | custom-call | tf_op jit(solution)/shard_map/weight_sums/pallas_call | solution.py:598
  33.3 0.0 collective-permute-start.2
  33.3 1.1 %bias_rows.1.rows_ref = bf16[104,384]{1,0:T(8,128)(2,1)S(1)} custom-call(s32[1,4]{1,0:T(1,128)S(1)} %get-tuple-element.40.kind_ref, f32[3,64,384]{2,1,0:T(8,128)S(1)} %get-tuple-element.41.folded_ref), custom_call_target="tpu_custom_call" | custom-call | tf_op jit(solution)/shard_map/bias_rows/pallas_call | solution.py:615
  34.3 0.3 collective-permute-done.2.got_ref
  34.7 2.8 %collective-permute-start.5 = (bf16[296,384]{1,0:T(8,128)(2,1)S(1)}, bf16[296,384]{1,0:T(8,128)(2,1)S(1)}, u32[]{:S(2)}, u32[]{:S(2)}) collective-permute-start(bf16[296,384]{1,0:T(8,128)(2,1)S(1)} %pair.1.refs_0_), channel_id=1, source_target_pairs={{0,24},{4,28},{8,16},{12,20},{16,8},{20,12},{24,0},{28,4},{1,25},{... | collective-permute-start | bytes 681992 | tf_op jit(solution)/shard_map/ppermute | solution.py:649
  37.4 0.5 collective-permute-start.4
  38.0 0.3 collective-permute-start.3
  38.3 5.9 %collective-permute-done.5.refs_3_ = bf16[296,384]{1,0:T(8,128)(2,1)S(1)} collective-permute-done((bf16[296,384]{1,0:T(8,128)(2,1)S(1)}, bf16[296,384]{1,0:T(8,128)(2,1)S(1)}, u32[]{:S(2)}, u32[]{:S(2)}) %collective-permute-start.5) | collective-permute-done | bytes 227360 | tf_op jit(solution)/shard_map/ppermute | solution.py:649
  44.1 4.4 %collective-permute-done.4.refs_2_ = bf16[296,384]{1,0:T(8,128)(2,1)S(1)} collective-permute-done((bf16[296,384]{1,0:T(8,128)(2,1)S(1)}, bf16[296,384]{1,0:T(8,128)(2,1)S(1)}, u32[]{:S(2)}, u32[]{:S(2)}) %collective-permute-start.4) | collective-permute-done | bytes 227360 | tf_op jit(solution)/shard_map/ppermute | solution.py:649
  48.5 0.0 collective-permute-done.3.refs_1_
  48.5 0.2 merge.1.refs_0_
  48.8 0.1 collective-permute-start.6
  48.9 1.6 %collective-permute-start.7 = (bf16[432,128]{1,0:T(8,128)(2,1)S(1)}, bf16[432,128]{1,0:T(8,128)(2,1)S(1)}, u32[]{:S(2)}, u32[]{:S(2)}) collective-permute-start(bf16[432,128]{1,0:T(8,128)(2,1)S(1)} %get-tuple-element.43), channel_id=1, source_target_pairs={{0,1},{1,2},{2,3},{3,0},{4,5},{5,6},{6,7},{7,4},{8,9},{9,10},{10,1... | collective-permute-start | bytes 331784 | tf_op jit(solution)/shard_map/ppermute | solution.py:592
  50.5 2.6 %collective-permute-start.8 = (bf16[432,128]{1,0:T(8,128)(2,1)S(1)}, bf16[432,128]{1,0:T(8,128)(2,1)S(1)}, u32[]{:S(2)}, u32[]{:S(2)}) collective-permute-start(bf16[432,128]{1,0:T(8,128)(2,1)S(1)} %get-tuple-element.44), channel_id=1, source_target_pairs={{0,2},{1,3},{2,0},{3,1},{4,6},{5,7},{6,4},{7,5},{8,10},{9,11},{10,... | collective-permute-start | bytes 331784 | tf_op jit(solution)/shard_map/ppermute | solution.py:592
  53.1 1.3 %collective-permute-start.9 = (bf16[432,128]{1,0:T(8,128)(2,1)S(1)}, bf16[432,128]{1,0:T(8,128)(2,1)S(1)}, u32[]{:S(2)}, u32[]{:S(2)}) collective-permute-start(bf16[432,128]{1,0:T(8,128)(2,1)S(1)} %get-tuple-element.45), channel_id=1, source_target_pairs={{0,3},{1,0},{2,1},{3,2},{4,7},{5,4},{6,5},{7,6},{8,11},{9,8},{10,9... | collective-permute-start | bytes 331784 | tf_op jit(solution)/shard_map/ppermute | solution.py:592
  54.4 2.3 %collective-permute-done.7.refs_1_ = bf16[432,128]{1,0:T(8,128)(2,1)S(1)} collective-permute-done((bf16[432,128]{1,0:T(8,128)(2,1)S(1)}, bf16[432,128]{1,0:T(8,128)(2,1)S(1)}, u32[]{:S(2)}, u32[]{:S(2)}) %collective-permute-start.7) | collective-permute-done | bytes 110624 | tf_op jit(solution)/shard_map/ppermute | solution.py:592
  56.7 4.3 %collective-permute-done.8.refs_2_ = bf16[432,128]{1,0:T(8,128)(2,1)S(1)} collective-permute-done((bf16[432,128]{1,0:T(8,128)(2,1)S(1)}, bf16[432,128]{1,0:T(8,128)(2,1)S(1)}, u32[]{:S(2)}, u32[]{:S(2)}) %collective-permute-start.8) | collective-permute-done | bytes 110624 | tf_op jit(solution)/shard_map/ppermute | solution.py:592
  61.0 0.0 collective-permute-done.9.refs_3_
  61.0 0.7 %sum_heads.1 = (bf16[12,48,96]{2,1,0:T(8,128)(2,1)S(1)}, bf16[6,48,96]{2,1,0:T(8,128)(2,1)S(1)}) custom-call(s32[1]{0:T(128)} %get-tuple-element.28.shift_ref, bf16[432,128]{1,0:T(8,128)(2,1)S(1)} %get-tuple-element.42.refs_0_, bf16[432,128]{1,0:T(8,128)(2,1)S(1)} %collective-permute-done.7.refs_1_, bf16[432,128]{1,0:T(8,128)(2,1)S(1)} %collective-permute-done.8.refs_2_, ...), custom_call_target="tpu_custom_call" | custom-call | tf_op jit(solution)/shard_map/sum_heads/pallas_call | solution.py:628
  61.7 1.5 %collective-permute-start.10 = (bf16[6,48,96]{2,1,0:T(8,128)(2,1)S(1)}, bf16[6,48,96]{2,1,0:T(8,128)(2,1)S(1)}, u32[]{:S(2)}, u32[]{:S(2)}) collective-permute-start(bf16[6,48,96]{2,1,0:T(8,128)(2,1)S(1)} %get-tuple-element.47), channel_id=1, source_target_pairs={{0,16},{16,0},{1,17},{17,1},{2,18},{18,2},{3,19},{19,3},{4,20},{20... | collective-permute-start | bytes 165896 | tf_op jit(solution)/shard_map/ppermute | solution.py:495
  63.2 2.9 %collective-permute-done.10.refs_3_ = bf16[6,48,96]{2,1,0:T(8,128)(2,1)S(1)} collective-permute-done((bf16[6,48,96]{2,1,0:T(8,128)(2,1)S(1)}, bf16[6,48,96]{2,1,0:T(8,128)(2,1)S(1)}, u32[]{:S(2)}, u32[]{:S(2)}) %collective-permute-start.10) | collective-permute-done | bytes 55328 | tf_op jit(solution)/shard_map/ppermute | solution.py:495
  66.1 0.0 collective-permute-done.6.refs_1_
  66.1 2.8 %finish.1 = (bf16[6,12,8,96]{3,2,1,0:T(8,128)(2,1)}, f32[3,96,384]{2,1,0:T(8,128)}, f32[96,384]{1,0:T(8,128)}, f32[3,64,3312]{2,1,0:T(8,128)}) custom-call(s32[1]{0:T(128)} %get-tuple-element.28.shift_ref, bf16[2,200,384]{2,1,0:T(8,128)(2,1)S(1)} %merge.1.refs_0_, bf16[2,200,384]{2,1,0:T(8,128)(2,1)S(1)} %collective-permute-done.6.refs_1_, ...), custom_call_target="tpu_custom_call" | custom-call | tf_op jit(solution)/shard_map/finish/pallas_call | solution.py:671
  (1 shorter events, 0.0 us)
Async XLA Ops:
  3.1 0.7 copy-start
  7.5 23.9 %collective-permute-start = (bf16[2,6,6,8,384]{4,3,2,1,0:T(8,128)(2,1)S(1)}, bf16[2,6,6,8,384]{4,3,2,1,0:T(8,128)(2,1)S(1)}, u32[]{:S(2)}, u32[]{:S(2)}) collective-permute-start(bf16[2,6,6,8,384]{4,3,2,1,0:T(8,128)(2,1)S(1)} %get-tuple-element.32), channel_id=1, source_target_pairs={{0,16},{16,0},{1,17},{17,1},{2,18},{18,2},{3,19},{19,3},{4,20},{20... | collective-permute-start | bytes 1327112 | tf_op jit(solution)/shard_map/ppermute | solution.py:495
  10.5 14.9 %collective-permute-start.1 = (bf16[6,48,384]{2,1,0:T(8,128)(2,1)S(1)}, bf16[6,48,384]{2,1,0:T(8,128)(2,1)S(1)}, u32[]{:S(2)}, u32[]{:S(2)}) collective-permute-start(bf16[6,48,384]{2,1,0:T(8,128)(2,1)S(1)} %get-tuple-element.33), channel_id=1, source_target_pairs={{0,16},{16,0},{1,17},{17,1},{2,18},{18,2},{3,19},{19,3},{4,20},{20... | collective-permute-start | bytes 663560 | tf_op jit(solution)/shard_map/ppermute | solution.py:495
  33.3 1.4 %collective-permute-start.2 = (bf16[192,384]{1,0:T(8,128)(2,1)S(1)}, bf16[192,384]{1,0:T(8,128)(2,1)S(1)}, u32[]{:S(2)}, u32[]{:S(2)}) collective-permute-start(bf16[192,384]{1,0:T(8,128)(2,1)S(1)} %get-tuple-element.39), channel_id=1, source_target_pairs={{0,4},{4,0},{8,12},{12,8},{1,5},{5,1},{9,13},{13,9},{2,6},{6,2},{1... | collective-permute-start | bytes 442376 | tf_op jit(solution)/shard_map/ppermute | solution.py:608
  34.7 9.4 %collective-permute-start.5 = (bf16[296,384]{1,0:T(8,128)(2,1)S(1)}, bf16[296,384]{1,0:T(8,128)(2,1)S(1)}, u32[]{:S(2)}, u32[]{:S(2)}) collective-permute-start(bf16[296,384]{1,0:T(8,128)(2,1)S(1)} %pair.1.refs_0_), channel_id=1, source_target_pairs={{0,24},{4,28},{8,16},{12,20},{16,8},{20,12},{24,0},{28,4},{1,25},{... | collective-permute-start | bytes 681992 | tf_op jit(solution)/shard_map/ppermute | solution.py:649
  37.4 11.1 %collective-permute-start.4 = (bf16[296,384]{1,0:T(8,128)(2,1)S(1)}, bf16[296,384]{1,0:T(8,128)(2,1)S(1)}, u32[]{:S(2)}, u32[]{:S(2)}) collective-permute-start(bf16[296,384]{1,0:T(8,128)(2,1)S(1)} %pair.1.refs_0_), channel_id=1, source_target_pairs={{0,16},{4,20},{8,24},{12,28},{16,0},{20,4},{24,8},{28,12},{1,17},{... | collective-permute-start | bytes 681992 | tf_op jit(solution)/shard_map/ppermute | solution.py:649
  38.0 10.6 %collective-permute-start.3 = (bf16[296,384]{1,0:T(8,128)(2,1)S(1)}, bf16[296,384]{1,0:T(8,128)(2,1)S(1)}, u32[]{:S(2)}, u32[]{:S(2)}) collective-permute-start(bf16[296,384]{1,0:T(8,128)(2,1)S(1)} %pair.1.refs_0_), channel_id=1, source_target_pairs={{0,8},{4,12},{8,0},{12,4},{16,24},{20,28},{24,16},{28,20},{1,9},{5... | collective-permute-start | bytes 681992 | tf_op jit(solution)/shard_map/ppermute | solution.py:649
  48.8 17.3 %collective-permute-start.6 = (bf16[2,200,384]{2,1,0:T(8,128)(2,1)S(1)}, bf16[2,200,384]{2,1,0:T(8,128)(2,1)S(1)}, u32[]{:S(2)}, u32[]{:S(2)}) collective-permute-start(bf16[2,200,384]{2,1,0:T(8,128)(2,1)S(1)} %merge.1.refs_0_), channel_id=1, source_target_pairs={{0,4},{4,0},{8,12},{12,8},{1,5},{5,1},{9,13},{13,9},{2,6},{6,2},{1... | collective-permute-start | bytes 921608 | tf_op jit(solution)/shard_map/ppermute | solution.py:659
  48.9 7.9 %collective-permute-start.7 = (bf16[432,128]{1,0:T(8,128)(2,1)S(1)}, bf16[432,128]{1,0:T(8,128)(2,1)S(1)}, u32[]{:S(2)}, u32[]{:S(2)}) collective-permute-start(bf16[432,128]{1,0:T(8,128)(2,1)S(1)} %get-tuple-element.43), channel_id=1, source_target_pairs={{0,1},{1,2},{2,3},{3,0},{4,5},{5,6},{6,7},{7,4},{8,9},{9,10},{10,1... | collective-permute-start | bytes 331784 | tf_op jit(solution)/shard_map/ppermute | solution.py:592
  50.5 10.5 %collective-permute-start.8 = (bf16[432,128]{1,0:T(8,128)(2,1)S(1)}, bf16[432,128]{1,0:T(8,128)(2,1)S(1)}, u32[]{:S(2)}, u32[]{:S(2)}) collective-permute-start(bf16[432,128]{1,0:T(8,128)(2,1)S(1)} %get-tuple-element.44), channel_id=1, source_target_pairs={{0,2},{1,3},{2,0},{3,1},{4,6},{5,7},{6,4},{7,5},{8,10},{9,11},{10,... | collective-permute-start | bytes 331784 | tf_op jit(solution)/shard_map/ppermute | solution.py:592
  53.1 7.9 %collective-permute-start.9 = (bf16[432,128]{1,0:T(8,128)(2,1)S(1)}, bf16[432,128]{1,0:T(8,128)(2,1)S(1)}, u32[]{:S(2)}, u32[]{:S(2)}) collective-permute-start(bf16[432,128]{1,0:T(8,128)(2,1)S(1)} %get-tuple-element.45), channel_id=1, source_target_pairs={{0,3},{1,0},{2,1},{3,2},{4,7},{5,4},{6,5},{7,6},{8,11},{9,8},{10,9... | collective-permute-start | bytes 331784 | tf_op jit(solution)/shard_map/ppermute | solution.py:592
  61.7 4.4 %collective-permute-start.10 = (bf16[6,48,96]{2,1,0:T(8,128)(2,1)S(1)}, bf16[6,48,96]{2,1,0:T(8,128)(2,1)S(1)}, u32[]{:S(2)}, u32[]{:S(2)}) collective-permute-start(bf16[6,48,96]{2,1,0:T(8,128)(2,1)S(1)} %get-tuple-element.47), channel_id=1, source_target_pairs={{0,16},{16,0},{1,17},{17,1},{2,18},{18,2},{3,19},{19,3},{4,20},{20... | collective-permute-start | bytes 165896 | tf_op jit(solution)/shard_map/ppermute | solution.py:495

commit v7 on v6

--- a/solution.py
+++ b/solution.py
@@ -327,27 +327,32 @@
                 ref[i * width : (i + 1) * width, :] = sums_ref[2 * side + i]
 
 
-def pair_kernel(kept_ref, got_ref, rows_ref, out_ref):
+def pair_kernel(kept_ref, got_ref, rows_ref, first_ref, second_ref):
     count = rows_ref.shape[0]
-    out_ref[:count, :] = rows_ref[...]
-    out_ref[count:, :] = (kept_ref[...].astype(F32) + got_ref[...].astype(F32)).astype(BF16)
-
-
-def merge_kernel(*refs):
-    *parts, out_ref, all_ref = refs
-    chip = lax.axis_index("lon") * 2 + lax.div(lax.axis_index("lat"), 2)
-    for i, part in enumerate(parts):
-        all_ref[lax.bitwise_xor(chip, i)] = part[...]
-    share = (parts[0].shape[0] - BIAS_ROWS) // 2
+    cut = first_ref.shape[0] - count
+    total = (kept_ref[...].astype(F32) + got_ref[...].astype(F32)).astype(BF16)
+    first_ref[:count, :] = rows_ref[...]
+    first_ref[count:, :] = total[:cut, :]
+    second_ref[...] = total[cut:, :]
+
+
+def add_kernel(first_ref, got_first_ref, second_ref, got_second_ref, *outs):
+    for out, own, got in zip(outs, (first_ref, second_ref), (got_first_ref, got_second_ref)):
+        out[...] = (own[...].astype(F32) + got[...].astype(F32)).astype(BF16)
+
+
+def merge_kernel(first_ref, got_first_ref, second_ref, got_second_ref, out_ref, sums_ref):
+    row = lax.rem(lax.div(lax.axis_index("lat"), 2), 2)
+    cut = first_ref.shape[0] - BIAS_ROWS
+    share = out_ref.shape[1] - BIAS_ROWS
+    out_ref[row, :BIAS_ROWS, :] = first_ref[:BIAS_ROWS, :]
+    out_ref[1 - row, :BIAS_ROWS, :] = got_first_ref[:BIAS_ROWS, :]
+    sums_ref[:cut, :] = first_ref[BIAS_ROWS:, :].astype(F32) + got_first_ref[
+        BIAS_ROWS:, :
+    ].astype(F32)
+    sums_ref[cut:, :] = second_ref[...].astype(F32) + got_second_ref[...].astype(F32)
     for j in range(2):
-        low = all_ref[j, :BIAS_ROWS, :].astype(F32)
-        high = all_ref[2 + j, :BIAS_ROWS, :].astype(F32)
-        out_ref[j, :BIAS_ROWS, :] = (low + high).astype(BF16)
-        start = BIAS_ROWS + j * share
-        total = all_ref[0, start : start + share, :].astype(F32)
-        for i in range(1, 4):
-            total = total + all_ref[i, start : start + share, :].astype(F32)
-        out_ref[j, BIAS_ROWS:, :] = total.astype(BF16)
+        out_ref[j, BIAS_ROWS:, :] = sums_ref[j * share : (j + 1) * share, :].astype(BF16)
 
 
 def bias_kernel(kind_ref, folded_ref, out_ref, pieces_ref, natural_ref, dense_ref):
@@ -635,27 +640,43 @@
     )(shift, *parts)
     returned = exchange(back, "lon", shift, -1)
     if paired:
-        part = pl.pallas_call(
+        cut = width // 2
+        pair_shapes = [
+            shape((rows.shape[0] + cut, depth), BF16),
+            shape((2 * width - cut, depth), BF16),
+        ]
+        first, second = pl.pallas_call(
             pair_kernel,
             name="pair",
-            out_shape=shape((rows.shape[0] + 2 * width, depth), BF16),
+            out_shape=pair_shapes,
             in_specs=[VMEM] * 3,
-            out_specs=VMEM,
+            out_specs=[VMEM] * 2,
             compiler_params=small(4),
         )(halves[0], got, rows)
-        chips = [part]
-        for step in range(1, 4):
-            ring = [(i, i ^ (2 * step)) for i in range(n_every)]
-            chips.append(lax.ppermute(part, every, ring))
+
+        def across(array, mask):
+            ring = [(i, i ^ mask) for i in range(n_every)]
+            return lax.ppermute(array, every, ring)
+
+        operands = (first, across(first, n_lat), second, across(second, 2))
+        first, second = pl.pallas_call(
+            add_kernel,
+            name="add",
+            out_shape=pair_shapes,
+            in_specs=[VMEM] * 4,
+            out_specs=[VMEM] * 2,
+            compiler_params=small(4),
+        )(*operands)
+        operands = (first, across(first, 2), second, across(second, n_lat))
         merged = pl.pallas_call(
             merge_kernel,
             name="merge",
             out_shape=shape((2, rows.shape[0] + width, depth), BF16),
             in_specs=[VMEM] * 4,
             out_specs=VMEM,
-            scratch_shapes=[pltpu.VMEM((4, *part.shape), BF16)],
+            scratch_shapes=[pltpu.VMEM((2 * width, depth), F32)],
             compiler_params=small(6),
-        )(*chips)
+        )(*operands)
         other = lax.ppermute(merged, "lat", [(i, i ^ 1) for i in range(n_lat)])
         gathered = [merged, other]
     else:

time: 69.2 us -> 68.4 us (0.988)
  waiting for transfers between devices: 34.9 us -> 33.1 us
  starting transfers between devices: 13.8 us -> 14.8 us
    ppermute x3 -> x4, waiting for transfers between devices: 10.3 us -> 7.6 us  [across(): return lax.ppermute(array, every, ring)]
    ppermute x3 -> x4, starting transfers between devices: 3.55 us -> 5.46 us  [across(): return lax.ppermute(array, every, ring)]
    ppermute x3, waiting for transfers between devices: 17.7 us -> 18.7 us  [exchange(): lax.ppermute(x, axis, [(i, (i - sign) % count) for i in range(count)])]
    ppermute x3, starting transfers between devices: 4.65 us -> 3.71 us  [exchange(): lax.ppermute(x, axis, [(i, (i - sign) % count) for i in range(count)])]
  transfers between devices with their start and end apart: 11 -> 12, of which waited for: 7 -> 7; matrix products, arithmetic and copies ran while one was open for 0% -> 0% of each run, Pallas kernels for 11% -> 11%
where the time goes in v7:
time: 68.4 us; the launch traced here: 68.1 us
  waiting for transfers between devices  33.1 us (48%)
  Pallas kernels  18.2 us (27%)
  starting transfers between devices  14.8 us (22%)
  between operations  1.36 us (2%)
    ppermute x3, waiting for transfers between devices, exchange(): lax.ppermute(x, axis, [(i, (i - sign) % count) for i in range(count)])  18.7 us
    ppermute x4, waiting for transfers between devices, across(): return lax.ppermute(array, every, ring)  7.6 us
    ppermute x3, waiting for transfers between devices, per_device(): parts.append(lax.ppermute(pieces[step], 'head', ring))  6.57 us
    pallas_call x1, Pallas kernels, per_device(): pl.pallas_call(main_kernel, name='main', out_shape=[shape((packed, LANES)...  5.96 us
    ppermute x3, starting transfers between devices, per_device(): parts.append(lax.ppermute(pieces[step], 'head', ring))  5.54 us
    ppermute x4, starting transfers between devices, across(): return lax.ppermute(array, every, ring)  5.46 us
    pallas_call x1, Pallas kernels, per_device(): prepare(shift, own_x, own_g, rows, bias_type.reshape(1, slots), stored(ta...  3.73 us
    ppermute x3, starting transfers between devices, exchange(): lax.ppermute(x, axis, [(i, (i - sign) % count) for i in range(count)])  3.71 us
  transfers between devices with their start and end apart: 12, of which 7 were waited for; matrix products, arithmetic and copies ran while one was open for 0% of the time, Pallas kernels for 11%

profile of v7, /device:TPU:0, one launch (start us, length us, event | category | flops | bytes accessed | tf_op | source)
XLA Modules:
  0.0 68.1 jit_solution(11353884806042339122)
XLA Ops:
  1.3 1.8 %start.1 = (s32[1]{0:T(128)}, bf16[6,12,8,384]{3,2,1,0:T(8,128)(2,1)S(1)}, bf16[6,12,8,384]{3,2,1,0:T(8,128)(2,1)S(1)}, bf16[6,48,384]{2,1,0:T(8,128)(2,1)S(1)}, bf16[384,384]{1,0:T(8,128)(2,1)S(1)}) custom-call(s32[1]{0:T(128)S(6)} %copy.11.shift_ref, bf16[6,12,8,384]{3,2,1,0:T(8,128)(2,1)} %bitcast.10, bf16[6,12,8,384]{3,2,1,0:T(8,128)(2,1)} %bitcast.11, ...), custom_call_target="tpu_custom_call" | custom-call | tf_op jit(solution)/shard_map/start/pallas_call | solution.py:529
  3.1 0.0 copy-start
  3.1 0.6 copy-done
  3.7 3.7 %prepare.1 = (s32[1,4]{1,0:T(1,128)S(1)}, bf16[2,6,6,8,384]{4,3,2,1,0:T(8,128)(2,1)S(1)}, f32[4,576,192]{2,1,0:T(8,128)S(1)}, bf16[12,48,512]{2,1,0:T(8,128)(2,1)S(1)}, bf16[512,384]{1,0:T(8,128)(2,1)S(1)}) custom-call(s32[1]{0:T(128)} %get-tuple-element.32.shift_ref, bf16[6,12,8,384]{3,2,1,0:T(8,128)(2,1)S(1)} %get-tuple-element.33.x_ref, ...), custom_call_target="tpu_custom_call" | custom-call | tf_op jit(solution)/shard_map/prepare/pallas_call | solution.py:566
  7.5 3.0 %collective-permute-start = (bf16[2,6,6,8,384]{4,3,2,1,0:T(8,128)(2,1)S(1)}, bf16[2,6,6,8,384]{4,3,2,1,0:T(8,128)(2,1)S(1)}, u32[]{:S(2)}, u32[]{:S(2)}) collective-permute-start(bf16[2,6,6,8,384]{4,3,2,1,0:T(8,128)(2,1)S(1)} %get-tuple-element.36), channel_id=1, source_target_pairs={{0,16},{16,0},{1,17},{17,1},{2,18},{18,2},{3,19},{19,3},{4,20},{20... | collective-permute-start | bytes 1327112 | tf_op jit(solution)/shard_map/ppermute | solution.py:500
  10.5 0.1 collective-permute-start.1
  10.6 14.8 %collective-permute-done.1.far_ref = bf16[6,48,384]{2,1,0:T(8,128)(2,1)S(1)} collective-permute-done((bf16[6,48,384]{2,1,0:T(8,128)(2,1)S(1)}, bf16[6,48,384]{2,1,0:T(8,128)(2,1)S(1)}, u32[]{:S(2)}, u32[]{:S(2)}) %collective-permute-start.1) | collective-permute-done | bytes 221216 | tf_op jit(solution)/shard_map/ppermute | solution.py:500
  25.4 6.0 %main.1 = (bf16[432,128]{1,0:T(8,128)(2,1)S(1)}, bf16[432,128]{1,0:T(8,128)(2,1)S(1)}, bf16[432,128]{1,0:T(8,128)(2,1)S(1)}, bf16[432,128]{1,0:T(8,128)(2,1)S(1)...) custom-call(s32[1]{0:T(128)} %get-tuple-element.32.shift_ref, ...), custom_call_target="tpu_custom_call" | custom-call | tf_op jit(solution)/shard_map/main/pallas_call | solution.py:571
  31.4 0.0 collective-permute-done.far_ref
  31.4 1.9 %weight_sums.1 = (bf16[192,384]{1,0:T(8,128)(2,1)S(1)}, bf16[192,384]{1,0:T(8,128)(2,1)S(1)}, bf16[4,96,384]{2,1,0:T(8,128)(2,1)}) custom-call(s32[1]{0:T(128)} %get-tuple-element.32.shift_ref, bf16[6,12,8,384]{3,2,1,0:T(8,128)(2,1)S(1)} %get-tuple-element.33.x_ref, bf16[6,12,8,384]{3,2,1,0:T(8,128)(2,1)S(1)} %get-tuple-element.34.g_ref, ...), custom_call_target="tpu_custom_call" | custom-call | tf_op jit(solution)/shard_map/weight_sums/pallas_call | solution.py:603
  33.3 0.0 collective-permute-start.2
  33.3 1.1 %bias_rows.1.rows_ref = bf16[104,384]{1,0:T(8,128)(2,1)S(1)} custom-call(s32[1,4]{1,0:T(1,128)S(1)} %get-tuple-element.44.kind_ref, f32[3,64,384]{2,1,0:T(8,128)S(1)} %get-tuple-element.45.folded_ref), custom_call_target="tpu_custom_call" | custom-call | tf_op jit(solution)/shard_map/bias_rows/pallas_call | solution.py:620
  34.4 0.3 collective-permute-done.2.got_ref
  34.7 1.8 %collective-permute-start.3 = (bf16[152,384]{1,0:T(8,128)(2,1)S(1)}, bf16[152,384]{1,0:T(8,128)(2,1)S(1)}, u32[]{:S(2)}, u32[]{:S(2)}) collective-permute-start(bf16[152,384]{1,0:T(8,128)(2,1)S(1)} %get-tuple-element.46.first_ref), channel_id=1, source_target_pairs={{0,16},{4,20},{8,24},{12,28},{16,0},{20,4},{24,8},{28,12},{1,17},{... | collective-permute-start | bytes 350216 | tf_op jit(solution)/shard_map/ppermute | solution.py:659
  36.5 1.5 %collective-permute-start.4 = (bf16[144,384]{1,0:T(8,128)(2,1)S(1)}, bf16[144,384]{1,0:T(8,128)(2,1)S(1)}, u32[]{:S(2)}, u32[]{:S(2)}) collective-permute-start(bf16[144,384]{1,0:T(8,128)(2,1)S(1)} %get-tuple-element.47.second_ref), channel_id=1, source_target_pairs={{0,8},{4,12},{8,0},{12,4},{16,24},{20,28},{24,16},{28,20},{1,9},{5... | collective-permute-start | bytes 331784 | tf_op jit(solution)/shard_map/ppermute | solution.py:659
  38.1 3.4 %collective-permute-done.4.got_second_ref = bf16[144,384]{1,0:T(8,128)(2,1)S(1)} collective-permute-done((bf16[144,384]{1,0:T(8,128)(2,1)S(1)}, bf16[144,384]{1,0:T(8,128)(2,1)S(1)}, u32[]{:S(2)}, u32[]{:S(2)}) %collective-permute-start.4) | collective-permute-done | bytes 110624 | tf_op jit(solution)/shard_map/ppermute | solution.py:659
  41.4 0.1 add.1
  41.5 1.6 %collective-permute-start.5 = (bf16[152,384]{1,0:T(8,128)(2,1)S(1)}, bf16[152,384]{1,0:T(8,128)(2,1)S(1)}, u32[]{:S(2)}, u32[]{:S(2)}) collective-permute-start(bf16[152,384]{1,0:T(8,128)(2,1)S(1)} %get-tuple-element.48.first_ref), channel_id=1, source_target_pairs={{0,8},{4,12},{8,0},{12,4},{16,24},{20,28},{24,16},{28,20},{1,9},{5... | collective-permute-start | bytes 350216 | tf_op jit(solution)/shard_map/ppermute | solution.py:659
  43.1 0.5 collective-permute-start.6
  43.6 4.2 %collective-permute-done.6.got_second_ref = bf16[144,384]{1,0:T(8,128)(2,1)S(1)} collective-permute-done((bf16[144,384]{1,0:T(8,128)(2,1)S(1)}, bf16[144,384]{1,0:T(8,128)(2,1)S(1)}, u32[]{:S(2)}, u32[]{:S(2)}) %collective-permute-start.6) | collective-permute-done | bytes 110624 | tf_op jit(solution)/shard_map/ppermute | solution.py:659
  47.8 0.0 collective-permute-done.5.got_first_ref
  47.9 0.1 merge.1.refs_0_
  47.9 0.1 collective-permute-start.7
  48.0 1.6 %collective-permute-start.8 = (bf16[432,128]{1,0:T(8,128)(2,1)S(1)}, bf16[432,128]{1,0:T(8,128)(2,1)S(1)}, u32[]{:S(2)}, u32[]{:S(2)}) collective-permute-start(bf16[432,128]{1,0:T(8,128)(2,1)S(1)} %get-tuple-element.51), channel_id=1, source_target_pairs={{0,1},{1,2},{2,3},{3,0},{4,5},{5,6},{6,7},{7,4},{8,9},{9,10},{10,1... | collective-permute-start | bytes 331784 | tf_op jit(solution)/shard_map/ppermute | solution.py:597
  49.6 2.6 %collective-permute-start.9 = (bf16[432,128]{1,0:T(8,128)(2,1)S(1)}, bf16[432,128]{1,0:T(8,128)(2,1)S(1)}, u32[]{:S(2)}, u32[]{:S(2)}) collective-permute-start(bf16[432,128]{1,0:T(8,128)(2,1)S(1)} %get-tuple-element.52), channel_id=1, source_target_pairs={{0,2},{1,3},{2,0},{3,1},{4,6},{5,7},{6,4},{7,5},{8,10},{9,11},{10,... | collective-permute-start | bytes 331784 | tf_op jit(solution)/shard_map/ppermute | solution.py:597
  52.2 1.3 %collective-permute-start.10 = (bf16[432,128]{1,0:T(8,128)(2,1)S(1)}, bf16[432,128]{1,0:T(8,128)(2,1)S(1)}, u32[]{:S(2)}, u32[]{:S(2)}) collective-permute-start(bf16[432,128]{1,0:T(8,128)(2,1)S(1)} %get-tuple-element.53), channel_id=1, source_target_pairs={{0,3},{1,0},{2,1},{3,2},{4,7},{5,4},{6,5},{7,6},{8,11},{9,8},{10,9... | collective-permute-start | bytes 331784 | tf_op jit(solution)/shard_map/ppermute | solution.py:597
  53.5 2.3 %collective-permute-done.8.refs_1_ = bf16[432,128]{1,0:T(8,128)(2,1)S(1)} collective-permute-done((bf16[432,128]{1,0:T(8,128)(2,1)S(1)}, bf16[432,128]{1,0:T(8,128)(2,1)S(1)}, u32[]{:S(2)}, u32[]{:S(2)}) %collective-permute-start.8) | collective-permute-done | bytes 110624 | tf_op jit(solution)/shard_map/ppermute | solution.py:597
  55.9 4.2 %collective-permute-done.9.refs_2_ = bf16[432,128]{1,0:T(8,128)(2,1)S(1)} collective-permute-done((bf16[432,128]{1,0:T(8,128)(2,1)S(1)}, bf16[432,128]{1,0:T(8,128)(2,1)S(1)}, u32[]{:S(2)}, u32[]{:S(2)}) %collective-permute-start.9) | collective-permute-done | bytes 110624 | tf_op jit(solution)/shard_map/ppermute | solution.py:597
  60.1 0.7 %sum_heads.1 = (bf16[12,48,96]{2,1,0:T(8,128)(2,1)S(1)}, bf16[6,48,96]{2,1,0:T(8,128)(2,1)S(1)}) custom-call(s32[1]{0:T(128)} %get-tuple-element.32.shift_ref, bf16[432,128]{1,0:T(8,128)(2,1)S(1)} %get-tuple-element.50.refs_0_, bf16[432,128]{1,0:T(8,128)(2,1)S(1)} %collective-permute-done.8.refs_1_, bf16[432,128]{1,0:T(8,128)(2,1)S(1)} %collective-permute-done.9.refs_2_, ...), custom_call_target="tpu_custom_call" | custom-call | tf_op jit(solution)/shard_map/sum_heads/pallas_call | solution.py:633
  60.8 0.6 collective-permute-start.11
  61.4 3.8 %collective-permute-done.11.refs_3_ = bf16[6,48,96]{2,1,0:T(8,128)(2,1)S(1)} collective-permute-done((bf16[6,48,96]{2,1,0:T(8,128)(2,1)S(1)}, bf16[6,48,96]{2,1,0:T(8,128)(2,1)S(1)}, u32[]{:S(2)}, u32[]{:S(2)}) %collective-permute-start.11) | collective-permute-done | bytes 55328 | tf_op jit(solution)/shard_map/ppermute | solution.py:500
  65.2 2.8 %finish.1 = (bf16[6,12,8,96]{3,2,1,0:T(8,128)(2,1)}, f32[3,96,384]{2,1,0:T(8,128)}, f32[96,384]{1,0:T(8,128)}, f32[3,64,3312]{2,1,0:T(8,128)}) custom-call(s32[1]{0:T(128)} %get-tuple-element.32.shift_ref, bf16[2,200,384]{2,1,0:T(8,128)(2,1)S(1)} %merge.1.refs_0_, bf16[2,200,384]{2,1,0:T(8,128)(2,1)S(1)} %collective-permute-done.7.refs_1_, ...), custom_call_target="tpu_custom_call" | custom-call | tf_op jit(solution)/shard_map/finish/pallas_call | solution.py:692
  (4 shorter events, 0.1 us)
Async XLA Ops:
  3.1 0.7 copy-start
  7.5 23.9 %collective-permute-start = (bf16[2,6,6,8,384]{4,3,2,1,0:T(8,128)(2,1)S(1)}, bf16[2,6,6,8,384]{4,3,2,1,0:T(8,128)(2,1)S(1)}, u32[]{:S(2)}, u32[]{:S(2)}) collective-permute-start(bf16[2,6,6,8,384]{4,3,2,1,0:T(8,128)(2,1)S(1)} %get-tuple-element.36), channel_id=1, source_target_pairs={{0,16},{16,0},{1,17},{17,1},{2,18},{18,2},{3,19},{19,3},{4,20},{20... | collective-permute-start | bytes 1327112 | tf_op jit(solution)/shard_map/ppermute | solution.py:500
  10.5 14.9 %collective-permute-start.1 = (bf16[6,48,384]{2,1,0:T(8,128)(2,1)S(1)}, bf16[6,48,384]{2,1,0:T(8,128)(2,1)S(1)}, u32[]{:S(2)}, u32[]{:S(2)}) collective-permute-start(bf16[6,48,384]{2,1,0:T(8,128)(2,1)S(1)} %get-tuple-element.37), channel_id=1, source_target_pairs={{0,16},{16,0},{1,17},{17,1},{2,18},{18,2},{3,19},{19,3},{4,20},{20... | collective-permute-start | bytes 663560 | tf_op jit(solution)/shard_map/ppermute | solution.py:500
  33.3 1.4 %collective-permute-start.2 = (bf16[192,384]{1,0:T(8,128)(2,1)S(1)}, bf16[192,384]{1,0:T(8,128)(2,1)S(1)}, u32[]{:S(2)}, u32[]{:S(2)}) collective-permute-start(bf16[192,384]{1,0:T(8,128)(2,1)S(1)} %get-tuple-element.43), channel_id=1, source_target_pairs={{0,4},{4,0},{8,12},{12,8},{1,5},{5,1},{9,13},{13,9},{2,6},{6,2},{1... | collective-permute-start | bytes 442376 | tf_op jit(solution)/shard_map/ppermute | solution.py:613
  34.7 6.7 %collective-permute-start.3 = (bf16[152,384]{1,0:T(8,128)(2,1)S(1)}, bf16[152,384]{1,0:T(8,128)(2,1)S(1)}, u32[]{:S(2)}, u32[]{:S(2)}) collective-permute-start(bf16[152,384]{1,0:T(8,128)(2,1)S(1)} %get-tuple-element.46.first_ref), channel_id=1, source_target_pairs={{0,16},{4,20},{8,24},{12,28},{16,0},{20,4},{24,8},{28,12},{1,17},{... | collective-permute-start | bytes 350216 | tf_op jit(solution)/shard_map/ppermute | solution.py:659
  36.5 4.9 %collective-permute-start.4 = (bf16[144,384]{1,0:T(8,128)(2,1)S(1)}, bf16[144,384]{1,0:T(8,128)(2,1)S(1)}, u32[]{:S(2)}, u32[]{:S(2)}) collective-permute-start(bf16[144,384]{1,0:T(8,128)(2,1)S(1)} %get-tuple-element.47.second_ref), channel_id=1, source_target_pairs={{0,8},{4,12},{8,0},{12,4},{16,24},{20,28},{24,16},{28,20},{1,9},{5... | collective-permute-start | bytes 331784 | tf_op jit(solution)/shard_map/ppermute | solution.py:659
  41.5 6.4 %collective-permute-start.5 = (bf16[152,384]{1,0:T(8,128)(2,1)S(1)}, bf16[152,384]{1,0:T(8,128)(2,1)S(1)}, u32[]{:S(2)}, u32[]{:S(2)}) collective-permute-start(bf16[152,384]{1,0:T(8,128)(2,1)S(1)} %get-tuple-element.48.first_ref), channel_id=1, source_target_pairs={{0,8},{4,12},{8,0},{12,4},{16,24},{20,28},{24,16},{28,20},{1,9},{5... | collective-permute-start | bytes 350216 | tf_op jit(solution)/shard_map/ppermute | solution.py:659
  43.1 4.7 %collective-permute-start.6 = (bf16[144,384]{1,0:T(8,128)(2,1)S(1)}, bf16[144,384]{1,0:T(8,128)(2,1)S(1)}, u32[]{:S(2)}, u32[]{:S(2)}) collective-permute-start(bf16[144,384]{1,0:T(8,128)(2,1)S(1)} %get-tuple-element.49.second_ref), channel_id=1, source_target_pairs={{0,16},{4,20},{8,24},{12,28},{16,0},{20,4},{24,8},{28,12},{1,17},{... | collective-permute-start | bytes 331784 | tf_op jit(solution)/shard_map/ppermute | solution.py:659
  47.9 17.3 %collective-permute-start.7 = (bf16[2,200,384]{2,1,0:T(8,128)(2,1)S(1)}, bf16[2,200,384]{2,1,0:T(8,128)(2,1)S(1)}, u32[]{:S(2)}, u32[]{:S(2)}) collective-permute-start(bf16[2,200,384]{2,1,0:T(8,128)(2,1)S(1)} %merge.1.refs_0_), channel_id=1, source_target_pairs={{0,4},{4,0},{8,12},{12,8},{1,5},{5,1},{9,13},{13,9},{2,6},{6,2},{1... | collective-permute-start | bytes 921608 | tf_op jit(solution)/shard_map/ppermute | solution.py:680
  48.0 7.9 %collective-permute-start.8 = (bf16[432,128]{1,0:T(8,128)(2,1)S(1)}, bf16[432,128]{1,0:T(8,128)(2,1)S(1)}, u32[]{:S(2)}, u32[]{:S(2)}) collective-permute-start(bf16[432,128]{1,0:T(8,128)(2,1)S(1)} %get-tuple-element.51), channel_id=1, source_target_pairs={{0,1},{1,2},{2,3},{3,0},{4,5},{5,6},{6,7},{7,4},{8,9},{9,10},{10,1... | collective-permute-start | bytes 331784 | tf_op jit(solution)/shard_map/ppermute | solution.py:597
  49.6 10.5 %collective-permute-start.9 = (bf16[432,128]{1,0:T(8,128)(2,1)S(1)}, bf16[432,128]{1,0:T(8,128)(2,1)S(1)}, u32[]{:S(2)}, u32[]{:S(2)}) collective-permute-start(bf16[432,128]{1,0:T(8,128)(2,1)S(1)} %get-tuple-element.52), channel_id=1, source_target_pairs={{0,2},{1,3},{2,0},{3,1},{4,6},{5,7},{6,4},{7,5},{8,10},{9,11},{10,... | collective-permute-start | bytes 331784 | tf_op jit(solution)/shard_map/ppermute | solution.py:597
  52.2 7.9 %collective-permute-start.10 = (bf16[432,128]{1,0:T(8,128)(2,1)S(1)}, bf16[432,128]{1,0:T(8,128)(2,1)S(1)}, u32[]{:S(2)}, u32[]{:S(2)}) collective-permute-start(bf16[432,128]{1,0:T(8,128)(2,1)S(1)} %get-tuple-element.53), channel_id=1, source_target_pairs={{0,3},{1,0},{2,1},{3,2},{4,7},{5,4},{6,5},{7,6},{8,11},{9,8},{10,9... | collective-permute-start | bytes 331784 | tf_op jit(solution)/shard_map/ppermute | solution.py:597
  60.8 4.4 %collective-permute-start.11 = (bf16[6,48,96]{2,1,0:T(8,128)(2,1)S(1)}, bf16[6,48,96]{2,1,0:T(8,128)(2,1)S(1)}, u32[]{:S(2)}, u32[]{:S(2)}) collective-permute-start(bf16[6,48,96]{2,1,0:T(8,128)(2,1)S(1)} %get-tuple-element.55), channel_id=1, source_target_pairs={{0,16},{16,0},{1,17},{17,1},{2,18},{18,2},{3,19},{19,3},{4,20},{20... | collective-permute-start | bytes 165896 | tf_op jit(solution)/shard_map/ppermute | solution.py:500

commit v8 on v7

--- a/solution.py
+++ b/solution.py
@@ -262,16 +262,20 @@
             exact_ref[half, at, :WIDE] = grad_scores
         for h in range(heads):
             total = jnp.zeros((PAD, SPAN), F32)
-            for col in range(WIN_LON):
+            apart = LANES // PAD
+            for col in range(apart):
+                low = h * WIDE + col * PAD
+                part = exact_ref[half, low : low + PAD, :WIDE]
                 by = (WIN_LON - 1 - col) * PAD
-                start = h * WIDE + col * PAD
-                part = jnp.concatenate(
-                    [
-                        exact_ref[half, start : start + PAD, :WIDE],
-                        jnp.zeros((PAD, SPAN - WIDE), F32),
-                    ],
-                    axis=1,
-                )
+                rest = jnp.zeros((PAD, SPAN - WIDE), F32)
+                if col + apart < WIN_LON:
+                    by = by - LANES
+                    high = low + apart * PAD
+                    twin = exact_ref[half, high : high + PAD, :WIDE]
+                    moved = jnp.concatenate([rest[:, :LANES], part, rest[:, LANES:]], axis=1)
+                    part = moved + jnp.concatenate([twin, rest], axis=1)
+                else:
+                    part = jnp.concatenate([part, rest], axis=1)
                 total = total + (part if by == 0 else pltpu.roll(part, by, 1))
             folded_ref[h, slot * PAD : (slot + 1) * PAD, :] = total
         results = (

time: 68.4 us -> 68.3 us (level)
  no operation moved by 1% of the time
where the time goes in v8:
time: 68.3 us; the launch traced here: 68.1 us
  waiting for transfers between devices  33.1 us (48%)
  Pallas kernels  18.2 us (27%)
  starting transfers between devices  14.8 us (22%)
  between operations  1.36 us (2%)
    ppermute x3, waiting for transfers between devices, exchange(): lax.ppermute(x, axis, [(i, (i - sign) % count) for i in range(count)])  18.6 us
    ppermute x4, waiting for transfers between devices, across(): return lax.ppermute(array, every, ring)  7.6 us
    ppermute x3, waiting for transfers between devices, per_device(): parts.append(lax.ppermute(pieces[step], 'head', ring))  6.57 us
    pallas_call x1, Pallas kernels, per_device(): pl.pallas_call(main_kernel, name='main', out_shape=[shape((packed, LANES)...  5.96 us
    ppermute x3, starting transfers between devices, per_device(): parts.append(lax.ppermute(pieces[step], 'head', ring))  5.54 us
    ppermute x4, starting transfers between devices, across(): return lax.ppermute(array, every, ring)  5.45 us
    pallas_call x1, Pallas kernels, per_device(): prepare(shift, own_x, own_g, rows, bias_type.reshape(1, slots), stored(ta...  3.73 us
    ppermute x3, starting transfers between devices, exchange(): lax.ppermute(x, axis, [(i, (i - sign) % count) for i in range(count)])  3.71 us
  transfers between devices with their start and end apart: 12, of which 7 were waited for; matrix products, arithmetic and copies ran while one was open for 0% of the time, Pallas kernels for 11%

profile of v8, /device:TPU:0, one launch (start us, length us, event | category | flops | bytes accessed | tf_op | source)
XLA Modules:
  0.0 68.1 jit_solution(8502369321010453565)
XLA Ops:
  1.3 1.8 %start.1 = (s32[1]{0:T(128)}, bf16[6,12,8,384]{3,2,1,0:T(8,128)(2,1)S(1)}, bf16[6,12,8,384]{3,2,1,0:T(8,128)(2,1)S(1)}, bf16[6,48,384]{2,1,0:T(8,128)(2,1)S(1)}, bf16[384,384]{1,0:T(8,128)(2,1)S(1)}) custom-call(s32[1]{0:T(128)S(6)} %copy.11.shift_ref, bf16[6,12,8,384]{3,2,1,0:T(8,128)(2,1)} %bitcast.10, bf16[6,12,8,384]{3,2,1,0:T(8,128)(2,1)} %bitcast.11, ...), custom_call_target="tpu_custom_call" | custom-call | tf_op jit(solution)/shard_map/start/pallas_call | solution.py:533
  3.1 0.0 copy-start
  3.1 0.6 copy-done
  3.7 3.7 %prepare.1 = (s32[1,4]{1,0:T(1,128)S(1)}, bf16[2,6,6,8,384]{4,3,2,1,0:T(8,128)(2,1)S(1)}, f32[4,576,192]{2,1,0:T(8,128)S(1)}, bf16[12,48,512]{2,1,0:T(8,128)(2,1)S(1)}, bf16[512,384]{1,0:T(8,128)(2,1)S(1)}) custom-call(s32[1]{0:T(128)} %get-tuple-element.32.shift_ref, bf16[6,12,8,384]{3,2,1,0:T(8,128)(2,1)S(1)} %get-tuple-element.33.x_ref, ...), custom_call_target="tpu_custom_call" | custom-call | tf_op jit(solution)/shard_map/prepare/pallas_call | solution.py:570
  7.5 3.0 %collective-permute-start = (bf16[2,6,6,8,384]{4,3,2,1,0:T(8,128)(2,1)S(1)}, bf16[2,6,6,8,384]{4,3,2,1,0:T(8,128)(2,1)S(1)}, u32[]{:S(2)}, u32[]{:S(2)}) collective-permute-start(bf16[2,6,6,8,384]{4,3,2,1,0:T(8,128)(2,1)S(1)} %get-tuple-element.36), channel_id=1, source_target_pairs={{0,16},{16,0},{1,17},{17,1},{2,18},{18,2},{3,19},{19,3},{4,20},{20... | collective-permute-start | bytes 1327112 | tf_op jit(solution)/shard_map/ppermute | solution.py:504
  10.5 0.1 collective-permute-start.1
  10.6 14.8 %collective-permute-done.1.far_ref = bf16[6,48,384]{2,1,0:T(8,128)(2,1)S(1)} collective-permute-done((bf16[6,48,384]{2,1,0:T(8,128)(2,1)S(1)}, bf16[6,48,384]{2,1,0:T(8,128)(2,1)S(1)}, u32[]{:S(2)}, u32[]{:S(2)}) %collective-permute-start.1) | collective-permute-done | bytes 221216 | tf_op jit(solution)/shard_map/ppermute | solution.py:504
  25.4 6.0 %main.1 = (bf16[432,128]{1,0:T(8,128)(2,1)S(1)}, bf16[432,128]{1,0:T(8,128)(2,1)S(1)}, bf16[432,128]{1,0:T(8,128)(2,1)S(1)}, bf16[432,128]{1,0:T(8,128)(2,1)S(1)...) custom-call(s32[1]{0:T(128)} %get-tuple-element.32.shift_ref, ...), custom_call_target="tpu_custom_call" | custom-call | tf_op jit(solution)/shard_map/main/pallas_call | solution.py:575
  31.4 0.0 collective-permute-done.far_ref
  31.4 1.9 %weight_sums.1 = (bf16[192,384]{1,0:T(8,128)(2,1)S(1)}, bf16[192,384]{1,0:T(8,128)(2,1)S(1)}, bf16[4,96,384]{2,1,0:T(8,128)(2,1)}) custom-call(s32[1]{0:T(128)} %get-tuple-element.32.shift_ref, bf16[6,12,8,384]{3,2,1,0:T(8,128)(2,1)S(1)} %get-tuple-element.33.x_ref, bf16[6,12,8,384]{3,2,1,0:T(8,128)(2,1)S(1)} %get-tuple-element.34.g_ref, ...), custom_call_target="tpu_custom_call" | custom-call | tf_op jit(solution)/shard_map/weight_sums/pallas_call | solution.py:607
  33.3 0.0 collective-permute-start.2
  33.3 1.1 %bias_rows.1.rows_ref = bf16[104,384]{1,0:T(8,128)(2,1)S(1)} custom-call(s32[1,4]{1,0:T(1,128)S(1)} %get-tuple-element.44.kind_ref, f32[3,64,384]{2,1,0:T(8,128)S(1)} %get-tuple-element.45.folded_ref), custom_call_target="tpu_custom_call" | custom-call | tf_op jit(solution)/shard_map/bias_rows/pallas_call | solution.py:624
  34.4 0.3 collective-permute-done.2.got_ref
  34.7 1.8 %collective-permute-start.3 = (bf16[152,384]{1,0:T(8,128)(2,1)S(1)}, bf16[152,384]{1,0:T(8,128)(2,1)S(1)}, u32[]{:S(2)}, u32[]{:S(2)}) collective-permute-start(bf16[152,384]{1,0:T(8,128)(2,1)S(1)} %get-tuple-element.46.first_ref), channel_id=1, source_target_pairs={{0,16},{4,20},{8,24},{12,28},{16,0},{20,4},{24,8},{28,12},{1,17},{... | collective-permute-start | bytes 350216 | tf_op jit(solution)/shard_map/ppermute | solution.py:663
  36.5 1.5 %collective-permute-start.4 = (bf16[144,384]{1,0:T(8,128)(2,1)S(1)}, bf16[144,384]{1,0:T(8,128)(2,1)S(1)}, u32[]{:S(2)}, u32[]{:S(2)}) collective-permute-start(bf16[144,384]{1,0:T(8,128)(2,1)S(1)} %get-tuple-element.47.second_ref), channel_id=1, source_target_pairs={{0,8},{4,12},{8,0},{12,4},{16,24},{20,28},{24,16},{28,20},{1,9},{5... | collective-permute-start | bytes 331784 | tf_op jit(solution)/shard_map/ppermute | solution.py:663
  38.1 3.4 %collective-permute-done.4.got_second_ref = bf16[144,384]{1,0:T(8,128)(2,1)S(1)} collective-permute-done((bf16[144,384]{1,0:T(8,128)(2,1)S(1)}, bf16[144,384]{1,0:T(8,128)(2,1)S(1)}, u32[]{:S(2)}, u32[]{:S(2)}) %collective-permute-start.4) | collective-permute-done | bytes 110624 | tf_op jit(solution)/shard_map/ppermute | solution.py:663
  41.4 0.1 add.1
  41.5 1.6 %collective-permute-start.5 = (bf16[152,384]{1,0:T(8,128)(2,1)S(1)}, bf16[152,384]{1,0:T(8,128)(2,1)S(1)}, u32[]{:S(2)}, u32[]{:S(2)}) collective-permute-start(bf16[152,384]{1,0:T(8,128)(2,1)S(1)} %get-tuple-element.48.first_ref), channel_id=1, source_target_pairs={{0,8},{4,12},{8,0},{12,4},{16,24},{20,28},{24,16},{28,20},{1,9},{5... | collective-permute-start | bytes 350216 | tf_op jit(solution)/shard_map/ppermute | solution.py:663
  43.1 0.5 collective-permute-start.6
  43.6 4.2 %collective-permute-done.6.got_second_ref = bf16[144,384]{1,0:T(8,128)(2,1)S(1)} collective-permute-done((bf16[144,384]{1,0:T(8,128)(2,1)S(1)}, bf16[144,384]{1,0:T(8,128)(2,1)S(1)}, u32[]{:S(2)}, u32[]{:S(2)}) %collective-permute-start.6) | collective-permute-done | bytes 110624 | tf_op jit(solution)/shard_map/ppermute | solution.py:663
  47.8 0.0 collective-permute-done.5.got_first_ref
  47.8 0.1 merge.1.refs_0_
  47.9 0.1 collective-permute-start.7
  48.0 1.6 %collective-permute-start.8 = (bf16[432,128]{1,0:T(8,128)(2,1)S(1)}, bf16[432,128]{1,0:T(8,128)(2,1)S(1)}, u32[]{:S(2)}, u32[]{:S(2)}) collective-permute-start(bf16[432,128]{1,0:T(8,128)(2,1)S(1)} %get-tuple-element.51), channel_id=1, source_target_pairs={{0,1},{1,2},{2,3},{3,0},{4,5},{5,6},{6,7},{7,4},{8,9},{9,10},{10,1... | collective-permute-start | bytes 331784 | tf_op jit(solution)/shard_map/ppermute | solution.py:601
  49.6 2.6 %collective-permute-start.9 = (bf16[432,128]{1,0:T(8,128)(2,1)S(1)}, bf16[432,128]{1,0:T(8,128)(2,1)S(1)}, u32[]{:S(2)}, u32[]{:S(2)}) collective-permute-start(bf16[432,128]{1,0:T(8,128)(2,1)S(1)} %get-tuple-element.52), channel_id=1, source_target_pairs={{0,2},{1,3},{2,0},{3,1},{4,6},{5,7},{6,4},{7,5},{8,10},{9,11},{10,... | collective-permute-start | bytes 331784 | tf_op jit(solution)/shard_map/ppermute | solution.py:601
  52.2 1.3 %collective-permute-start.10 = (bf16[432,128]{1,0:T(8,128)(2,1)S(1)}, bf16[432,128]{1,0:T(8,128)(2,1)S(1)}, u32[]{:S(2)}, u32[]{:S(2)}) collective-permute-start(bf16[432,128]{1,0:T(8,128)(2,1)S(1)} %get-tuple-element.53), channel_id=1, source_target_pairs={{0,3},{1,0},{2,1},{3,2},{4,7},{5,4},{6,5},{7,6},{8,11},{9,8},{10,9... | collective-permute-start | bytes 331784 | tf_op jit(solution)/shard_map/ppermute | solution.py:601
  53.5 2.3 %collective-permute-done.8.refs_1_ = bf16[432,128]{1,0:T(8,128)(2,1)S(1)} collective-permute-done((bf16[432,128]{1,0:T(8,128)(2,1)S(1)}, bf16[432,128]{1,0:T(8,128)(2,1)S(1)}, u32[]{:S(2)}, u32[]{:S(2)}) %collective-permute-start.8) | collective-permute-done | bytes 110624 | tf_op jit(solution)/shard_map/ppermute | solution.py:601
  55.9 4.2 %collective-permute-done.9.refs_2_ = bf16[432,128]{1,0:T(8,128)(2,1)S(1)} collective-permute-done((bf16[432,128]{1,0:T(8,128)(2,1)S(1)}, bf16[432,128]{1,0:T(8,128)(2,1)S(1)}, u32[]{:S(2)}, u32[]{:S(2)}) %collective-permute-start.9) | collective-permute-done | bytes 110624 | tf_op jit(solution)/shard_map/ppermute | solution.py:601
  60.1 0.7 %sum_heads.1 = (bf16[12,48,96]{2,1,0:T(8,128)(2,1)S(1)}, bf16[6,48,96]{2,1,0:T(8,128)(2,1)S(1)}) custom-call(s32[1]{0:T(128)} %get-tuple-element.32.shift_ref, bf16[432,128]{1,0:T(8,128)(2,1)S(1)} %get-tuple-element.50.refs_0_, bf16[432,128]{1,0:T(8,128)(2,1)S(1)} %collective-permute-done.8.refs_1_, bf16[432,128]{1,0:T(8,128)(2,1)S(1)} %collective-permute-done.9.refs_2_, ...), custom_call_target="tpu_custom_call" | custom-call | tf_op jit(solution)/shard_map/sum_heads/pallas_call | solution.py:637
  60.8 0.6 collective-permute-start.11
  61.4 3.8 %collective-permute-done.11.refs_3_ = bf16[6,48,96]{2,1,0:T(8,128)(2,1)S(1)} collective-permute-done((bf16[6,48,96]{2,1,0:T(8,128)(2,1)S(1)}, bf16[6,48,96]{2,1,0:T(8,128)(2,1)S(1)}, u32[]{:S(2)}, u32[]{:S(2)}) %collective-permute-start.11) | collective-permute-done | bytes 55328 | tf_op jit(solution)/shard_map/ppermute | solution.py:504
  65.2 2.8 %finish.1 = (bf16[6,12,8,96]{3,2,1,0:T(8,128)(2,1)}, f32[3,96,384]{2,1,0:T(8,128)}, f32[96,384]{1,0:T(8,128)}, f32[3,64,3312]{2,1,0:T(8,128)}) custom-call(s32[1]{0:T(128)} %get-tuple-element.32.shift_ref, bf16[2,200,384]{2,1,0:T(8,128)(2,1)S(1)} %merge.1.refs_0_, bf16[2,200,384]{2,1,0:T(8,128)(2,1)S(1)} %collective-permute-done.7.refs_1_, ...), custom_call_target="tpu_custom_call" | custom-call | tf_op jit(solution)/shard_map/finish/pallas_call | solution.py:696
  (4 shorter events, 0.1 us)
Async XLA Ops:
  3.1 0.7 copy-start
  7.5 23.9 %collective-permute-start = (bf16[2,6,6,8,384]{4,3,2,1,0:T(8,128)(2,1)S(1)}, bf16[2,6,6,8,384]{4,3,2,1,0:T(8,128)(2,1)S(1)}, u32[]{:S(2)}, u32[]{:S(2)}) collective-permute-start(bf16[2,6,6,8,384]{4,3,2,1,0:T(8,128)(2,1)S(1)} %get-tuple-element.36), channel_id=1, source_target_pairs={{0,16},{16,0},{1,17},{17,1},{2,18},{18,2},{3,19},{19,3},{4,20},{20... | collective-permute-start | bytes 1327112 | tf_op jit(solution)/shard_map/ppermute | solution.py:504
  10.5 14.9 %collective-permute-start.1 = (bf16[6,48,384]{2,1,0:T(8,128)(2,1)S(1)}, bf16[6,48,384]{2,1,0:T(8,128)(2,1)S(1)}, u32[]{:S(2)}, u32[]{:S(2)}) collective-permute-start(bf16[6,48,384]{2,1,0:T(8,128)(2,1)S(1)} %get-tuple-element.37), channel_id=1, source_target_pairs={{0,16},{16,0},{1,17},{17,1},{2,18},{18,2},{3,19},{19,3},{4,20},{20... | collective-permute-start | bytes 663560 | tf_op jit(solution)/shard_map/ppermute | solution.py:504
  33.3 1.4 %collective-permute-start.2 = (bf16[192,384]{1,0:T(8,128)(2,1)S(1)}, bf16[192,384]{1,0:T(8,128)(2,1)S(1)}, u32[]{:S(2)}, u32[]{:S(2)}) collective-permute-start(bf16[192,384]{1,0:T(8,128)(2,1)S(1)} %get-tuple-element.43), channel_id=1, source_target_pairs={{0,4},{4,0},{8,12},{12,8},{1,5},{5,1},{9,13},{13,9},{2,6},{6,2},{1... | collective-permute-start | bytes 442376 | tf_op jit(solution)/shard_map/ppermute | solution.py:617
  34.7 6.7 %collective-permute-start.3 = (bf16[152,384]{1,0:T(8,128)(2,1)S(1)}, bf16[152,384]{1,0:T(8,128)(2,1)S(1)}, u32[]{:S(2)}, u32[]{:S(2)}) collective-permute-start(bf16[152,384]{1,0:T(8,128)(2,1)S(1)} %get-tuple-element.46.first_ref), channel_id=1, source_target_pairs={{0,16},{4,20},{8,24},{12,28},{16,0},{20,4},{24,8},{28,12},{1,17},{... | collective-permute-start | bytes 350216 | tf_op jit(solution)/shard_map/ppermute | solution.py:663
  36.5 4.9 %collective-permute-start.4 = (bf16[144,384]{1,0:T(8,128)(2,1)S(1)}, bf16[144,384]{1,0:T(8,128)(2,1)S(1)}, u32[]{:S(2)}, u32[]{:S(2)}) collective-permute-start(bf16[144,384]{1,0:T(8,128)(2,1)S(1)} %get-tuple-element.47.second_ref), channel_id=1, source_target_pairs={{0,8},{4,12},{8,0},{12,4},{16,24},{20,28},{24,16},{28,20},{1,9},{5... | collective-permute-start | bytes 331784 | tf_op jit(solution)/shard_map/ppermute | solution.py:663
  41.5 6.3 %collective-permute-start.5 = (bf16[152,384]{1,0:T(8,128)(2,1)S(1)}, bf16[152,384]{1,0:T(8,128)(2,1)S(1)}, u32[]{:S(2)}, u32[]{:S(2)}) collective-permute-start(bf16[152,384]{1,0:T(8,128)(2,1)S(1)} %get-tuple-element.48.first_ref), channel_id=1, source_target_pairs={{0,8},{4,12},{8,0},{12,4},{16,24},{20,28},{24,16},{28,20},{1,9},{5... | collective-permute-start | bytes 350216 | tf_op jit(solution)/shard_map/ppermute | solution.py:663
  43.1 4.7 %collective-permute-start.6 = (bf16[144,384]{1,0:T(8,128)(2,1)S(1)}, bf16[144,384]{1,0:T(8,128)(2,1)S(1)}, u32[]{:S(2)}, u32[]{:S(2)}) collective-permute-start(bf16[144,384]{1,0:T(8,128)(2,1)S(1)} %get-tuple-element.49.second_ref), channel_id=1, source_target_pairs={{0,16},{4,20},{8,24},{12,28},{16,0},{20,4},{24,8},{28,12},{1,17},{... | collective-permute-start | bytes 331784 | tf_op jit(solution)/shard_map/ppermute | solution.py:663
  47.9 17.3 %collective-permute-start.7 = (bf16[2,200,384]{2,1,0:T(8,128)(2,1)S(1)}, bf16[2,200,384]{2,1,0:T(8,128)(2,1)S(1)}, u32[]{:S(2)}, u32[]{:S(2)}) collective-permute-start(bf16[2,200,384]{2,1,0:T(8,128)(2,1)S(1)} %merge.1.refs_0_), channel_id=1, source_target_pairs={{0,4},{4,0},{8,12},{12,8},{1,5},{5,1},{9,13},{13,9},{2,6},{6,2},{1... | collective-permute-start | bytes 921608 | tf_op jit(solution)/shard_map/ppermute | solution.py:684
  48.0 7.9 %collective-permute-start.8 = (bf16[432,128]{1,0:T(8,128)(2,1)S(1)}, bf16[432,128]{1,0:T(8,128)(2,1)S(1)}, u32[]{:S(2)}, u32[]{:S(2)}) collective-permute-start(bf16[432,128]{1,0:T(8,128)(2,1)S(1)} %get-tuple-element.51), channel_id=1, source_target_pairs={{0,1},{1,2},{2,3},{3,0},{4,5},{5,6},{6,7},{7,4},{8,9},{9,10},{10,1... | collective-permute-start | bytes 331784 | tf_op jit(solution)/shard_map/ppermute | solution.py:601
  49.6 10.5 %collective-permute-start.9 = (bf16[432,128]{1,0:T(8,128)(2,1)S(1)}, bf16[432,128]{1,0:T(8,128)(2,1)S(1)}, u32[]{:S(2)}, u32[]{:S(2)}) collective-permute-start(bf16[432,128]{1,0:T(8,128)(2,1)S(1)} %get-tuple-element.52), channel_id=1, source_target_pairs={{0,2},{1,3},{2,0},{3,1},{4,6},{5,7},{6,4},{7,5},{8,10},{9,11},{10,... | collective-permute-start | bytes 331784 | tf_op jit(solution)/shard_map/ppermute | solution.py:601
  52.2 7.9 %collective-permute-start.10 = (bf16[432,128]{1,0:T(8,128)(2,1)S(1)}, bf16[432,128]{1,0:T(8,128)(2,1)S(1)}, u32[]{:S(2)}, u32[]{:S(2)}) collective-permute-start(bf16[432,128]{1,0:T(8,128)(2,1)S(1)} %get-tuple-element.53), channel_id=1, source_target_pairs={{0,3},{1,0},{2,1},{3,2},{4,7},{5,4},{6,5},{7,6},{8,11},{9,8},{10,9... | collective-permute-start | bytes 331784 | tf_op jit(solution)/shard_map/ppermute | solution.py:601
  60.8 4.4 %collective-permute-start.11 = (bf16[6,48,96]{2,1,0:T(8,128)(2,1)S(1)}, bf16[6,48,96]{2,1,0:T(8,128)(2,1)S(1)}, u32[]{:S(2)}, u32[]{:S(2)}) collective-permute-start(bf16[6,48,96]{2,1,0:T(8,128)(2,1)S(1)} %get-tuple-element.55), channel_id=1, source_target_pairs={{0,16},{16,0},{1,17},{17,1},{2,18},{18,2},{3,19},{19,3},{4,20},{20... | collective-permute-start | bytes 165896 | tf_op jit(solution)/shard_map/ppermute | solution.py:504
